TPU v7x, 128 devices: a whole 4x4x4 slice. The times are simulated.
128 devices in a mesh: local: 16 (over z, y), data: 8 (over x, core).
Axes of the slice: x: 4, y: 4, z: 4, core: 2. Of those that a mesh axis runs over, the one named last changes fastest.
Arguments:
- tokens: bfloat16 [16384, 2048], P(('local', 'data'))
- cotangent: bfloat16 [16384, 2048], P(('local', 'data'))
- w_in: bfloat16 [2, 2048, 8192], P(None, 'local')
- w_out: bfloat16 [2, 8192, 2048], P(None, 'local')
Outputs:
- output 1: bfloat16 [16384, 2048], P(('local', 'data'))
- output 2: float32 [2, 2048, 8192], P(None, 'local')
- output 3: float32 [2, 8192, 2048], P(None, 'local')
- output 4: bfloat16 [16384, 2048], P(('local', 'data'))
All inputs are finite; a program needn't handle non-finite values.
Results may differ from a plain program's by a relative error of at most 0.0134477.
Values are sent between devices in bfloat16 or wider.
A program may use at most 1 GiB of HBM per device.

v0:
```python
import jax
import jax.numpy as jnp
from jax import lax
from jax.sharding import PartitionSpec as P

EPSILON = 1e-6


def norm_rows(x_f):
    return x_f * lax.rsqrt(jnp.mean(x_f * x_f, axis=-1, keepdims=True) + EPSILON)


def layer_forward(x_in, w_first, w_second):
    normed = norm_rows(x_in.astype(jnp.float32)).astype(jnp.bfloat16)
    pre_act = jnp.dot(normed, w_first, preferred_element_type=jnp.float32).astype(jnp.bfloat16)
    hidden = jax.nn.gelu(pre_act.astype(jnp.float32)).astype(jnp.bfloat16)
    branch = jnp.dot(hidden, w_second, preferred_element_type=jnp.float32)
    return (x_in.astype(jnp.float32) + branch).astype(jnp.bfloat16), pre_act


def layer_backward(grad_next, x_in, pre_act, w_first, w_second):
    normed_f, norm_vjp = jax.vjp(norm_rows, x_in.astype(jnp.float32))
    normed = normed_f.astype(jnp.bfloat16)
    hidden_f, gelu_vjp = jax.vjp(jax.nn.gelu, pre_act.astype(jnp.float32))
    hidden = hidden_f.astype(jnp.bfloat16)
    grad_b = grad_next.astype(jnp.bfloat16)
    grad_second = lax.dot_general(hidden, grad_b, (((0,), (0,)), ((), ())), preferred_element_type=jnp.float32)
    grad_hidden = lax.dot_general(grad_b, w_second, (((1,), (1,)), ((), ())), preferred_element_type=jnp.float32)
    grad_pre = gelu_vjp(grad_hidden)[0].astype(jnp.bfloat16)
    grad_first = lax.dot_general(normed, grad_pre, (((0,), (0,)), ((), ())), preferred_element_type=jnp.float32)
    grad_normed = lax.dot_general(grad_pre, w_first, (((1,), (1,)), ((), ())), preferred_element_type=jnp.float32)
    grad_x = grad_next + norm_vjp(grad_normed)[0]
    return grad_x, grad_first, grad_second


def reduce_grad(grad_full):
    grad_part = lax.psum_scatter(grad_full, 'local', scatter_dimension=0, tiled=True)
    return lax.psum(grad_part, 'data')


def solution(mesh):
    tok_spec = P(('local', 'data'), None)
    w_spec = P(None, 'local', None)

    def device_step(tokens, cotangent, w_in, w_out):
        layer_count = w_in.shape[0]
        current = tokens
        saved_acts = []
        for layer_idx in range(layer_count):
            w_first = lax.all_gather(w_in[layer_idx], 'local', axis=0, tiled=True)
            w_second = lax.all_gather(w_out[layer_idx], 'local', axis=0, tiled=True)
            next_act, pre_act = layer_forward(current, w_first, w_second)
            saved_acts.append((current, pre_act))
            current = next_act
        grad_up = cotangent.astype(jnp.float32)
        grads_first = []
        grads_second = []
        for layer_idx in reversed(range(layer_count)):
            w_first = lax.all_gather(w_in[layer_idx], 'local', axis=0, tiled=True)
            w_second = lax.all_gather(w_out[layer_idx], 'local', axis=0, tiled=True)
            grad_up, grad_first, grad_second = layer_backward(grad_up, saved_acts[layer_idx][0], saved_acts[layer_idx][1], w_first, w_second)
            grads_first.append(reduce_grad(grad_first))
            grads_second.append(reduce_grad(grad_second))
        return current, jnp.stack(grads_first[::-1]), jnp.stack(grads_second[::-1]), grad_up.astype(jnp.bfloat16)

    return jax.shard_map(device_step, mesh=mesh, in_specs=(tok_spec, tok_spec, w_spec, w_spec), out_specs=(tok_spec, w_spec, w_spec, tok_spec), check_vma=False)
```

profile of v0, /device:TPU:1, one launch (start us, length us, event | category | flops | bytes accessed | tf_op | source)
XLA Modules:
  0.0 2542.2 jit_solution(7535417635891009726)
XLA Ops:
  7.2 4.7 fusion.77
  12.0 4.8 fusion.78
  18.4 193.7 %all-gather.9.cloned.1.call-done = bf16[1,2048,8192]{2,1,0:T(8,128)(2,1)} async-done(((bf16[1,128,8192]{2,1,0:T(8,128)(2,1)}), bf16[1,2048,8192]{2,1,0:T(8,128)(2,1)}) %all-gather.9.cloned.1.call-update) | async-done | bytes 33554448 | tf_op jit(solution)/shard_map/all_gather | solution.py:50
  212.1 17.2 fusion.19
  229.3 182.3 %all-gather.11.cloned.1.call-done = bf16[1,8192,2048]{2,1,0:T(8,128)(2,1)} async-done(((bf16[1,512,2048]{2,1,0:T(8,128)(2,1)}), bf16[1,8192,2048]{2,1,0:T(8,128)(2,1)}) %all-gather.11.cloned.1.call-update) | async-done | bytes 33554448 | tf_op jit(solution)/shard_map/all_gather | solution.py:51
  411.6 14.9 multiply_reduce_fusion.1
  426.5 183.9 %all-gather.13.cloned.1.call-done = bf16[1,2048,8192]{2,1,0:T(8,128)(2,1)} async-done(((bf16[1,128,8192]{2,1,0:T(8,128)(2,1)}), bf16[1,2048,8192]{2,1,0:T(8,128)(2,1)}) %all-gather.13.cloned.1.call-update) | async-done | bytes 33554448 | tf_op jit(solution)/shard_map/all_gather | solution.py:50
  610.4 17.2 fusion.25
  627.6 181.5 %all-gather.15.cloned.1.call-done = bf16[1,8192,2048]{2,1,0:T(8,128)(2,1)} async-done(((bf16[1,512,2048]{2,1,0:T(8,128)(2,1)}), bf16[1,8192,2048]{2,1,0:T(8,128)(2,1)}) %all-gather.15.cloned.1.call-update) | async-done | bytes 33554448 | tf_op jit(solution)/shard_map/all_gather | solution.py:51
  809.1 18.9 fusion.41
  828.1 21.2 multiply_reduce_fusion
  851.8 24.4 fusion.67
  876.2 25.4 %fusion.76 = f32[8192,2048]{1,0:T(8,128)} fusion(bf16[128,2048]{1,0:T(8,128)(2,1)S(1)} %copy-done.12, f32[128,8192]{1,0:T(8,128)} %fusion.25), kind=kOutput, calls=%fused_computation.73 | convolution fusion | flops 4304404480 | bytes 71827456 | tf_op jit(solution)/shard_map/dot_general | solution.py:27
  903.6 23.2 fusion.75
  926.9 18.2 fusion.34
  945.1 23.3 fusion.70
  968.4 270.8 %reduce-scatter.9.cloned.1.call-done = f32[512,2048]{1,0:T(8,128)} async-done(((f32[8192,2048]{1,0:T(8,128)}), f32[512,2048]{1,0:T(8,128)}) %reduce-scatter.9.cloned.1.call-update) | async-done | bytes 4194320 | tf_op jit(solution)/shard_map/reduce_scatter | solution.py:37
  1239.3 366.3 %reduce-scatter.11.cloned.1.call-done = f32[512,2048]{1,0:T(8,128)} async-done(((f32[8192,2048]{1,0:T(8,128)}), f32[512,2048]{1,0:T(8,128)}) %reduce-scatter.11.cloned.1.call-update) | async-done | bytes 4194320 | tf_op jit(solution)/shard_map/reduce_scatter | solution.py:37
  1605.6 366.5 %reduce-scatter.7.cloned.1.call-done = f32[128,8192]{1,0:T(8,128)} async-done(((f32[2048,8192]{1,0:T(8,128)}), f32[128,8192]{1,0:T(8,128)}) %reduce-scatter.7.cloned.1.call-update) | async-done | bytes 4194320 | tf_op jit(solution)/shard_map/reduce_scatter | solution.py:37
  1972.0 366.5 %reduce-scatter.5.cloned.1.call-done = f32[128,8192]{1,0:T(8,128)} async-done(((f32[2048,8192]{1,0:T(8,128)}), f32[128,8192]{1,0:T(8,128)}) %reduce-scatter.5.cloned.1.call-update) | async-done | bytes 4194320 | tf_op jit(solution)/shard_map/reduce_scatter | solution.py:37
  2338.5 17.9 fusion.66
  2358.8 16.7 fusion.52
  2375.5 147.8 %all-reduce.3.cloned.1.call-done = (f32[1,128,8192]{2,1,0:T(8,128)}, f32[1,128,8192]{2,1,0:T(8,128)}, f32[1,512,2048]{2,1,0:T(8,128)}, f32[1,512,2048]{2,1,0:T(8,128)}) async-done(((f32[1,128,8192]{2,1,0:T(8,128)}, f32[1,128,8192]{2,1,0:T(8,128)}, f32[1,512,2048]{2,1,0:T(8,128)}, f32[1,512,2048]{2,1,0:T(8,128)}), (f32[1,128,8192]{2,1,0:T(8,128)}, f32[1,128,8192]{2,1,0:T(8,128)}, f32[1,512,2048]{2,1,0:T(8,128)}, ...) | async-done | bytes 16777232 | tf_op jit(solution)/shard_map/psum | solution.py:38
  2523.3 7.9 pad_maximum_fusion
  (60 shorter events, 12.6 us)
Async XLA Ops:
  7.2 205.0 %all-gather.9.cloned.1.call-start = ((), (), s32[]{:S(2)}) async-start(), calls=%async_computation.8 | async-start | bytes 35651584 | tf_op jit(solution)/shard_map/all_gather | solution.py:50
  11.9 399.7 %all-gather.11.cloned.1.call-start = ((), (), s32[]{:S(2)}) async-start(), calls=%async_computation.9 | async-start | bytes 35651584 | tf_op jit(solution)/shard_map/all_gather | solution.py:51
  16.8 593.6 %all-gather.13.cloned.1.call-start = ((), (), s32[]{:S(2)}) async-start(), calls=%async_computation.10 | async-start | bytes 35651584 | tf_op jit(solution)/shard_map/all_gather | solution.py:50
  17.5 791.6 %all-gather.15.cloned.1.call-start = ((), (), s32[]{:S(2)}) async-start(), calls=%async_computation.11 | async-start | bytes 35651584 | tf_op jit(solution)/shard_map/all_gather | solution.py:51
  18.1 1221.2 %reduce-scatter.9.cloned.1.call-start = ((), (), s32[]{:S(2)}) async-start(), calls=%async_computation.6 | async-start | bytes 71303168 | tf_op jit(solution)/shard_map/reduce_scatter | solution.py:37
  18.4 210.9 %copy-start.15 = (f32[128]{0:T(128)}, f32[128]{0:T(128)S(1)}, u32[]{:S(2)}) copy-start(f32[128]{0:T(128)S(1)} %fusion.64) | copy-start | bytes 1540
  18.4 210.9 %copy-start.13 = (f32[128]{0:T(128)}, f32[128]{0:T(128)S(1)}, u32[]{:S(2)}) copy-start(f32[128]{0:T(128)S(1)} %fusion.73) | copy-start | bytes 1540
  426.5 201.1 %copy-start.2 = (f32[128,2048]{1,0:T(8,128)}, f32[128,2048]{1,0:T(8,128)S(1)}, u32[]{:S(2)}) copy-start(f32[128,2048]{1,0:T(8,128)S(1)} %get-tuple-element.13) | copy-start | bytes 3145732
  610.4 198.7 %copy-start.12 = (bf16[128,2048]{1,0:T(8,128)(2,1)S(1)}, bf16[128,2048]{1,0:T(8,128)(2,1)}, u32[]{:S(2)}) copy-start(bf16[128,2048]{1,0:T(8,128)(2,1)} %param.5) | copy-start | bytes 1572868
  828.1 21.2 copy-start.3
  828.1 23.7 copy-start
  876.2 729.4 %reduce-scatter.11.cloned.1.call-start = ((), (), s32[]{:S(2)}) async-start(), calls=%async_computation.7 | async-start | bytes 71303168 | tf_op jit(solution)/shard_map/reduce_scatter | solution.py:37
  901.6 1.9 copy-start.8
  901.7 1070.4 %reduce-scatter.7.cloned.1.call-start = ((), (), s32[]{:S(2)}) async-start(), calls=%async_computation.5 | async-start | bytes 71303168 | tf_op jit(solution)/shard_map/reduce_scatter | solution.py:37
  926.8 18.3 copy-start.6
  926.8 18.3 copy-start.14
  926.8 1411.7 %reduce-scatter.5.cloned.1.call-start = ((), (), s32[]{:S(2)}) async-start(), calls=%async_computation.4 | async-start | bytes 71303168 | tf_op jit(solution)/shard_map/reduce_scatter | solution.py:37
  945.1 23.3 copy-start.7
  968.4 1554.9 %all-reduce.3.cloned.1.call-start = ((), (), s32[]{:S(2)}) async-start(), calls=%async_computation.12 | async-start | bytes 33554432 | tf_op jit(solution)/shard_map/psum | solution.py:38
  2338.5 17.9 copy-start.16
  2338.5 17.9 copy-start.9
  2338.5 20.3 copy-start.1
  2523.3 7.9 copy-start.10
  2523.3 7.9 copy-start.11
  (2 other events, 2.6 us)
Sparse Core Ops, SparseCore 0:
  12.0 200.0 all-gather.8
  214.8 196.6 all-gather.10
  413.7 196.6 all-gather.12
  612.4 196.6 all-gather.14
  876.3 362.9 reduce-scatter.8
  1242.6 362.8 reduce-scatter.10
  1609.1 362.9 reduce-scatter.6
  1975.6 362.8 reduce-scatter.4
  2341.2 182.0 all-reduce.2
where the time goes:
time: 2550 us; the launch traced here: 2540 us
  waiting for transfers between devices  2260 us (89%)
  matrix products  238 us (9%)
    reduce_scatter x4, waiting for transfers between devices, reduce_grad(): lax.psum_scatter(grad_full, 'local', scatter_dimension=0, tiled=True)  1370 us
    all_gather x2, waiting for transfers between devices, device_step(): w_first = lax.all_gather(w_in[layer_idx], 'local', axis=0, tiled=True)  378 us
    all_gather x2, waiting for transfers between devices, device_step(): w_second = lax.all_gather(w_out[layer_idx], 'local', axis=0, tiled=True)  364 us
    psum x1, waiting for transfers between devices, reduce_grad(): return lax.psum(grad_part, 'data')  148 us
  transfers between devices with their start and end apart: 9, of which 9 were waited for; matrix products, arithmetic and copies ran while one was open for 7% of the time, Pallas kernels for 0%

commit v1 on v0

v1 whole, which is shorter than its diff:
```python
import functools

import jax
import jax.numpy as jnp
from jax import lax
from jax.experimental import pallas as pl
from jax.experimental.pallas import tpu as pltpu
from jax.sharding import PartitionSpec as P

EPSILON = 1e-6
GELU_SCALE = 0.7978845608028654
GELU_CUBE = 0.044715
BF16 = jnp.bfloat16
F32 = jnp.float32
MESH = pl.DeviceIdType.MESH
HBM = pltpu.HBM
VMEM = pltpu.VMEM


class Comm:
    def __init__(self, send_sems, recv_sems):
        l = lax.axis_index('local')
        d = lax.axis_index('data')
        self.l, self.d = l, d
        self.z, self.y, self.x, self.c = l // 4, l % 4, d // 2, d % 2
        self.send_sems, self.recv_sems = send_sems, recv_sems
        self.count = 0
        self.open_sends = []
        self.partner = (l, self.x * 2 + 1 - self.c)

    def pos(self, axis):
        return {'x': self.x, 'y': self.y, 'z': self.z}[axis]

    def neighbor(self, axis, delta):
        p = (self.pos(axis) + delta) % 4
        if axis == 'x':
            return (self.l, p * 2 + self.c)
        if axis == 'y':
            return (self.z * 4 + p, self.d)
        return (p * 4 + self.y, self.d)

    def barrier(self, axes):
        sem = pltpu.get_barrier_semaphore()
        devices = [self.partner]
        for axis in axes:
            devices += [self.neighbor(axis, 1), self.neighbor(axis, 3)]
        for device in devices:
            pl.semaphore_signal(sem, inc=1, device_id=device, device_id_type=MESH)
        pl.semaphore_wait(sem, len(devices))

    def send(self, src, dst, device):
        k = self.count
        self.count += 1
        copy = pltpu.make_async_remote_copy(
            src_ref=src, dst_ref=dst, send_sem=self.send_sems.at[k], recv_sem=self.recv_sems.at[k],
            device_id=device, device_id_type=MESH)
        copy.start()
        self.open_sends.append((k, copy))
        return k

    def wait_recv(self, k, ref, device):
        pltpu.make_async_remote_copy(
            src_ref=ref, dst_ref=ref, send_sem=self.send_sems.at[k], recv_sem=self.recv_sems.at[k],
            device_id=device, device_id_type=MESH).wait_recv()

    def wait_sends(self, keys=None):
        rest = []
        for k, copy in self.open_sends:
            if keys is None or k in keys:
                copy.wait_send()
            else:
                rest.append((k, copy))
        self.open_sends = rest


class RingGather:
    def __init__(self, comm, axis, own, slot):
        self.comm, self.own, self.slot = comm, own, slot
        self.me = comm.pos(axis)
        self.right, self.left = (self.me + 1) % 4, (self.me + 3) % 4
        self.far = (self.me + 2) % 4
        self.to_right, self.to_left = comm.neighbor(axis, 1), comm.neighbor(axis, 3)

    def start(self):
        send, own, slot, me = self.comm.send, self.own, self.slot, self.me
        self.r0 = send(own(0), slot(me, 0), self.to_right)
        self.l0 = send(own(1), slot(me, 1), self.to_left)
        self.r1 = send(own(1), slot(me, 1), self.to_right)
        self.l1 = send(own(0), slot(me, 0), self.to_left)

    def forward(self):
        c, slot = self.comm, self.slot
        c.wait_recv(self.r0, slot(self.left, 0), self.to_left)
        self.r2 = c.send(slot(self.left, 0), slot(self.left, 0), self.to_right)
        c.wait_recv(self.l0, slot(self.right, 1), self.to_right)
        self.l2 = c.send(slot(self.right, 1), slot(self.right, 1), self.to_left)

    def near(self):
        c, slot = self.comm, self.slot
        c.wait_recv(self.r1, slot(self.left, 1), self.to_left)
        c.wait_recv(self.l1, slot(self.right, 0), self.to_right)

    def finish(self):
        c, slot = self.comm, self.slot
        c.wait_recv(self.r2, slot(self.far, 0), self.to_left)
        c.wait_recv(self.l2, slot(self.far, 1), self.to_right)


class RingReduce:
    def __init__(self, comm, axis, part, landing):
        self.comm, self.part, self.landing = comm, part, landing
        self.me = comm.pos(axis)
        self.right, self.left = (self.me + 1) % 4, (self.me + 3) % 4
        self.far = (self.me + 2) % 4
        self.to_right, self.to_left = comm.neighbor(axis, 1), comm.neighbor(axis, 3)

    def send_far(self, half):
        ref = self.part(self.far, half)
        if half == 0:
            self.r0 = self.comm.send(ref, self.landing.at[0], self.to_right)
        else:
            self.l0 = self.comm.send(ref, self.landing.at[3], self.to_left)

    def send_near(self, half):
        if half == 1:
            self.r1 = self.comm.send(self.part(self.right, 1), self.landing.at[1], self.to_right)
        else:
            self.l1 = self.comm.send(self.part(self.left, 0), self.landing.at[4], self.to_left)

    def start(self):
        self.send_far(0)
        self.send_far(1)
        self.send_near(1)
        self.send_near(0)

    def middle(self, add):
        c, landing = self.comm, self.landing
        c.wait_recv(self.r0, landing.at[0], self.to_left)
        add(landing.at[0], self.right, 0)
        self.r2 = c.send(landing.at[0], landing.at[2], self.to_right)
        c.wait_recv(self.l0, landing.at[3], self.to_right)
        add(landing.at[3], self.left, 1)
        self.l2 = c.send(landing.at[3], landing.at[5], self.to_left)

    def finish(self):
        c, landing = self.comm, self.landing
        c.wait_recv(self.r1, landing.at[1], self.to_left)
        c.wait_recv(self.l1, landing.at[4], self.to_right)
        c.wait_recv(self.r2, landing.at[2], self.to_left)
        c.wait_recv(self.l2, landing.at[5], self.to_right)


def add_from(part):
    def add(ref, pos, half):
        ref[...] = ref[...] + part(pos, half)[...]
    return add


class WeightGather:
    def __init__(self, comm, first, second, full, own):
        self.comm, self.full, self.second = comm, full, second
        c = comm.c
        b = comm.pos(second)
        half_rows = full.shape[3] // 2
        rows = lambda h: pl.ds(h * half_rows, half_rows)
        self.b = b
        self.ring1 = RingGather(comm, first, own=lambda h: own.at[rows(h)],
                                slot=lambda p, h: full.at[p, b, c, rows(h)])
        pair = lambda p, h: full.at[pl.ds(2 * h, 2), p, c]
        self.ring2 = RingGather(comm, second, own=lambda h: pair(b, h), slot=pair)
        self.pushed = []

    def start1(self):
        self.ring1.start()

    def forward1(self):
        self.ring1.forward()

    def start2(self):
        self.ring1.near()
        self.ring1.finish()
        self.ring2.start()
        self.push(self.b)

    def push(self, p):
        c = self.comm
        mine = self.full.at[:, p, c.c]
        self.pushed.append((p, c.send(mine, mine, c.partner)))

    def forward2(self):
        self.ring2.forward()
        self.ring2.near()
        self.push(self.ring2.left)
        self.push(self.ring2.right)

    def finish2(self):
        self.ring2.finish()
        self.push(self.ring2.far)

    def arrived(self):
        c = self.comm
        for p, k in self.pushed:
            c.wait_recv(k, self.full.at[:, p, 1 - c.c], c.partner)


def start_local(copies, sems, first):
    out = []
    for i, (src, dst) in enumerate(copies):
        copy = pltpu.make_async_copy(src, dst, sems.at[first + i])
        copy.start()
        out.append(copy)
    return out


def wait_local(copies):
    for copy in copies:
        copy.wait()


def w1_strips(comm, w_in, layer, dst, rows):
    width = w_in.shape[2] // 64
    out = []
    for y in range(4):
        for z in range(4):
            start = (4 * z + y) * 4 * width + comm.x * width
            out.append((w_in.at[layer, pl.ds(comm.c * rows, rows), pl.ds(pl.multiple_of(start, width), width)],
                        dst.at[:, pl.ds((4 * y + z) * width, width)]))
    return out


def w2_rows(comm, w_out, layer, rows):
    start = (comm.x * 2 + comm.c) * rows
    return w_out.at[layer, pl.ds(pl.multiple_of(start, rows), rows)]


def norm_rows(x):
    return x * lax.rsqrt(jnp.mean(x * x, axis=-1, keepdims=True) + EPSILON)


def norm_rows_vjp(x, g):
    r = lax.rsqrt(jnp.mean(x * x, axis=-1, keepdims=True) + EPSILON)
    dot = jnp.mean(x * g, axis=-1, keepdims=True)
    return r * g - x * (r * r * r * dot)


def gelu(x):
    t = jnp.tanh(GELU_SCALE * (x + GELU_CUBE * (x * x * x)))
    return x * (0.5 * (1.0 + t))


def gelu_grad(x):
    x2 = x * x
    t = jnp.tanh(GELU_SCALE * (x + GELU_CUBE * (x2 * x)))
    return 0.5 * (1.0 + t) + (0.5 * x) * (1.0 - t * t) * (GELU_SCALE * (1.0 + (3.0 * GELU_CUBE) * x2))


def dot(a, b):
    return lax.dot_general(a, b, (((1,), (0,)), ((), ())), preferred_element_type=F32)


def dot_bt(a, b):
    return lax.dot_general(a, b, (((1,), (1,)), ((), ())), preferred_element_type=F32)


def dot_at(a, b):
    return lax.dot_general(a, b, (((0,), (0,)), ((), ())), preferred_element_type=F32)


def flat(value):
    return value.reshape(-1, value.shape[-1])


def tile_of(n):
    return min(256, n)


def forward_acts(u, w1, a, s):
    width = a.shape[1]
    t = tile_of(width)

    def step(i, _):
        cols = pl.ds(pl.multiple_of(i * t, t), t)
        acc = dot(flat(u[...]), flat(w1[:, :, :, :, cols])).astype(BF16)
        a[:, cols] = acc
        s[:, cols] = gelu(acc.astype(F32)).astype(BF16)
        return 0

    lax.fori_loop(0, width // t, step, 0)


def forward_part(s, w2, part, half):
    width = part.shape[1] // 2
    t = tile_of(width)

    def step(i, _):
        cols = pl.ds(pl.multiple_of(half * width + i * t, t), t)
        part[:, cols] = dot(s[...], flat(w2[:, :, :, :, cols]))
        return 0

    lax.fori_loop(0, width // t, step, 0)


def backward_acts(d, w2, a, q):
    rows = 2 * w2.shape[2] * w2.shape[3]

    def step(i, _):
        cols = pl.ds(pl.multiple_of(i * rows, rows), rows)
        w = flat(w2[i // 2, pl.ds((i % 2) * 2, 2)])
        c = dot_bt(flat(d[...]), w)
        q[:, cols] = (c * gelu_grad(a[:, cols].astype(F32))).astype(BF16)
        return 0

    lax.fori_loop(0, 8, step, 0)


def backward_part(q, w1, part, half):
    rows = 2 * w1.shape[2] * w1.shape[3]

    def step(j, _):
        i = half * 4 + j
        cols = pl.ds(pl.multiple_of(i * rows, rows), rows)
        w = flat(w1[i // 2, pl.ds((i % 2) * 2, 2)])
        part[:, cols] = dot_bt(q[...], w)
        return 0

    lax.fori_loop(0, 4, step, 0)


def part_block(part, tokens):
    width = part.shape[1] // 2
    return lambda pos, half: part.at[pl.ds(pl.multiple_of(pos * tokens, tokens), tokens),
                                     pl.ds(half * width, width)]


def reduced(part, ring, tokens):
    block = part_block(part, tokens)
    landing = ring.landing
    left = block(ring.me, 0)[...] + landing[2] + landing[4]
    right = block(ring.me, 1)[...] + landing[1] + landing[5]
    return jnp.concatenate([left, right], axis=1)


def forward_first(x0, cot, w_in, w_out,
                  x1, u1, u_all, s_all, a_out, cot_all, w1_next, w2_next,
                  w1, w2, uf, a, s, part, landing, stage1, stage2, send_sems, recv_sems, local_sems):
    comm = Comm(send_sems, recv_sems)
    tokens = x0.shape[0]
    rows1, rows2 = w1.shape[3], w2.shape[3]
    z, y, x, c = comm.z, comm.y, comm.x, comm.c

    own1, own2 = w1.at[z, y, c], w2.at[y, z, c]
    strips = start_local(w1_strips(comm, w_in, 0, own1, rows1), local_sems, 0)
    strips += start_local([(w2_rows(comm, w_out, 0, rows2), own2)], local_sems, 16)
    strips1 = start_local(w1_strips(comm, w_in, 1, stage1, rows1), local_sems, 17)
    strips1 += start_local([(w2_rows(comm, w_out, 1, rows2), stage2)], local_sems, 33)

    uf[x] = norm_rows(x0[...].astype(F32)).astype(BF16)
    comm.barrier('xyz')

    half_tokens = tokens // 2
    half_of = lambda h: pl.ds(h * half_tokens, half_tokens)
    gather_u = RingGather(comm, 'x', own=lambda h: uf.at[x, half_of(h)], slot=lambda p, h: uf.at[p, half_of(h)])
    gather_cot = RingGather(comm, 'x', own=lambda h: cot.at[half_of(h)], slot=lambda p, h: cot_all.at[p, half_of(h)])
    wait_local(strips)
    g1 = WeightGather(comm, 'z', 'y', w1, own1)
    g2 = WeightGather(comm, 'y', 'z', w2, own2)
    g1.start1()
    g2.start1()
    gather_u.start()
    g1.forward1()
    g2.forward1()
    gather_u.forward()
    gather_cot.start()
    g1.start2()
    g2.start2()

    wait_local(strips1)
    n1 = WeightGather(comm, 'z', 'y', w1_next, stage1)
    n2 = WeightGather(comm, 'y', 'z', w2_next, stage2)
    keep = start_local([(stage1, w1_next.at[z, y, c]), (stage2, w2_next.at[y, z, c])], local_sems, 34)

    gather_u.near()
    gather_u.finish()
    push_u = comm.send(uf, u_all.at[1], comm.partner)
    keep_u = start_local([(uf, u_all.at[0])], local_sems, 36)
    gather_cot.forward()
    g1.forward2()
    g2.forward2()
    wait_local(keep)
    n1.start1()
    n2.start1()
    gather_cot.near()
    gather_cot.finish()
    g1.finish2()
    g2.finish2()
    g1.arrived()
    n1.forward1()
    n2.forward1()
    forward_acts(uf, w1, a, s)
    g2.arrived()
    block = part_block(part, tokens)
    ring = RingReduce(comm, 'x', block, landing)
    forward_part(s, w2, part, 0)
    ring.send_far(0)
    ring.send_near(0)
    n1.start2()
    n2.start2()
    forward_part(s, w2, part, 1)
    ring.send_far(1)
    ring.send_near(1)
    push_s = comm.send(s, s_all.at[1], comm.partner)
    keep_s = start_local([(s, s_all.at[0]), (a, a_out)], local_sems, 37)
    ring.middle(add_from(block))
    n1.forward2()
    n2.forward2()
    ring.finish()
    x_next = (x0[...].astype(F32) + reduced(part, ring, tokens)).astype(BF16)
    x1[...] = x_next
    u1[...] = norm_rows(x_next.astype(F32)).astype(BF16)
    n1.finish2()
    n2.finish2()
    n1.arrived()
    n2.arrived()
    comm.wait_recv(push_u, u_all.at[1], comm.partner)
    comm.wait_recv(push_s, s_all.at[1], comm.partner)
    wait_local(keep_u)
    wait_local(keep_s)
    comm.wait_sends()


def sds(shape, dtype):
    return jax.ShapeDtypeStruct(shape, dtype)


def sems(n):
    return pltpu.SemaphoreType.DMA((n,))


def hbm():
    return pl.BlockSpec(memory_space=HBM)


def vmem():
    return pl.BlockSpec(memory_space=VMEM)


def params(collective_id):
    return pltpu.CompilerParams(collective_id=collective_id, has_side_effects=True,
                                vmem_limit_bytes=67043328)


def call_forward_first(x0, cot, w_in, w_out):
    tokens, width = x0.shape
    inner = w_in.shape[2]
    group = 4 * tokens
    slice_ = inner // 4
    w1_shape = (4, 4, 2, width // 32, slice_)
    w2_shape = (4, 4, 2, inner // 128, width)
    return pl.pallas_call(
        forward_first,
        name='forward_first',
        out_shape=(sds((tokens, width), BF16), sds((tokens, width), BF16),
                   sds((2, 4, tokens, width), BF16), sds((2, group, slice_), BF16), sds((group, slice_), BF16),
                   sds((4, tokens, width), BF16), sds(w1_shape, BF16), sds(w2_shape, BF16)),
        in_specs=[vmem(), hbm(), hbm(), hbm()],
        out_specs=(vmem(), vmem(), hbm(), hbm(), hbm(), hbm(), hbm(), hbm()),
        scratch_shapes=[VMEM(w1_shape, BF16), VMEM(w2_shape, BF16), VMEM((4, tokens, width), BF16),
                        VMEM((group, slice_), BF16), VMEM((group, slice_), BF16), VMEM((group, width), F32),
                        VMEM((6, tokens, width // 2), F32), VMEM(w1_shape[3:], BF16), VMEM(w2_shape[3:], BF16),
                        sems(96), sems(96), sems(40)],
        compiler_params=params(1),
        cost_estimate=pl.CostEstimate(flops=4 * group * width * slice_, bytes_accessed=1 << 24, transcendentals=0),
    )(x0, cot, w_in, w_out)


def top_layer(x1, u1, cot, cot_all, w1_fwd, w2_fwd, w_in, w_out,
              x2, e1, d0, u_all, s_all, q_half, d_half, w1_back, w2_back, w1_next, w2_next,
              w1, w2, uf, df, a, s, q, part, part_e, landing, landing_e, stages1, stages2,
              send_sems, recv_sems, local_sems):
    comm = Comm(send_sems, recv_sems)
    tokens = x1.shape[0]
    rows1, rows2 = w1.shape[3], w2.shape[3]
    z, y, x, c = comm.z, comm.y, comm.x, comm.c

    strips = start_local(w1_strips(comm, w_in, 1, stages1.at[0], rows1), local_sems, 0)
    strips += start_local([(w2_rows(comm, w_out, 1, rows2), stages2.at[0])], local_sems, 16)
    load1 = start_local([(w1_fwd, w1)], local_sems, 17)
    load2 = start_local([(w2_fwd, w2)], local_sems, 18)
    strips0 = start_local(w1_strips(comm, w_in, 0, stages1.at[1], rows1), local_sems, 19)
    strips0 += start_local([(w2_rows(comm, w_out, 0, rows2), stages2.at[1])], local_sems, 35)
    others = [(x + k) % 4 for k in (1, 2, 3)]
    load_d = start_local([(cot_all.at[p], df.at[p]) for p in others], local_sems, 36)
    df[x] = cot[...]
    uf[x] = u1[...]
    wait_local(strips)
    keep = start_local([(stages1.at[0], w1_back.at[z, y, c]), (stages2.at[0], w2_back.at[y, z, c])], local_sems, 39)
    comm.barrier('xyz')

    half_tokens = tokens // 2
    half_of = lambda h: pl.ds(h * half_tokens, half_tokens)
    gather_u = RingGather(comm, 'x', own=lambda h: uf.at[x, half_of(h)], slot=lambda p, h: uf.at[p, half_of(h)])
    g1 = WeightGather(comm, 'z', 'y', w1_back, stages1.at[0])
    g2 = WeightGather(comm, 'y', 'z', w2_back, stages2.at[0])
    gather_u.start()
    g1.start1()
    g2.start1()
    g1.forward1()
    g2.forward1()
    gather_u.forward()
    wait_local(keep)
    g1.start2()
    g2.start2()
    gather_u.near()
    gather_u.finish()
    push_u = comm.send(uf, u_all.at[1], comm.partner)
    keep_u = start_local([(uf, u_all.at[0])], local_sems, 41)
    wait_local(load1)
    forward_acts(uf, w1, a, s)
    wait_local(load2)
    block = part_block(part, tokens)
    ring = RingReduce(comm, 'x', block, landing)
    forward_part(s, w2, part, 0)
    ring.send_far(0)
    ring.send_near(0)
    g1.forward2()
    g2.forward2()
    forward_part(s, w2, part, 1)
    ring.send_far(1)
    ring.send_near(1)
    push_s = comm.send(s, s_all.at[1], comm.partner)
    keep_s = start_local([(s, s_all.at[0])], local_sems, 42)
    wait_local(load_d)
    mine = lambda ref, k: ref.at[..., pl.ds(pl.multiple_of(k * (ref.shape[-1] // 2), ref.shape[-1] // 2),
                                            ref.shape[-1] // 2)]
    push_d = comm.send(mine(df, 1 - c), d_half.at[1], comm.partner)
    keep_d = start_local([(mine(df, c), d_half.at[0])], local_sems, 43)

    wait_local(strips0)
    keep0 = start_local([(stages1.at[1], w1_next.at[z, y, c]), (stages2.at[1], w2_next.at[y, z, c])], local_sems, 44)
    n1 = WeightGather(comm, 'z', 'y', w1_next, stages1.at[1])
    n2 = WeightGather(comm, 'y', 'z', w2_next, stages2.at[1])
    n1.start1()
    n2.start1()
    ring.middle(add_from(block))
    g2.finish2()
    g1.finish2()
    g2.arrived()
    load2 = start_local([(w2_back, w2)], local_sems, 46)
    g1.arrived()
    load1 = start_local([(w1_back, w1)], local_sems, 47)
    n1.forward1()
    n2.forward1()
    wait_local(load2)
    backward_acts(df, w2, a, q)
    wait_local(keep0)
    n1.start2()
    n2.start2()
    wait_local(load1)
    block_e = part_block(part_e, tokens)
    ring_e = RingReduce(comm, 'x', block_e, landing_e)
    backward_part(q, w1, part_e, 0)
    ring_e.send_far(0)
    ring_e.send_near(0)
    backward_part(q, w1, part_e, 1)
    ring_e.send_far(1)
    ring_e.send_near(1)
    push_q = comm.send(mine(q, 1 - c), q_half.at[1], comm.partner)
    keep_q = start_local([(mine(q, c), q_half.at[0])], local_sems, 48)
    ring.finish()
    xf = x1[...].astype(F32)
    x2[...] = (xf + reduced(part, ring, tokens)).astype(BF16)
    ring_e.middle(add_from(block_e))
    n1.forward2()
    n2.forward2()
    ring_e.finish()
    e = cot[...].astype(F32) + norm_rows_vjp(x1[...].astype(F32), reduced(part_e, ring_e, tokens))
    e1[...] = e
    d0[...] = e.astype(BF16)
    n1.finish2()
    n2.finish2()
    n1.arrived()
    n2.arrived()
    for k, ref in ((push_u, u_all), (push_s, s_all), (push_d, d_half), (push_q, q_half)):
        comm.wait_recv(k, ref.at[1], comm.partner)
    wait_local(keep_u + keep_s + keep_d + keep_q)
    comm.wait_sends()


def call_top_layer(x1, u1, cot, cot_all, w1_fwd, w2_fwd, w_in, w_out):
    tokens, width = x1.shape
    group = 4 * tokens
    slice_ = w_in.shape[2] // 4
    w1_shape, w2_shape = w1_fwd.shape, w2_fwd.shape
    acts = VMEM((group, slice_), BF16)
    parts = VMEM((group, width), F32)
    landing = VMEM((6, tokens, width // 2), F32)
    return pl.pallas_call(
        top_layer,
        name='top_layer',
        out_shape=(sds((tokens, width), BF16), sds((tokens, width), F32), sds((tokens, width), BF16),
                   sds((2, 4, tokens, width), BF16), sds((2, group, slice_), BF16),
                   sds((2, group, slice_ // 2), BF16), sds((2, 4, tokens, width // 2), BF16),
                   sds(w1_shape, BF16), sds(w2_shape, BF16), sds(w1_shape, BF16), sds(w2_shape, BF16)),
        in_specs=[vmem(), vmem(), vmem()] + [hbm()] * 5,
        out_specs=(vmem(), vmem(), vmem()) + (hbm(),) * 8,
        scratch_shapes=[VMEM(w1_shape, BF16), VMEM(w2_shape, BF16), VMEM((4, tokens, width), BF16),
                        VMEM((4, tokens, width), BF16), acts, acts, acts, parts, parts, landing, landing,
                        VMEM((2,) + w1_shape[3:], BF16), VMEM((2,) + w2_shape[3:], BF16),
                        sems(96), sems(96), sems(52)],
        compiler_params=params(2),
        cost_estimate=pl.CostEstimate(flops=8 * group * width * slice_, bytes_accessed=1 << 24, transcendentals=0),
    )(x1, u1, cot, cot_all, w1_fwd, w2_fwd, w_in, w_out)


class GradReduce:
    def __init__(self, comm, axis1, axis2, a, b, first_column, sends, landing1, landing2, result):
        self.comm, self.axis1, self.axis2 = comm, axis1, axis2
        self.a, self.b, self.first_column = a, b, first_column
        self.sends, self.landing2, self.result = sends, landing2, result
        self.half = sends.shape[2]
        self.rows = sends.shape[1]
        self.ring = RingReduce(comm, axis1, None, landing1)

    def product(self, pos, half):
        rows = pl.ds(pl.multiple_of(pos * self.rows, self.rows), self.rows)
        cols = pl.ds(self.first_column + half * self.half, self.half)
        return dot_at(flat(self.a[..., rows]), flat(self.b[..., cols]))

    def start(self):
        ring, sends = self.ring, self.sends
        plan = ((ring.far, 0), (ring.far, 1), (ring.right, 1), (ring.left, 0))
        ring.part = lambda pos, half: sends.at[self.slot]
        for self.slot, (pos, half) in enumerate(plan):
            sends[self.slot] = self.product(pos, half)
            if self.slot < 2:
                ring.send_far(half)
            else:
                ring.send_near(half)

    def middle(self):
        def add(ref, pos, half):
            ref[...] = ref[...] + self.product(pos, half)
        self.ring.middle(add)

    def turn(self):
        ring, sends, landing = self.ring, self.sends, self.ring.landing
        ring.finish()
        self.comm.wait_sends((ring.r0, ring.l0))
        sends[0] = self.product(ring.me, 0) + landing[2] + landing[4]
        sends[1] = self.product(ring.me, 1) + landing[1] + landing[5]
        rows = self.rows // 4
        self.block = lambda pos, half: sends.at[half, pl.ds(pl.multiple_of(pos * rows, rows), rows)]
        self.ring2 = RingReduce(self.comm, self.axis2, self.block, self.landing2)
        self.ring2.start()

    def middle2(self):
        self.ring2.middle(add_from(self.block))

    def finish(self):
        ring, landing, w = self.ring2, self.landing2, self.half
        ring.finish()
        self.result[:, 0:w] = self.block(ring.me, 0)[...] + landing[2] + landing[4]
        self.result[:, w:2 * w] = self.block(ring.me, 1)[...] + landing[1] + landing[5]


CHUNKS = 2


def grad_scratch(width, slice_):
    out = []
    for rows, cols in ((width // 4, slice_ // 2), (slice_ // 4, width // 2)):
        w = cols // CHUNKS // 2
        out += [VMEM((CHUNKS, 4, rows, w), F32), VMEM((CHUNKS, 6, rows, w), F32), VMEM((CHUNKS, 6, rows // 4, w), F32)]
    return out


def grad_reduces(comm, u, q, s, d, bufs, results):
    out = []
    for k in range(CHUNKS):
        for (axis1, axis2, a, b), (sends, land1, land2), result in zip(
                (('z', 'y', u, q), ('y', 'z', s, d)), (bufs[:3], bufs[3:]), results):
            first = k * 2 * sends.shape[3]
            out.append(GradReduce(comm, axis1, axis2, a, b, first, sends.at[k], land1.at[k], land2.at[k], result.at[k]))
    return out


def bottom_layer(x0, e1, d0, w1_hbm, w2_hbm, a_hbm, u_top, s_top, q_top, d_top,
                 grad, q_half, d_half, res_in, res_out,
                 w, df, a, q, part, landing, gu, gs, gq, gd, *rest):
    bufs, (send_sems, recv_sems, local_sems) = rest[:6], rest[6:]
    comm = Comm(send_sems, recv_sems)
    tokens = x0.shape[0]
    x, c = comm.x, comm.c
    loads = start_local([(u_top, gu), (q_top, gq), (s_top, gs), (d_top, gd)], local_sems, 0)
    load2 = start_local([(w2_hbm, w), (a_hbm, a)], local_sems, 4)
    df[x] = d0[...]
    comm.barrier('xyz')

    half_tokens = tokens // 2
    half_of = lambda h: pl.ds(h * half_tokens, half_tokens)
    gather_d = RingGather(comm, 'x', own=lambda h: df.at[x, half_of(h)], slot=lambda p, h: df.at[p, half_of(h)])
    gather_d.start()
    wait_local(loads)
    top = grad_reduces(comm, gu, gq, gs, gd, bufs, (res_in, res_out))
    first, second = top[:2], top[2:]
    for g in first:
        g.start()
    gather_d.forward()
    for g in second:
        g.start()
    gather_d.near()
    gather_d.finish()
    wait_local(load2)
    backward_acts(df, w, a, q)
    load1 = start_local([(w1_hbm, w)], local_sems, 6)
    mine = lambda ref, k: ref.at[..., pl.ds(pl.multiple_of(k * (ref.shape[-1] // 2), ref.shape[-1] // 2),
                                            ref.shape[-1] // 2)]
    push_d = comm.send(mine(df, 1 - c), d_half.at[1], comm.partner)
    push_q = comm.send(mine(q, 1 - c), q_half.at[1], comm.partner)
    keep = start_local([(mine(df, c), d_half.at[0]), (mine(q, c), q_half.at[0])], local_sems, 7)
    for g in first:
        g.middle()
    wait_local(load1)
    block = part_block(part, tokens)
    ring = RingReduce(comm, 'x', block, landing)
    backward_part(q, w, part, 0)
    ring.send_far(0)
    ring.send_near(0)
    backward_part(q, w, part, 1)
    ring.send_far(1)
    ring.send_near(1)
    for g in first:
        g.turn()
    for g in second:
        g.middle()
    ring.middle(add_from(block))
    for g in first:
        g.middle2()
    for g in second:
        g.turn()
    for g in first:
        g.finish()
    ring.finish()
    grad[...] = (e1[...] + norm_rows_vjp(x0[...].astype(F32), reduced(part, ring, tokens))).astype(BF16)
    for g in second:
        g.middle2()
    for g in second:
        g.finish()
    comm.wait_recv(push_d, d_half.at[1], comm.partner)
    comm.wait_recv(push_q, q_half.at[1], comm.partner)
    wait_local(keep)
    comm.wait_sends()


def result_shapes(width, slice_):
    return ((CHUNKS, width // 16, slice_ // 2 // CHUNKS), (CHUNKS, slice_ // 16, width // 2 // CHUNKS))


def call_bottom_layer(x0, e1, d0, w1_hbm, w2_hbm, a_hbm, u_top, s_top, q_top, d_top):
    tokens, width = x0.shape
    group, slice_ = a_hbm.shape
    acts = VMEM((group, slice_), BF16)
    shapes = result_shapes(width, slice_)
    return pl.pallas_call(
        bottom_layer,
        name='bottom_layer',
        out_shape=(sds((tokens, width), BF16), sds(q_top.shape, BF16), sds(d_top.shape, BF16),
                   sds(shapes[0], F32), sds(shapes[1], F32)),
        in_specs=[vmem()] * 3 + [hbm()] * 7,
        out_specs=(vmem(), hbm(), hbm(), vmem(), vmem()),
        scratch_shapes=[VMEM(w1_hbm.shape, BF16), VMEM((4, tokens, width), BF16), acts, acts, VMEM((group, width), F32),
                        VMEM((6, tokens, width // 2), F32), VMEM(u_top.shape, BF16), VMEM(s_top.shape, BF16),
                        VMEM(q_top.shape, BF16), VMEM(d_top.shape, BF16)] + grad_scratch(width, slice_)
        + [sems(80), sems(80), sems(10)],
        compiler_params=params(3),
        cost_estimate=pl.CostEstimate(flops=8 * group * width * slice_, bytes_accessed=1 << 24, transcendentals=0),
    )(x0, e1, d0, w1_hbm, w2_hbm, a_hbm, u_top, s_top, q_top, d_top)


class BlockGather:
    def __init__(self, comm, own, out):
        self.comm, self.own, self.out = comm, own, out
        c = comm.c
        rows = own.shape[0] // 2
        half = lambda h: pl.ds(h * rows, rows)
        self.ring = RingGather(comm, 'x', own=lambda h: own.at[half(h)], slot=lambda p, h: out.at[p, c, half(h)])
        self.pushed = []

    def push(self, pos, src):
        c = self.comm
        self.pushed.append((pos, c.send(src, self.out.at[pos, c.c], c.partner)))

    def start(self):
        self.ring.start()
        self.push(self.ring.me, self.own)

    def forward(self):
        self.ring.forward()

    def near(self):
        ring, c = self.ring, self.comm.c
        ring.near()
        self.push(ring.left, self.out.at[ring.left, c])
        self.push(ring.right, self.out.at[ring.right, c])

    def finish(self):
        ring, c = self.ring, self.comm.c
        ring.finish()
        self.push(ring.far, self.out.at[ring.far, c])

    def arrived(self):
        c = self.comm
        for pos, k in self.pushed:
            c.wait_recv(k, self.out.at[pos, 1 - c.c], c.partner)


def last_grads(u_hbm, q_hbm, s_hbm, d_hbm, top_in, top_out, all_in, all_out,
               gu, gs, gq, gd, res_in, res_out, *rest):
    bufs, (send_sems, recv_sems, local_sems) = rest[:6], rest[6:]
    comm = Comm(send_sems, recv_sems)
    x, c = comm.x, comm.c
    loads = start_local([(u_hbm, gu), (q_hbm, gq), (s_hbm, gs), (d_hbm, gd)], local_sems, 0)
    keep = start_local([(top_in.at[k], all_in.at[1, k, x, c]) for k in range(CHUNKS)]
                       + [(top_out.at[k], all_out.at[1, k, x, c]) for k in range(CHUNKS)], local_sems, 4)
    comm.barrier('xyz')
    wait_local(loads)
    grads = grad_reduces(comm, gu, gq, gs, gd, bufs, (res_in, res_out))
    first, second = grads[:2], grads[2:]
    for g in first:
        g.start()
    for g in second:
        g.start()
    top = []
    for k in range(CHUNKS):
        top += [BlockGather(comm, top_in.at[k], all_in.at[1, k]), BlockGather(comm, top_out.at[k], all_out.at[1, k])]
    for b in top:
        b.start()
    for g in first:
        g.middle()
    for b in top:
        b.forward()
    for b in top:
        b.near()
    for g in first:
        g.turn()
    for g in second:
        g.middle()
    for b in top:
        b.finish()
    for g in first:
        g.middle2()
    for g in second:
        g.turn()
    for g in first:
        g.finish()
    low = [BlockGather(comm, res.at[k], out.at[0, k]) for k in range(CHUNKS)
           for res, out in ((res_in, all_in), (res_out, all_out))]
    for b in low[:2]:
        b.start()
    for g in second:
        g.middle2()
    for b in low[:2]:
        b.forward()
    for g in second:
        g.finish()
    for b in low[2:]:
        b.start()
    keep += start_local([(res_in.at[k], all_in.at[0, k, x, c]) for k in range(CHUNKS)]
                        + [(res_out.at[k], all_out.at[0, k, x, c]) for k in range(CHUNKS)], local_sems, 4 + 2 * CHUNKS)
    for b in low[:2]:
        b.near()
    for b in low[2:]:
        b.forward()
    for b in low[:2]:
        b.finish()
    for b in low[2:]:
        b.near()
    for b in low[2:]:
        b.finish()
    for b in top + low:
        b.arrived()
    wait_local(keep)
    comm.wait_sends()


def call_last_grads(u_hbm, q_hbm, s_hbm, d_hbm, top_in, top_out):
    slice_ = s_hbm.shape[2]
    width = u_hbm.shape[3]
    shapes = result_shapes(width, slice_)
    outs = [sds((2, CHUNKS, 4, 2) + shape[1:], F32) for shape in shapes]
    return pl.pallas_call(
        last_grads,
        name='last_grads',
        out_shape=tuple(outs),
        in_specs=[hbm()] * 4 + [vmem()] * 2,
        out_specs=(hbm(), hbm()),
        scratch_shapes=[VMEM(r.shape, BF16) for r in (u_hbm, s_hbm, q_hbm, d_hbm)] + [VMEM(s, F32) for s in shapes]
        + grad_scratch(width, slice_) + [sems(144), sems(144), sems(4 + 4 * CHUNKS)],
        compiler_params=params(4),
        cost_estimate=pl.CostEstimate(flops=8 * 8 * width * slice_ * 64, bytes_accessed=1 << 24, transcendentals=0),
    )(u_hbm, q_hbm, s_hbm, d_hbm, top_in, top_out)


def solution(mesh):
    tok_spec = P(('local', 'data'), None)
    w_spec = P(None, 'local', None)

    def device_step(tokens, cotangent, w_in, w_out):
        x1, u1, u0_all, s0_all, a0, cot_all, w1_top, w2_top = call_forward_first(tokens, cotangent, w_in, w_out)
        (x2, e1, d0, u1_all, s1_all, q1_half, d1_half, _, _, w1_low, w2_low) = call_top_layer(
            x1, u1, cotangent, cot_all, w1_top, w2_top, w_in, w_out)
        grad, q0_half, d0_half, top_in, top_out = call_bottom_layer(
            tokens, e1, d0, w1_low, w2_low, a0, u1_all, s1_all, q1_half, d1_half)
        all_in, all_out = call_last_grads(u0_all, q0_half, s0_all, d0_half, top_in, top_out)
        rows = w_in.shape[1]
        strip = w_in.shape[2] // 64
        per = 2 // CHUNKS
        grad_in = all_in.reshape(2, CHUNKS, 4, 2, rows, per, 4, strip)
        grad_in = grad_in.transpose(0, 4, 6, 3, 1, 5, 2, 7).reshape(w_in.shape)
        grad_out = all_out.transpose(0, 2, 4, 3, 1, 5).reshape(w_out.shape)
        return x2, grad_in, grad_out, grad

    return jax.shard_map(device_step, mesh=mesh, in_specs=(tok_spec, tok_spec, w_spec, w_spec),
                         out_specs=(tok_spec, w_spec, w_spec, tok_spec), check_vma=False)
```

time: 2550 us -> 527 us (0.21)
  waiting for transfers between devices: 2260 us -> 0 us
  Pallas kernels: 0 us -> 458 us
  matrix products: 238 us -> 0 us
  local copies, waits for them, and re-layouts: 11.4 us -> 61.4 us
    reduce_scatter x4 -> x0, waiting for transfers between devices: 1370 us -> none  [reduce_grad(): lax.psum_scatter(grad_full, 'local', scatter_dimension=0, tiled=True)]
    all_gather x4 -> x0, waiting for transfers between devices: 741 us -> none  [the longest x2 378 us: device_step(): w_first = lax.all_gather(w_in[layer_idx], 'local', axis=0, tiled=True)]
    pallas_call x0 -> x4, Pallas kernels: none -> 458 us  [the longest x1 125 us: call_last_grads(): pl.pallas_call(last_grads, name='last_grads', out_shape=tuple(outs), in_s...]
    dot_general x12 -> x0, matrix products: 238 us -> none  [the longest x2 49.8 us: layer_backward(): lax.dot_general(hidden, grad_b, (((0,), (0,)), ((), ())), preferred_eleme...]
    psum x1 -> x0, waiting for transfers between devices: 148 us -> none  [reduce_grad(): return lax.psum(grad_part, 'data')]
    reshape x0 -> x3, local copies, waits for them, and re-layouts: none -> 32.4 us  [the longest x1 11.9 us: device_step(): grad_out = all_out.transpose(0, 2, 4, 3, 1, 5).reshape(w_out.shape)]
    transpose x0 -> x2, local copies, waits for them, and re-layouts: none -> 27.4 us  [the longest x1 15.4 us: device_step(): grad_out = all_out.transpose(0, 2, 4, 3, 1, 5).reshape(w_out.shape)]
  transfers between devices with their start and end apart: 9 -> 0, of which waited for: 9 -> 0; matrix products, arithmetic and copies ran while one was open for 7% -> 0% of each run, Pallas kernels for 0% -> 0%
where the time goes in v1:
time: 527 us; the launch traced here: 520 us
  Pallas kernels  458 us (87%)
  local copies, waits for them, and re-layouts  61.4 us (12%)
    pallas_call x1, Pallas kernels, call_last_grads(): pl.pallas_call(last_grads, name='last_grads', out_shape=tuple(outs), in_s...  125 us
    pallas_call x1, Pallas kernels, call_top_layer(): pl.pallas_call(top_layer, name='top_layer', out_shape=(sds((tokens, width...  118 us
    pallas_call x1, Pallas kernels, call_forward_first(): pl.pallas_call(forward_first, name='forward_first', out_shape=(sds((token...  113 us
    pallas_call x1, Pallas kernels, call_bottom_layer(): pl.pallas_call(bottom_layer, name='bottom_layer', out_shape=(sds((tokens,...  101 us
    transpose x1, local copies, waits for them, and re-layouts, device_step(): grad_out = all_out.transpose(0, 2, 4, 3, 1, 5).reshape(w_out.shape)  15.4 us
    transpose x1, local copies, waits for them, and re-layouts, device_step(): grad_in = grad_in.transpose(0, 4, 6, 3, 1, 5, 2, 7).reshape(w_in.shape)  12 us
    reshape x1, local copies, waits for them, and re-layouts, device_step(): grad_out = all_out.transpose(0, 2, 4, 3, 1, 5).reshape(w_out.shape)  11.9 us

profile of v1, /device:TPU:1, one launch (start us, length us, event | category | flops | bytes accessed | tf_op | source)
XLA Modules:
  0.0 520.1 jit_solution(1644989267929604356)
XLA Ops:
  0.6 112.9 %forward_first.1 = (bf16[128,2048]{1,0:T(8,128)(2,1)}, bf16[128,2048]{1,0:T(8,128)(2,1)}, bf16[2,4,128,2048]{3,2,1,0:T(8,128)(2,1)}, bf16[2,512,2048]{2,1,0:T(8,...) custom-call(bf16[128,2048]{1,0:T(8,128)(2,1)} %x0.3, ...), custom_call_target="tpu_custom_call" | custom-call | flops 8589934592 | bytes 16777216 | tf_op jit(solution)/shard_map/forward_first/pallas_call | solution.py:459
  113.5 118.2 %top_layer.1 = (bf16[128,2048]{1,0:T(8,128)(2,1)}, f32[128,2048]{1,0:T(8,128)}, bf16[128,2048]{1,0:T(8,128)(2,1)}, bf16[2,4,128,2048]{3,2,1,0:T(8,128)(2,1)}, bf...) custom-call(bf16[128,2048]{1,0:T(8,128)(2,1)} %get-tuple-element.28., ...), custom_call_target="tpu_custom_call" | custom-call | flops 17179869184 | bytes 16777216 | tf_op jit(solution)/shard_map/top_layer/pallas_call | solution.py:597
  231.7 101.3 %bottom_layer.1 = (bf16[128,2048]{1,0:T(8,128)(2,1)}, bf16[2,512,1024]{2,1,0:T(8,128)(2,1)}, bf16[2,4,128,1024]{3,2,1,0:T(8,128)(2,1)}, f32[2,128,512]{2,1,0:T(8,128)}, f32[2,128,512]{2,1,0:T(8,128)}) custom-call(bf16[128,2048]{1,0:T(8,128)(2,1)} %x0.3, f32[128,2048]{1,0:T(8,128)} %get-tuple-element.35.e1, bf16[128,2048]{1,0:T(8,128)(2,1)} %get-tuple-element.36.d0, ...), custom_call_target="tpu_custom_call" | custom-call | flops 17179869184 | bytes 16777216 | tf_op jit(solution)/shard_map/bottom_layer/pallas_call | solution.py:764
  333.0 125.2 %last_grads.1 = (f32[2,2,4,2,128,512]{5,4,3,2,1,0:T(8,128)}, f32[2,2,4,2,128,512]{5,4,3,2,1,0:T(8,128)}) custom-call(bf16[2,4,128,2048]{3,2,1,0:T(8,128)(2,1)} %get-tuple-element.34.u_hbm, bf16[2,512,1024]{2,1,0:T(8,128)(2,1)} %get-tuple-element.44.q_hbm, bf16[2,512,2048]{2,1,0:T(8,128)(2,1)} %get-tuple-element.45.s_hbm, ...), custom_call_target="tpu_custom_call" | custom-call | flops 17179869184 | bytes 16777216 | tf_op jit(solution)/shard_map/last_grads/pallas_call | solution.py:891
  458.2 10.1 %reshape.17 = f32[2,2,4,2,128,1,4,128]{7,6,4,3,2,1,0,5:T(4,128)} reshape(f32[2,2,4,2,128,512]{5,4,3,2,1,0:T(8,128)} %get-tuple-element.49) | data formatting | bytes 16777216 | tf_op jit(solution)/shard_map/reshape | solution.py:918
  468.3 12.0 %copy.9 = f32[2,128,4,2,2,1,4,128]{7,6,4,3,2,1,0,5:T(4,128)} copy(f32[2,128,4,2,2,1,4,128]{7,2,1,3,6,4,0,5:T(4,128)} %bitcast.6) | data formatting | bytes 16777216 | tf_op jit(solution)/shard_map/transpose | solution.py:919
  480.3 10.5 %reshape.18 = f32[2,128,8192]{2,1,0:T(8,128)} reshape(f32[2,128,4,2,2,1,4,128]{7,6,4,3,2,1,0,5:T(4,128)} %copy.9) | data formatting | bytes 16777216 | tf_op jit(solution)/shard_map/reshape | solution.py:919
  490.8 15.4 %copy.10 = f32[2,4,128,2,2,512]{5,4,3,2,1,0:T(2,128)} copy(f32[2,4,128,2,2,512]{5,2,3,1,4,0:T(8,128)} %bitcast.7) | data formatting | bytes 16777216 | tf_op jit(solution)/shard_map/transpose | solution.py:920
  506.2 0.0 copy-start
  506.2 0.0 copy-start.1
  506.2 11.9 %reshape.19 = f32[2,512,2048]{2,1,0:T(8,128)} reshape(f32[2,4,128,2,2,512]{5,4,3,2,1,0:T(2,128)} %copy.10) | data formatting | bytes 16777216 | tf_op jit(solution)/shard_map/reshape | solution.py:920
  518.1 0.0 copy-done
  518.1 0.8 copy.13
  518.9 0.0 copy-done.1
  518.9 0.8 copy.14
Async XLA Ops:
  506.2 11.9 %copy-start = (bf16[128,2048]{1,0:T(8,128)(2,1)S(1)}, bf16[128,2048]{1,0:T(8,128)(2,1)}, u32[]{:S(2)}) copy-start(bf16[128,2048]{1,0:T(8,128)(2,1)} %get-tuple-element.56) | copy-start | bytes 1572868
  506.2 12.7 %copy-start.1 = (bf16[128,2048]{1,0:T(8,128)(2,1)S(1)}, bf16[128,2048]{1,0:T(8,128)(2,1)}, u32[]{:S(2)}) copy-start(bf16[128,2048]{1,0:T(8,128)(2,1)} %get-tuple-element.59) | copy-start | bytes 1572868

commit v2 on v1

--- a/solution.py
+++ b/solution.py
@@ -133,14 +133,21 @@
         self.send_near(1)
         self.send_near(0)
 
-    def middle(self, add):
+    def middle_right(self, add):
         c, landing = self.comm, self.landing
         c.wait_recv(self.r0, landing.at[0], self.to_left)
         add(landing.at[0], self.right, 0)
         self.r2 = c.send(landing.at[0], landing.at[2], self.to_right)
+
+    def middle_left(self, add):
+        c, landing = self.comm, self.landing
         c.wait_recv(self.l0, landing.at[3], self.to_right)
         add(landing.at[3], self.left, 1)
         self.l2 = c.send(landing.at[3], landing.at[5], self.to_left)
+
+    def middle(self, add):
+        self.middle_right(add)
+        self.middle_left(add)
 
     def finish(self):
         c, landing = self.comm, self.landing
@@ -156,19 +163,34 @@
     return add
 
 
-class WeightGather:
-    def __init__(self, comm, first, second, full, own):
-        self.comm, self.full, self.second = comm, full, second
+class HalfGather:
+    def __init__(self, comm, dims, first, full, own, part):
+        self.comm, self.full = comm, full
         c = comm.c
+        lead = dims[0] == first
+        second = dims[1] if lead else dims[0]
         b = comm.pos(second)
-        half_rows = full.shape[3] // 2
+        half_rows, width = full.shape[3] // 2, full.shape[4] // 2
         rows = lambda h: pl.ds(h * half_rows, half_rows)
-        self.b = b
-        self.ring1 = RingGather(comm, first, own=lambda h: own.at[rows(h)],
-                                slot=lambda p, h: full.at[p, b, c, rows(h)])
-        pair = lambda p, h: full.at[pl.ds(2 * h, 2), p, c]
-        self.ring2 = RingGather(comm, second, own=lambda h: pair(b, h), slot=pair)
+        self.cols = cols = pl.ds(part * width, width)
+        self.b, self.lead = b, lead
+        if lead:
+            slot1 = lambda p, h: full.at[p, b, c, rows(h), cols]
+            slot2 = lambda p, h: full.at[pl.ds(2 * h, 2), p, c, :, cols]
+        else:
+            slot1 = lambda p, h: full.at[b, p, c, rows(h), cols]
+            slot2 = lambda p, h: full.at[p, pl.ds(2 * h, 2), c, :, cols]
+        self.ring1 = RingGather(comm, first, own=lambda h: own.at[rows(h), cols], slot=slot1)
+        self.ring2 = RingGather(comm, second, own=lambda h: slot2(b, h), slot=slot2)
         self.pushed = []
+
+    def line(self, p, core):
+        return self.full.at[:, p, core, :, self.cols] if self.lead else self.full.at[p, :, core, :, self.cols]
+
+    def push(self, p):
+        c = self.comm
+        mine = self.line(p, c.c)
+        self.pushed.append((p, c.send(mine, mine, c.partner)))
 
     def start1(self):
         self.ring1.start()
@@ -182,11 +204,6 @@
         self.ring2.start()
         self.push(self.b)
 
-    def push(self, p):
-        c = self.comm
-        mine = self.full.at[:, p, c.c]
-        self.pushed.append((p, c.send(mine, mine, c.partner)))
-
     def forward2(self):
         self.ring2.forward()
         self.ring2.near()
@@ -200,7 +217,18 @@
     def arrived(self):
         c = self.comm
         for p, k in self.pushed:
-            c.wait_recv(k, self.full.at[:, p, 1 - c.c], c.partner)
+            c.wait_recv(k, self.line(p, 1 - c.c), c.partner)
+
+
+class WeightGather:
+    def __init__(self, comm, dims, full, own):
+        self.halves = [HalfGather(comm, dims, dims[k], full, own, k) for k in (0, 1)]
+
+    def __getattr__(self, step):
+        def run():
+            for half in self.halves:
+                getattr(half, step)()
+        return run
 
 
 def start_local(copies, sems, first):
@@ -353,7 +381,6 @@
     strips += start_local([(w2_rows(comm, w_out, 0, rows2), own2)], local_sems, 16)
     strips1 = start_local(w1_strips(comm, w_in, 1, stage1, rows1), local_sems, 17)
     strips1 += start_local([(w2_rows(comm, w_out, 1, rows2), stage2)], local_sems, 33)
-
     uf[x] = norm_rows(x0[...].astype(F32)).astype(BF16)
     comm.barrier('xyz')
 
@@ -362,62 +389,61 @@
     gather_u = RingGather(comm, 'x', own=lambda h: uf.at[x, half_of(h)], slot=lambda p, h: uf.at[p, half_of(h)])
     gather_cot = RingGather(comm, 'x', own=lambda h: cot.at[half_of(h)], slot=lambda p, h: cot_all.at[p, half_of(h)])
     wait_local(strips)
-    g1 = WeightGather(comm, 'z', 'y', w1, own1)
-    g2 = WeightGather(comm, 'y', 'z', w2, own2)
+    g1 = WeightGather(comm, 'zy', w1, own1)
+    g2 = WeightGather(comm, 'yz', w2, own2)
+    n1 = WeightGather(comm, 'zy', w1_next, stage1)
+    n2 = WeightGather(comm, 'yz', w2_next, stage2)
     g1.start1()
+    gather_u.start()
     g2.start1()
-    gather_u.start()
+    wait_local(strips1)
+    keep = start_local([(stage1, w1_next.at[z, y, c]), (stage2, w2_next.at[y, z, c])], local_sems, 34)
     g1.forward1()
-    g2.forward1()
     gather_u.forward()
     gather_cot.start()
+    g2.forward1()
     g1.start2()
+    g1.forward2()
     g2.start2()
-
-    wait_local(strips1)
-    n1 = WeightGather(comm, 'z', 'y', w1_next, stage1)
-    n2 = WeightGather(comm, 'y', 'z', w2_next, stage2)
-    keep = start_local([(stage1, w1_next.at[z, y, c]), (stage2, w2_next.at[y, z, c])], local_sems, 34)
-
     gather_u.near()
     gather_u.finish()
     push_u = comm.send(uf, u_all.at[1], comm.partner)
     keep_u = start_local([(uf, u_all.at[0])], local_sems, 36)
     gather_cot.forward()
-    g1.forward2()
-    g2.forward2()
-    wait_local(keep)
     n1.start1()
     n2.start1()
+    g1.finish2()
+    g1.arrived()
+    forward_acts(uf, w1, a, s)
+    g2.forward2()
     gather_cot.near()
     gather_cot.finish()
-    g1.finish2()
-    g2.finish2()
-    g1.arrived()
+    push_s = comm.send(s, s_all.at[1], comm.partner)
+    keep_s = start_local([(s, s_all.at[0]), (a, a_out)], local_sems, 37)
     n1.forward1()
     n2.forward1()
-    forward_acts(uf, w1, a, s)
+    g2.finish2()
     g2.arrived()
     block = part_block(part, tokens)
     ring = RingReduce(comm, 'x', block, landing)
     forward_part(s, w2, part, 0)
     ring.send_far(0)
     ring.send_near(0)
+    wait_local(keep)
     n1.start2()
-    n2.start2()
     forward_part(s, w2, part, 1)
     ring.send_far(1)
     ring.send_near(1)
-    push_s = comm.send(s, s_all.at[1], comm.partner)
-    keep_s = start_local([(s, s_all.at[0]), (a, a_out)], local_sems, 37)
-    ring.middle(add_from(block))
     n1.forward2()
+    n2.start2()
+    ring.middle_right(add_from(block))
+    n1.finish2()
     n2.forward2()
+    ring.middle_left(add_from(block))
     ring.finish()
     x_next = (x0[...].astype(F32) + reduced(part, ring, tokens)).astype(BF16)
     x1[...] = x_next
     u1[...] = norm_rows(x_next.astype(F32)).astype(BF16)
-    n1.finish2()
     n2.finish2()
     n1.arrived()
     n2.arrived()
@@ -467,119 +493,109 @@
         scratch_shapes=[VMEM(w1_shape, BF16), VMEM(w2_shape, BF16), VMEM((4, tokens, width), BF16),
                         VMEM((group, slice_), BF16), VMEM((group, slice_), BF16), VMEM((group, width), F32),
                         VMEM((6, tokens, width // 2), F32), VMEM(w1_shape[3:], BF16), VMEM(w2_shape[3:], BF16),
-                        sems(96), sems(96), sems(40)],
+                        sems(160), sems(160), sems(40)],
         compiler_params=params(1),
         cost_estimate=pl.CostEstimate(flops=4 * group * width * slice_, bytes_accessed=1 << 24, transcendentals=0),
     )(x0, cot, w_in, w_out)
 
 
+def last_dim_half(ref, k):
+    width = ref.shape[-1] // 2
+    return ref.at[..., pl.ds(pl.multiple_of(k * width, width), width)]
+
+
 def top_layer(x1, u1, cot, cot_all, w1_fwd, w2_fwd, w_in, w_out,
-              x2, e1, d0, u_all, s_all, q_half, d_half, w1_back, w2_back, w1_next, w2_next,
-              w1, w2, uf, df, a, s, q, part, part_e, landing, landing_e, stages1, stages2,
+              e1, d0, part_out, u_all, s_all, q_half, d_half, w1_next, w2_next,
+              w1, w2, w1_back, w2_back, uf, df, a, s, q, part, landing, stage1, stage2,
               send_sems, recv_sems, local_sems):
     comm = Comm(send_sems, recv_sems)
     tokens = x1.shape[0]
     rows1, rows2 = w1.shape[3], w2.shape[3]
     z, y, x, c = comm.z, comm.y, comm.x, comm.c
 
-    strips = start_local(w1_strips(comm, w_in, 1, stages1.at[0], rows1), local_sems, 0)
-    strips += start_local([(w2_rows(comm, w_out, 1, rows2), stages2.at[0])], local_sems, 16)
+    own1, own2 = w1_back.at[z, y, c], w2_back.at[y, z, c]
+    strips = start_local(w1_strips(comm, w_in, 1, own1, rows1), local_sems, 0)
+    strips += start_local([(w2_rows(comm, w_out, 1, rows2), own2)], local_sems, 16)
     load1 = start_local([(w1_fwd, w1)], local_sems, 17)
-    load2 = start_local([(w2_fwd, w2)], local_sems, 18)
-    strips0 = start_local(w1_strips(comm, w_in, 0, stages1.at[1], rows1), local_sems, 19)
-    strips0 += start_local([(w2_rows(comm, w_out, 0, rows2), stages2.at[1])], local_sems, 35)
     others = [(x + k) % 4 for k in (1, 2, 3)]
     load_d = start_local([(cot_all.at[p], df.at[p]) for p in others], local_sems, 36)
+    load2 = start_local([(w2_fwd, w2)], local_sems, 18)
+    strips0 = start_local(w1_strips(comm, w_in, 0, stage1, rows1), local_sems, 19)
+    strips0 += start_local([(w2_rows(comm, w_out, 0, rows2), stage2)], local_sems, 35)
     df[x] = cot[...]
     uf[x] = u1[...]
-    wait_local(strips)
-    keep = start_local([(stages1.at[0], w1_back.at[z, y, c]), (stages2.at[0], w2_back.at[y, z, c])], local_sems, 39)
     comm.barrier('xyz')
 
     half_tokens = tokens // 2
     half_of = lambda h: pl.ds(h * half_tokens, half_tokens)
     gather_u = RingGather(comm, 'x', own=lambda h: uf.at[x, half_of(h)], slot=lambda p, h: uf.at[p, half_of(h)])
-    g1 = WeightGather(comm, 'z', 'y', w1_back, stages1.at[0])
-    g2 = WeightGather(comm, 'y', 'z', w2_back, stages2.at[0])
+    g1 = WeightGather(comm, 'zy', w1_back, own1)
+    g2 = WeightGather(comm, 'yz', w2_back, own2)
+    n1 = WeightGather(comm, 'zy', w1_next, stage1)
+    n2 = WeightGather(comm, 'yz', w2_next, stage2)
     gather_u.start()
+    wait_local(strips)
+    g2.start1()
     g1.start1()
-    g2.start1()
-    g1.forward1()
     g2.forward1()
     gather_u.forward()
-    wait_local(keep)
+    g1.forward1()
+    g2.start2()
+    wait_local(strips0)
+    keep = start_local([(stage1, w1_next.at[z, y, c]), (stage2, w2_next.at[y, z, c])], local_sems, 39)
+    g2.forward2()
     g1.start2()
-    g2.start2()
     gather_u.near()
     gather_u.finish()
     push_u = comm.send(uf, u_all.at[1], comm.partner)
     keep_u = start_local([(uf, u_all.at[0])], local_sems, 41)
     wait_local(load1)
     forward_acts(uf, w1, a, s)
-    wait_local(load2)
-    block = part_block(part, tokens)
-    ring = RingReduce(comm, 'x', block, landing)
-    forward_part(s, w2, part, 0)
-    ring.send_far(0)
-    ring.send_near(0)
-    g1.forward2()
-    g2.forward2()
-    forward_part(s, w2, part, 1)
-    ring.send_far(1)
-    ring.send_near(1)
+    n2.start1()
+    n1.start1()
+    g2.finish2()
     push_s = comm.send(s, s_all.at[1], comm.partner)
     keep_s = start_local([(s, s_all.at[0])], local_sems, 42)
     wait_local(load_d)
-    mine = lambda ref, k: ref.at[..., pl.ds(pl.multiple_of(k * (ref.shape[-1] // 2), ref.shape[-1] // 2),
-                                            ref.shape[-1] // 2)]
-    push_d = comm.send(mine(df, 1 - c), d_half.at[1], comm.partner)
-    keep_d = start_local([(mine(df, c), d_half.at[0])], local_sems, 43)
-
-    wait_local(strips0)
-    keep0 = start_local([(stages1.at[1], w1_next.at[z, y, c]), (stages2.at[1], w2_next.at[y, z, c])], local_sems, 44)
-    n1 = WeightGather(comm, 'z', 'y', w1_next, stages1.at[1])
-    n2 = WeightGather(comm, 'y', 'z', w2_next, stages2.at[1])
-    n1.start1()
-    n2.start1()
-    ring.middle(add_from(block))
-    g2.finish2()
+    push_d = comm.send(last_dim_half(df, 1 - c), d_half.at[1], comm.partner)
+    keep_d = start_local([(last_dim_half(df, c), d_half.at[0])], local_sems, 43)
+    g2.arrived()
+    backward_acts(df, w2_back, a, q)
+    g1.forward2()
+    n2.forward1()
+    n1.forward1()
+    wait_local(load2)
+    forward_part(s, w2, part, 0)
+    forward_part(s, w2, part, 1)
+    keep_part = start_local([(part, part_out)], local_sems, 44)
+    push_q = comm.send(last_dim_half(q, 1 - c), q_half.at[1], comm.partner)
+    keep_q = start_local([(last_dim_half(q, c), q_half.at[0])], local_sems, 45)
+    wait_local(keep)
     g1.finish2()
-    g2.arrived()
-    load2 = start_local([(w2_back, w2)], local_sems, 46)
+    n2.start2()
     g1.arrived()
-    load1 = start_local([(w1_back, w1)], local_sems, 47)
-    n1.forward1()
-    n2.forward1()
-    wait_local(load2)
-    backward_acts(df, w2, a, q)
-    wait_local(keep0)
+    wait_local(keep_part)
+    block = part_block(part, tokens)
+    ring = RingReduce(comm, 'x', block, landing)
+    backward_part(q, w1_back, part, 0)
+    ring.send_far(0)
+    ring.send_near(0)
+    backward_part(q, w1_back, part, 1)
+    ring.send_far(1)
+    ring.send_near(1)
+    n2.forward2()
     n1.start2()
-    n2.start2()
-    wait_local(load1)
-    block_e = part_block(part_e, tokens)
-    ring_e = RingReduce(comm, 'x', block_e, landing_e)
-    backward_part(q, w1, part_e, 0)
-    ring_e.send_far(0)
-    ring_e.send_near(0)
-    backward_part(q, w1, part_e, 1)
-    ring_e.send_far(1)
-    ring_e.send_near(1)
-    push_q = comm.send(mine(q, 1 - c), q_half.at[1], comm.partner)
-    keep_q = start_local([(mine(q, c), q_half.at[0])], local_sems, 48)
+    ring.middle_right(add_from(block))
+    n2.finish2()
+    n1.forward2()
+    ring.middle_left(add_from(block))
     ring.finish()
-    xf = x1[...].astype(F32)
-    x2[...] = (xf + reduced(part, ring, tokens)).astype(BF16)
-    ring_e.middle(add_from(block_e))
-    n1.forward2()
-    n2.forward2()
-    ring_e.finish()
-    e = cot[...].astype(F32) + norm_rows_vjp(x1[...].astype(F32), reduced(part_e, ring_e, tokens))
+    e = cot[...].astype(F32) + norm_rows_vjp(x1[...].astype(F32), reduced(part, ring, tokens))
     e1[...] = e
     d0[...] = e.astype(BF16)
     n1.finish2()
-    n2.finish2()
+    n2.arrived()
     n1.arrived()
-    n2.arrived()
     for k, ref in ((push_u, u_all), (push_s, s_all), (push_d, d_half), (push_q, q_half)):
         comm.wait_recv(k, ref.at[1], comm.partner)
     wait_local(keep_u + keep_s + keep_d + keep_q)
@@ -592,21 +608,20 @@
     slice_ = w_in.shape[2] // 4
     w1_shape, w2_shape = w1_fwd.shape, w2_fwd.shape
     acts = VMEM((group, slice_), BF16)
-    parts = VMEM((group, width), F32)
-    landing = VMEM((6, tokens, width // 2), F32)
     return pl.pallas_call(
         top_layer,
         name='top_layer',
-        out_shape=(sds((tokens, width), BF16), sds((tokens, width), F32), sds((tokens, width), BF16),
+        out_shape=(sds((tokens, width), F32), sds((tokens, width), BF16), sds((group, width), F32),
                    sds((2, 4, tokens, width), BF16), sds((2, group, slice_), BF16),
                    sds((2, group, slice_ // 2), BF16), sds((2, 4, tokens, width // 2), BF16),
-                   sds(w1_shape, BF16), sds(w2_shape, BF16), sds(w1_shape, BF16), sds(w2_shape, BF16)),
+                   sds(w1_shape, BF16), sds(w2_shape, BF16)),
         in_specs=[vmem(), vmem(), vmem()] + [hbm()] * 5,
-        out_specs=(vmem(), vmem(), vmem()) + (hbm(),) * 8,
-        scratch_shapes=[VMEM(w1_shape, BF16), VMEM(w2_shape, BF16), VMEM((4, tokens, width), BF16),
-                        VMEM((4, tokens, width), BF16), acts, acts, acts, parts, parts, landing, landing,
-                        VMEM((2,) + w1_shape[3:], BF16), VMEM((2,) + w2_shape[3:], BF16),
-                        sems(96), sems(96), sems(52)],
+        out_specs=(vmem(), vmem()) + (hbm(),) * 7,
+        scratch_shapes=[VMEM(w1_shape, BF16), VMEM(w2_shape, BF16), VMEM(w1_shape, BF16), VMEM(w2_shape, BF16),
+                        VMEM((4, tokens, width), BF16), VMEM((4, tokens, width), BF16), acts, acts, acts,
+                        VMEM((group, width), F32), VMEM((6, tokens, width // 2), F32),
+                        VMEM(w1_shape[3:], BF16), VMEM(w2_shape[3:], BF16),
+                        sems(160), sems(160), sems(48)],
         compiler_params=params(2),
         cost_estimate=pl.CostEstimate(flops=8 * group * width * slice_, bytes_accessed=1 << 24, transcendentals=0),
     )(x1, u1, cot, cot_all, w1_fwd, w2_fwd, w_in, w_out)
@@ -621,33 +636,40 @@
         self.rows = sends.shape[1]
         self.ring = RingReduce(comm, axis1, None, landing1)
 
-    def product(self, pos, half):
-        rows = pl.ds(pl.multiple_of(pos * self.rows, self.rows), self.rows)
-        cols = pl.ds(self.first_column + half * self.half, self.half)
-        return dot_at(flat(self.a[..., rows]), flat(self.b[..., cols]))
+    def product(self, ref, pos, half, landed=()):
+        t = tile_of(self.rows)
+        cols = pl.ds(pl.multiple_of(self.first_column + half * self.half, self.half), self.half)
+
+        def step(i, _):
+            rows = pl.ds(pl.multiple_of(i * t, t), t)
+            columns = pl.ds(pl.multiple_of(pos * self.rows + i * t, t), t)
+            value = dot_at(flat(self.a[..., columns]), flat(self.b[..., cols]))
+            for other in landed:
+                value = value + other[rows]
+            ref[rows] = value
+            return 0
+
+        lax.fori_loop(0, self.rows // t, step, 0)
 
     def start(self):
         ring, sends = self.ring, self.sends
-        plan = ((ring.far, 0), (ring.far, 1), (ring.right, 1), (ring.left, 0))
-        ring.part = lambda pos, half: sends.at[self.slot]
-        for self.slot, (pos, half) in enumerate(plan):
-            sends[self.slot] = self.product(pos, half)
+        for self.slot, (pos, half) in enumerate(((ring.far, 0), (ring.far, 1), (ring.right, 1), (ring.left, 0))):
+            self.product(sends.at[self.slot], pos, half)
+            ring.part = lambda pos, half: sends.at[self.slot]
             if self.slot < 2:
                 ring.send_far(half)
             else:
                 ring.send_near(half)
 
     def middle(self):
-        def add(ref, pos, half):
-            ref[...] = ref[...] + self.product(pos, half)
-        self.ring.middle(add)
+        self.ring.middle(lambda ref, pos, half: self.product(ref, pos, half, (ref,)))
 
     def turn(self):
         ring, sends, landing = self.ring, self.sends, self.ring.landing
         ring.finish()
         self.comm.wait_sends((ring.r0, ring.l0))
-        sends[0] = self.product(ring.me, 0) + landing[2] + landing[4]
-        sends[1] = self.product(ring.me, 1) + landing[1] + landing[5]
+        self.product(sends.at[0], ring.me, 0, (landing.at[2], landing.at[4]))
+        self.product(sends.at[1], ring.me, 1, (landing.at[1], landing.at[5]))
         rows = self.rows // 4
         self.block = lambda pos, half: sends.at[half, pl.ds(pl.multiple_of(pos * rows, rows), rows)]
         self.ring2 = RingReduce(self.comm, self.axis2, self.block, self.landing2)
@@ -663,25 +685,31 @@
         self.result[:, w:2 * w] = self.block(ring.me, 1)[...] + landing[1] + landing[5]
 
 
-CHUNKS = 2
-
-
-def grad_scratch(width, slice_):
+TOP_CHUNKS = 2
+LOW_CHUNKS = 4
+
+
+def grad_scratch(width, slice_, chunks):
     out = []
     for rows, cols in ((width // 4, slice_ // 2), (slice_ // 4, width // 2)):
-        w = cols // CHUNKS // 2
-        out += [VMEM((CHUNKS, 4, rows, w), F32), VMEM((CHUNKS, 6, rows, w), F32), VMEM((CHUNKS, 6, rows // 4, w), F32)]
+        w = cols // chunks // 2
+        out += [VMEM((chunks, 4, rows, w), F32), VMEM((chunks, 6, rows, w), F32), VMEM((chunks, 6, rows // 4, w), F32)]
     return out
 
 
-def grad_reduces(comm, u, q, s, d, bufs, results):
-    out = []
-    for k in range(CHUNKS):
-        for (axis1, axis2, a, b), (sends, land1, land2), result in zip(
-                (('z', 'y', u, q), ('y', 'z', s, d)), (bufs[:3], bufs[3:]), results):
+class GradPair:
+    def __init__(self, comm, k, u, q, s, d, bufs, results):
+        self.both = []
+        for axes, a, b, (sends, land1, land2), result in zip(('zy', 'yz'), (u, s), (q, d), (bufs[:3], bufs[3:]), results):
             first = k * 2 * sends.shape[3]
-            out.append(GradReduce(comm, axis1, axis2, a, b, first, sends.at[k], land1.at[k], land2.at[k], result.at[k]))
-    return out
+            self.both.append(GradReduce(comm, axes[0], axes[1], a, b, first,
+                                        sends.at[k], land1.at[k], land2.at[k], result.at[k]))
+
+    def __getattr__(self, step):
+        def run():
+            for grad in self.both:
+                getattr(grad, step)()
+        return run
 
 
 def bottom_layer(x0, e1, d0, w1_hbm, w2_hbm, a_hbm, u_top, s_top, q_top, d_top,
@@ -701,25 +729,19 @@
     gather_d = RingGather(comm, 'x', own=lambda h: df.at[x, half_of(h)], slot=lambda p, h: df.at[p, half_of(h)])
     gather_d.start()
     wait_local(loads)
-    top = grad_reduces(comm, gu, gq, gs, gd, bufs, (res_in, res_out))
-    first, second = top[:2], top[2:]
-    for g in first:
-        g.start()
+    t0, t1 = [GradPair(comm, k, gu, gq, gs, gd, bufs, (res_in, res_out)) for k in range(TOP_CHUNKS)]
+    t0.start()
     gather_d.forward()
-    for g in second:
-        g.start()
+    t1.start()
     gather_d.near()
     gather_d.finish()
     wait_local(load2)
     backward_acts(df, w, a, q)
     load1 = start_local([(w1_hbm, w)], local_sems, 6)
-    mine = lambda ref, k: ref.at[..., pl.ds(pl.multiple_of(k * (ref.shape[-1] // 2), ref.shape[-1] // 2),
-                                            ref.shape[-1] // 2)]
-    push_d = comm.send(mine(df, 1 - c), d_half.at[1], comm.partner)
-    push_q = comm.send(mine(q, 1 - c), q_half.at[1], comm.partner)
-    keep = start_local([(mine(df, c), d_half.at[0]), (mine(q, c), q_half.at[0])], local_sems, 7)
-    for g in first:
-        g.middle()
+    push_d = comm.send(last_dim_half(df, 1 - c), d_half.at[1], comm.partner)
+    push_q = comm.send(last_dim_half(q, 1 - c), q_half.at[1], comm.partner)
+    keep = start_local([(last_dim_half(df, c), d_half.at[0]), (last_dim_half(q, c), q_half.at[0])], local_sems, 7)
+    t0.middle()
     wait_local(load1)
     block = part_block(part, tokens)
     ring = RingReduce(comm, 'x', block, landing)
@@ -729,38 +751,31 @@
     backward_part(q, w, part, 1)
     ring.send_far(1)
     ring.send_near(1)
-    for g in first:
-        g.turn()
-    for g in second:
-        g.middle()
+    t1.middle()
     ring.middle(add_from(block))
-    for g in first:
-        g.middle2()
-    for g in second:
-        g.turn()
-    for g in first:
-        g.finish()
+    t0.turn()
+    t0.middle2()
     ring.finish()
     grad[...] = (e1[...] + norm_rows_vjp(x0[...].astype(F32), reduced(part, ring, tokens))).astype(BF16)
-    for g in second:
-        g.middle2()
-    for g in second:
-        g.finish()
+    t0.finish()
+    t1.turn()
+    t1.middle2()
+    t1.finish()
     comm.wait_recv(push_d, d_half.at[1], comm.partner)
     comm.wait_recv(push_q, q_half.at[1], comm.partner)
     wait_local(keep)
     comm.wait_sends()
 
 
-def result_shapes(width, slice_):
-    return ((CHUNKS, width // 16, slice_ // 2 // CHUNKS), (CHUNKS, slice_ // 16, width // 2 // CHUNKS))
+def result_shapes(width, slice_, chunks):
+    return ((chunks, width // 16, slice_ // 2 // chunks), (chunks, slice_ // 16, width // 2 // chunks))
 
 
 def call_bottom_layer(x0, e1, d0, w1_hbm, w2_hbm, a_hbm, u_top, s_top, q_top, d_top):
     tokens, width = x0.shape
     group, slice_ = a_hbm.shape
     acts = VMEM((group, slice_), BF16)
-    shapes = result_shapes(width, slice_)
+    shapes = result_shapes(width, slice_, TOP_CHUNKS)
     return pl.pallas_call(
         bottom_layer,
         name='bottom_layer',
@@ -770,7 +785,7 @@
         out_specs=(vmem(), hbm(), hbm(), vmem(), vmem()),
         scratch_shapes=[VMEM(w1_hbm.shape, BF16), VMEM((4, tokens, width), BF16), acts, acts, VMEM((group, width), F32),
                         VMEM((6, tokens, width // 2), F32), VMEM(u_top.shape, BF16), VMEM(s_top.shape, BF16),
-                        VMEM(q_top.shape, BF16), VMEM(d_top.shape, BF16)] + grad_scratch(width, slice_)
+                        VMEM(q_top.shape, BF16), VMEM(d_top.shape, BF16)] + grad_scratch(width, slice_, TOP_CHUNKS)
         + [sems(80), sems(80), sems(10)],
         compiler_params=params(3),
         cost_estimate=pl.CostEstimate(flops=8 * group * width * slice_, bytes_accessed=1 << 24, transcendentals=0),
@@ -814,91 +829,151 @@
             c.wait_recv(k, self.out.at[pos, 1 - c.c], c.partner)
 
 
-def last_grads(u_hbm, q_hbm, s_hbm, d_hbm, top_in, top_out, all_in, all_out,
-               gu, gs, gq, gd, res_in, res_out, *rest):
+class PairGather:
+    def __init__(self, comm, k, results, outs):
+        self.both = [BlockGather(comm, res.at[k], out.at[k]) for res, out in zip(results, outs)]
+
+    def __getattr__(self, step):
+        def run():
+            for block in self.both:
+                getattr(block, step)()
+        return run
+
+
+def last_grads(u_hbm, q_hbm, s_hbm, d_hbm, top_in, top_out, x1, part_hbm,
+               x2, top_all_in, top_all_out, low_all_in, low_all_out,
+               gu, gs, gq, gd, part, landing, res_in, res_out, *rest):
     bufs, (send_sems, recv_sems, local_sems) = rest[:6], rest[6:]
     comm = Comm(send_sems, recv_sems)
+    tokens = x1.shape[0]
     x, c = comm.x, comm.c
     loads = start_local([(u_hbm, gu), (q_hbm, gq), (s_hbm, gs), (d_hbm, gd)], local_sems, 0)
-    keep = start_local([(top_in.at[k], all_in.at[1, k, x, c]) for k in range(CHUNKS)]
-                       + [(top_out.at[k], all_out.at[1, k, x, c]) for k in range(CHUNKS)], local_sems, 4)
+    load_part = start_local([(part_hbm, part)], local_sems, 4)
+    keep = start_local([(res.at[k], out.at[k, x, c]) for k in range(TOP_CHUNKS)
+                        for res, out in ((top_in, top_all_in), (top_out, top_all_out))], local_sems, 5)
     comm.barrier('xyz')
     wait_local(loads)
-    grads = grad_reduces(comm, gu, gq, gs, gd, bufs, (res_in, res_out))
-    first, second = grads[:2], grads[2:]
-    for g in first:
-        g.start()
-    for g in second:
-        g.start()
-    top = []
-    for k in range(CHUNKS):
-        top += [BlockGather(comm, top_in.at[k], all_in.at[1, k]), BlockGather(comm, top_out.at[k], all_out.at[1, k])]
-    for b in top:
-        b.start()
-    for g in first:
-        g.middle()
-    for b in top:
-        b.forward()
-    for b in top:
-        b.near()
-    for g in first:
-        g.turn()
-    for g in second:
-        g.middle()
-    for b in top:
-        b.finish()
-    for g in first:
-        g.middle2()
-    for g in second:
-        g.turn()
-    for g in first:
-        g.finish()
-    low = [BlockGather(comm, res.at[k], out.at[0, k]) for k in range(CHUNKS)
-           for res, out in ((res_in, all_in), (res_out, all_out))]
-    for b in low[:2]:
-        b.start()
-    for g in second:
-        g.middle2()
-    for b in low[:2]:
-        b.forward()
-    for g in second:
-        g.finish()
-    for b in low[2:]:
-        b.start()
-    keep += start_local([(res_in.at[k], all_in.at[0, k, x, c]) for k in range(CHUNKS)]
-                        + [(res_out.at[k], all_out.at[0, k, x, c]) for k in range(CHUNKS)], local_sems, 4 + 2 * CHUNKS)
-    for b in low[:2]:
-        b.near()
-    for b in low[2:]:
-        b.forward()
-    for b in low[:2]:
-        b.finish()
-    for b in low[2:]:
-        b.near()
-    for b in low[2:]:
-        b.finish()
-    for b in top + low:
-        b.arrived()
+    g = [GradPair(comm, k, gu, gq, gs, gd, bufs, (res_in, res_out)) for k in range(LOW_CHUNKS)]
+    top = [PairGather(comm, k, (top_in, top_out), (top_all_in, top_all_out)) for k in range(TOP_CHUNKS)]
+    low = [PairGather(comm, k, (res_in, res_out), (low_all_in, low_all_out)) for k in range(LOW_CHUNKS)]
+    g[0].start()
+    wait_local(load_part)
+    block = part_block(part, tokens)
+    ring = RingReduce(comm, 'x', block, landing)
+    ring.start()
+    g[1].start()
+    top[0].start()
+    g[0].middle()
+    ring.middle(add_from(block))
+    top[1].start()
+    g[2].start()
+    g[1].middle()
+    g[0].turn()
+    g[3].start()
+    ring.finish()
+    x2[...] = (x1[...].astype(F32) + reduced(part, ring, tokens)).astype(BF16)
+    top[0].forward()
+    g[0].middle2()
+    g[2].middle()
+    top[0].near()
+    top[1].forward()
+    g[1].turn()
+    g[0].finish()
+    low[0].start()
+    top[0].finish()
+    g[1].middle2()
+    g[3].middle()
+    top[1].near()
+    g[1].finish()
+    low[1].start()
+    low[0].forward()
+    top[1].finish()
+    g[2].turn()
+    low[0].near()
+    g[2].middle2()
+    low[1].forward()
+    low[0].finish()
+    g[3].turn()
+    g[2].finish()
+    low[2].start()
+    g[3].middle2()
+    low[1].near()
+    low[2].forward()
+    low[1].finish()
+    g[3].finish()
+    low[3].start()
+    keep += start_local([(res.at[k], out.at[k, x, c]) for k in range(LOW_CHUNKS)
+                         for res, out in ((res_in, low_all_in), (res_out, low_all_out))], local_sems, 5 + 2 * TOP_CHUNKS)
+    low[2].near()
+    low[3].forward()
+    low[2].finish()
+    low[3].near()
+    low[3].finish()
+    for pair in top + low:
+        pair.arrived()
     wait_local(keep)
     comm.wait_sends()
 
 
-def call_last_grads(u_hbm, q_hbm, s_hbm, d_hbm, top_in, top_out):
+def call_last_grads(u_hbm, q_hbm, s_hbm, d_hbm, top_in, top_out, x1, part_hbm):
     slice_ = s_hbm.shape[2]
-    width = u_hbm.shape[3]
-    shapes = result_shapes(width, slice_)
-    outs = [sds((2, CHUNKS, 4, 2) + shape[1:], F32) for shape in shapes]
+    tokens, width = x1.shape
+    low = result_shapes(width, slice_, LOW_CHUNKS)
+    outs = [sds((shape[0], 4, 2) + shape[1:], F32) for shape in (top_in.shape, top_out.shape) + low]
     return pl.pallas_call(
         last_grads,
         name='last_grads',
-        out_shape=tuple(outs),
-        in_specs=[hbm()] * 4 + [vmem()] * 2,
+        out_shape=(sds((tokens, width), BF16),) + tuple(outs),
+        in_specs=[hbm()] * 4 + [vmem()] * 3 + [hbm()],
+        out_specs=(vmem(),) + (hbm(),) * 4,
+        scratch_shapes=[VMEM(r.shape, BF16) for r in (u_hbm, s_hbm, q_hbm, d_hbm)]
+        + [VMEM(part_hbm.shape, F32), VMEM((6, tokens, width // 2), F32)] + [VMEM(s, F32) for s in low]
+        + grad_scratch(width, slice_, LOW_CHUNKS) + [sems(240), sems(240), sems(5 + 2 * TOP_CHUNKS + 2 * LOW_CHUNKS)],
+        compiler_params=params(4),
+        cost_estimate=pl.CostEstimate(flops=64 * tokens * width * slice_, bytes_accessed=1 << 24, transcendentals=0),
+    )(u_hbm, q_hbm, s_hbm, d_hbm, top_in, top_out, x1, part_hbm)
+
+
+def assemble(top_in, top_out, low_in, low_out, grad_in, grad_out, v_top_in, v_top_out, v_low_in, v_low_out,
+             load_sems, store_sems):
+    loads = []
+    for i, (src, dst) in enumerate(((low_in, v_low_in), (low_out, v_low_out), (top_in, v_top_in), (top_out, v_top_out))):
+        copy = pltpu.make_async_copy(src, dst, load_sems.at[i])
+        copy.start()
+        loads.append(copy)
+    strip = grad_in.shape[2] // 64
+    for i, ref in enumerate((v_low_in, v_low_out, v_top_in, v_top_out)):
+        loads[i].wait()
+        layer = i // 2
+        chunks, rows, width = ref.shape[0], ref.shape[3], ref.shape[4]
+        for k in range(chunks):
+            for x in range(4):
+                for c in range(2):
+                    if i % 2:
+                        dst = grad_out.at[layer, pl.ds(x * rows, rows), pl.ds((c * chunks + k) * width, width)]
+                        pltpu.make_async_copy(ref.at[k, x, c], dst, store_sems.at[1]).start()
+                        continue
+                    for j in range(width // strip):
+                        t = k * (width // strip) + j
+                        y, z = 2 * c + t // 4, t % 4
+                        dst = grad_in.at[layer, :, pl.ds(((4 * z + y) * 4 + x) * strip, strip)]
+                        pltpu.make_async_copy(ref.at[k, x, c, :, pl.ds(j * strip, strip)], dst, store_sems.at[0]).start()
+    pltpu.make_async_copy(grad_in, grad_in, store_sems.at[0]).wait()
+    pltpu.make_async_copy(grad_out, grad_out, store_sems.at[1]).wait()
+
+
+def call_assemble(top_in, top_out, low_in, low_out, in_shape, out_shape):
+    ins = (top_in, top_out, low_in, low_out)
+    return pl.pallas_call(
+        assemble,
+        name='assemble',
+        out_shape=(sds(in_shape, F32), sds(out_shape, F32)),
+        in_specs=[hbm()] * 4,
         out_specs=(hbm(), hbm()),
-        scratch_shapes=[VMEM(r.shape, BF16) for r in (u_hbm, s_hbm, q_hbm, d_hbm)] + [VMEM(s, F32) for s in shapes]
-        + grad_scratch(width, slice_) + [sems(144), sems(144), sems(4 + 4 * CHUNKS)],
-        compiler_params=params(4),
-        cost_estimate=pl.CostEstimate(flops=8 * 8 * width * slice_ * 64, bytes_accessed=1 << 24, transcendentals=0),
-    )(u_hbm, q_hbm, s_hbm, d_hbm, top_in, top_out)
+        scratch_shapes=[VMEM(r.shape, F32) for r in ins] + [sems(4), sems(2)],
+        compiler_params=pltpu.CompilerParams(vmem_limit_bytes=67043328),
+        cost_estimate=pl.CostEstimate(flops=1 << 30, bytes_accessed=1 << 25, transcendentals=0),
+    )(*ins)
 
 
 def solution(mesh):
@@ -907,17 +982,13 @@
 
     def device_step(tokens, cotangent, w_in, w_out):
         x1, u1, u0_all, s0_all, a0, cot_all, w1_top, w2_top = call_forward_first(tokens, cotangent, w_in, w_out)
-        (x2, e1, d0, u1_all, s1_all, q1_half, d1_half, _, _, w1_low, w2_low) = call_top_layer(
+        e1, d0, part_out, u1_all, s1_all, q1_half, d1_half, w1_low, w2_low = call_top_layer(
             x1, u1, cotangent, cot_all, w1_top, w2_top, w_in, w_out)
-        grad, q0_half, d0_half, top_in, top_out = call_bottom_layer(
+        grad, q0_half, d0_half, res_in, res_out = call_bottom_layer(
             tokens, e1, d0, w1_low, w2_low, a0, u1_all, s1_all, q1_half, d1_half)
-        all_in, all_out = call_last_grads(u0_all, q0_half, s0_all, d0_half, top_in, top_out)
-        rows = w_in.shape[1]
-        strip = w_in.shape[2] // 64
-        per = 2 // CHUNKS
-        grad_in = all_in.reshape(2, CHUNKS, 4, 2, rows, per, 4, strip)
-        grad_in = grad_in.transpose(0, 4, 6, 3, 1, 5, 2, 7).reshape(w_in.shape)
-        grad_out = all_out.transpose(0, 2, 4, 3, 1, 5).reshape(w_out.shape)
+        x2, top_in, top_out, low_in, low_out = call_last_grads(
+            u0_all, q0_half, s0_all, d0_half, res_in, res_out, x1, part_out)
+        grad_in, grad_out = call_assemble(top_in, top_out, low_in, low_out, w_in.shape, w_out.shape)
         return x2, grad_in, grad_out, grad
 
     return jax.shard_map(device_step, mesh=mesh, in_specs=(tok_spec, tok_spec, w_spec, w_spec),

time: 527 us -> 482 us (0.915)
  local copies, waits for them, and re-layouts: 61.4 us -> 3.76 us
  Pallas kernels: 458 us -> 468 us
    reshape x3 -> x0, local copies, waits for them, and re-layouts: 32.4 us -> none  [the longest x1 11.9 us: device_step(): grad_out = all_out.transpose(0, 2, 4, 3, 1, 5).reshape(w_out.shape)]
    transpose x2 -> x0, local copies, waits for them, and re-layouts: 27.4 us -> none  [the longest x1 15.4 us: device_step(): grad_out = all_out.transpose(0, 2, 4, 3, 1, 5).reshape(w_out.shape)]
    pallas_call x1 -> x2, Pallas kernels: 125 us -> 138 us  [the longest x1 127 us: call_last_grads(): pl.pallas_call(last_grads, name='last_grads', out_shape=(sds((tokens, wid...]
    pallas_call x1, Pallas kernels: 118 us -> 112 us  [call_top_layer(): pl.pallas_call(top_layer, name='top_layer', out_shape=(sds((tokens, width...]
where the time goes in v2:
time: 482 us; the launch traced here: 473 us
  Pallas kernels  468 us (97%)
    pallas_call x1, Pallas kernels, call_last_grads(): pl.pallas_call(last_grads, name='last_grads', out_shape=(sds((tokens, wid...  127 us
    pallas_call x1, Pallas kernels, call_forward_first(): pl.pallas_call(forward_first, name='forward_first', out_shape=(sds((token...  114 us
    pallas_call x1, Pallas kernels, call_top_layer(): pl.pallas_call(top_layer, name='top_layer', out_shape=(sds((tokens, width...  112 us
    pallas_call x1, Pallas kernels, call_bottom_layer(): pl.pallas_call(bottom_layer, name='bottom_layer', out_shape=(sds((tokens,...  104 us
    pallas_call x1, Pallas kernels, call_assemble(): pl.pallas_call(assemble, name='assemble', out_shape=(sds(in_shape, F32),...  11 us

profile of v2, /device:TPU:1, one launch (start us, length us, event | category | flops | bytes accessed | tf_op | source)
XLA Modules:
  0.0 472.9 jit_solution(3989611624468968005)
XLA Ops:
  0.6 114.3 %forward_first.1 = (bf16[128,2048]{1,0:T(8,128)(2,1)}, bf16[128,2048]{1,0:T(8,128)(2,1)}, bf16[2,4,128,2048]{3,2,1,0:T(8,128)(2,1)}, bf16[2,512,2048]{2,1,0:T(8,...) custom-call(bf16[128,2048]{1,0:T(8,128)(2,1)} %x0.3, ...), custom_call_target="tpu_custom_call" | custom-call | flops 8589934592 | bytes 16777216 | tf_op jit(solution)/shard_map/forward_first/pallas_call | solution.py:485
  115.0 112.0 %top_layer.1 = (f32[128,2048]{1,0:T(8,128)}, bf16[128,2048]{1,0:T(8,128)(2,1)}, f32[512,2048]{1,0:T(8,128)}, bf16[2,4,128,2048]{3,2,1,0:T(8,128)(2,1)}, bf16[2,5...) custom-call(bf16[128,2048]{1,0:T(8,128)(2,1)} %get-tuple-element.34., ...), custom_call_target="tpu_custom_call" | custom-call | flops 17179869184 | bytes 16777216 | tf_op jit(solution)/shard_map/top_layer/pallas_call | solution.py:611
  227.0 104.1 %bottom_layer.1 = (bf16[128,2048]{1,0:T(8,128)(2,1)}, bf16[2,512,1024]{2,1,0:T(8,128)(2,1)}, bf16[2,4,128,1024]{3,2,1,0:T(8,128)(2,1)}, f32[2,128,512]{2,1,0:T(8,128)}, f32[2,128,512]{2,1,0:T(8,128)}) custom-call(bf16[128,2048]{1,0:T(8,128)(2,1)} %x0.3, f32[128,2048]{1,0:T(8,128)} %get-tuple-element.39.e1, bf16[128,2048]{1,0:T(8,128)(2,1)} %get-tuple-element.40.d0, ...), custom_call_target="tpu_custom_call" | custom-call | flops 17179869184 | bytes 16777216 | tf_op jit(solution)/shard_map/bottom_layer/pallas_call | solution.py:779
  331.1 126.6 %last_grads.1 = (bf16[128,2048]{1,0:T(8,128)(2,1)}, f32[2,4,2,128,512]{4,3,2,1,0:T(8,128)}, f32[2,4,2,128,512]{4,3,2,1,0:T(8,128)}, f32[4,4,2,128,256]{4,3,2,1,0:T(8,128)}, f32[4,4,2,128,256]{4,3,2,1,0:T(8,128)}) custom-call(bf16[2,4,128,2048]{3,2,1,0:T(8,128)(2,1)} %get-tuple-element.33.u_hbm, bf16[2,512,1024]{2,1,0:T(8,128)(2,1)} %get-tuple-element.48.q_hbm, ...), custom_call_target="tpu_custom_call" | custom-call | flops 34359738368 | bytes 16777216 | tf_op jit(solution)/shard_map/last_grads/pallas_call | solution.py:923
  457.7 11.0 %assemble.1 = (f32[2,128,8192]{2,1,0:T(8,128)}, f32[2,512,2048]{2,1,0:T(8,128)}) custom-call(f32[2,4,2,128,512]{4,3,2,1,0:T(8,128)} %get-tuple-element.55.top_in, f32[2,4,2,128,512]{4,3,2,1,0:T(8,128)} %get-tuple-element.56.top_out, f32[4,4,2,128,256]{4,3,2,1,0:T(8,128)} %get-tuple-element.57.low_in, f32[4,4,2,128,256]{4,3,2,1,0:T(8,128)} %get-tuple-element.58.low_out), custom_call_target="tpu_custom_call" | custom-call | flops 1073741824 | bytes 33554432 | tf_op jit(solution)/shard_map/assemble/pallas_call | solution.py:967
  468.8 1.9 copy.10
  470.6 1.9 copy.11

commit v3 on v0

v3 whole, which is shorter than its diff:
```python
import functools

import jax
import jax.numpy as jnp
from jax import lax
from jax.experimental import pallas as pl
from jax.experimental.pallas import tpu as pltpu
from jax.sharding import PartitionSpec as P

EPSILON = 1e-6
GELU_SCALE = 0.7978845608028654
GELU_CUBE = 0.044715
BF16 = jnp.bfloat16
F32 = jnp.float32
MESH = pl.DeviceIdType.MESH
HBM = pltpu.HBM
VMEM = pltpu.VMEM
VMEM_BYTES = 67043328
UPPER = (67, 147)
LOWER = (59, 99, 34)


class Comm:
    def __init__(self, send_sems, recv_sems, local_sems):
        l = lax.axis_index('local')
        d = lax.axis_index('data')
        self.l, self.d = l, d
        self.z, self.y, self.x, self.c = l // 4, l % 4, d // 2, d % 2
        self.send_sems, self.recv_sems, self.local_sems = send_sems, recv_sems, local_sems
        self.sends = self.recvs = self.local_count = 0
        self.groups = []
        self.partner = (l, self.x * 2 + 1 - self.c)

    def pos(self, axis):
        return {'x': self.x, 'y': self.y, 'z': self.z}[axis]

    def neighbor(self, axis, delta):
        p = (self.pos(axis) + delta) % 4
        if axis == 'x':
            return (self.l, p * 2 + self.c)
        if axis == 'y':
            return (self.z * 4 + p, self.d)
        return (p * 4 + self.y, self.d)

    def peers(self, axes):
        out = [self.partner] if 'c' in axes else []
        for axis in axes.replace('c', ''):
            out += [self.neighbor(axis, 1), self.neighbor(axis, 3)]
        return out

    def signal(self, sem, axes):
        for device in self.peers(axes):
            pl.semaphore_signal(sem, inc=1, device_id=device, device_id_type=MESH)

    def wait(self, sem, axes):
        pl.semaphore_wait(sem, len(self.peers(axes)))

    def barrier(self, axes):
        sem = pltpu.get_barrier_semaphore()
        self.signal(sem, axes)
        self.wait(sem, axes)

    def send_sem(self):
        self.sends += 1
        return self.send_sems.at[self.sends - 1]

    def recv_sem(self):
        self.recvs += 1
        return self.recv_sems.at[self.recvs - 1]

    def copy(self, src, dst, device, send_sem, recv_sem):
        return pltpu.make_async_remote_copy(src_ref=src, dst_ref=dst, send_sem=send_sem, recv_sem=recv_sem,
                                            device_id=device, device_id_type=MESH)

    def send(self, src, dst, device, group, recv_sem):
        self.copy(src, dst, device, group.sem, recv_sem).start()

    def wait_recv(self, ref, recv_sem):
        self.copy(ref, ref, self.partner, self.send_sems.at[0], recv_sem).wait_recv()

    def push(self, src, dst):
        group, recv_sem = Sends(self, src), self.recv_sem()
        self.send(src, dst, self.partner, group, recv_sem)
        return group, lambda: self.wait_recv(dst, recv_sem)

    def local(self, *pairs):
        out = []
        for src, dst in pairs:
            copy = pltpu.make_async_copy(src, dst, self.local_sems.at[self.local_count])
            copy.start()
            self.local_count += 1
            out.append(copy)
        return out

    def end(self):
        for group in self.groups:
            group.wait()


class Sends:
    def __init__(self, comm, ref, sem=None):
        self.comm, self.ref, self.sem = comm, ref, sem or comm.send_sem()
        self.waited = False
        comm.groups.append(self)

    def wait(self):
        if not self.waited:
            self.waited = True
            c = self.comm
            c.copy(self.ref, self.ref, c.partner, self.sem, c.recv_sems.at[0]).wait_send()


def done(copies):
    for copy in copies:
        copy.wait()


class Every:
    def __init__(self, things):
        self.things = things

    def __getattr__(self, step):
        def run(*args):
            for thing in self.things:
                getattr(thing, step)(*args)
        return run


class RingGather:
    def __init__(self, comm, axis, own, slot, block, three):
        self.comm, self.own, self.slot, self.block = comm, own, slot, block
        self.me = comm.pos(axis)
        self.right, self.far, self.left = [(self.me + k) % 4 for k in (1, 2, 3)]
        self.to_right, self.to_left = comm.neighbor(axis, 1), comm.neighbor(axis, 3)
        self.group = Sends(comm, three)
        self.sems = [comm.recv_sem() for _ in range(3)]

    def both(self, k, right, right_slot, left, left_slot):
        self.comm.send(right, right_slot, self.to_right, self.group, self.sems[k])
        self.comm.send(left, left_slot, self.to_left, self.group, self.sems[k])

    def start(self):
        own, slot, me = self.own, self.slot, self.me
        self.both(0, own(0), slot(me, 0), own(1), slot(me, 1))
        self.both(1, own(1), slot(me, 1), own(0), slot(me, 0))

    def forward(self):
        self.comm.wait_recv(self.block, self.sems[0])
        right, left = self.slot(self.left, 0), self.slot(self.right, 1)
        self.both(2, right, right, left, left)

    def near(self):
        self.comm.wait_recv(self.block, self.sems[1])

    def finish(self):
        self.comm.wait_recv(self.block, self.sems[2])

    def sent(self):
        self.group.wait()


class RingReduce:
    def __init__(self, comm, axis, part, landing, before=None):
        self.comm, self.part, self.landing = comm, part, landing
        self.me = comm.pos(axis)
        self.right, self.far, self.left = [(self.me + k) % 4 for k in (1, 2, 3)]
        self.to_right, self.to_left = comm.neighbor(axis, 1), comm.neighbor(axis, 3)
        self.first = Sends(comm, landing.at[pl.ds(0, 2)], before and before.first.sem)
        self.rest = Sends(comm, landing.at[pl.ds(0, 4)], before and before.rest.sem)
        self.sems = before.sems if before else [comm.recv_sem() for _ in range(3)]

    def right_to(self, k, src, group, sem):
        self.comm.send(src, self.landing.at[k], self.to_right, group, sem)

    def left_to(self, k, src, group, sem):
        self.comm.send(src, self.landing.at[k], self.to_left, group, sem)

    def start(self, far0, far1, right1, left0):
        self.right_to(0, far0, self.first, self.sems[0])
        self.left_to(3, far1, self.first, self.sems[1])
        self.right_to(1, right1, self.rest, self.sems[2])
        self.left_to(4, left0, self.rest, self.sems[2])

    def start_all(self):
        part = self.part
        self.start(part(self.far, 0), part(self.far, 1), part(self.right, 1), part(self.left, 0))

    def start_half(self, half):
        if half == 0:
            self.right_to(0, self.part(self.far, 0), self.first, self.sems[0])
            self.left_to(4, self.part(self.left, 0), self.rest, self.sems[2])
        else:
            self.left_to(3, self.part(self.far, 1), self.first, self.sems[1])
            self.right_to(1, self.part(self.right, 1), self.rest, self.sems[2])

    def wait_right(self):
        self.comm.wait_recv(self.landing.at[0], self.sems[0])

    def wait_left(self):
        self.comm.wait_recv(self.landing.at[3], self.sems[1])

    def pass_right(self):
        self.right_to(2, self.landing.at[0], self.rest, self.sems[2])

    def pass_left(self):
        self.left_to(5, self.landing.at[3], self.rest, self.sems[2])

    def middle_right(self):
        landing = self.landing
        self.wait_right()
        landing[0] = landing[0] + self.part(self.right, 0)[...]
        self.pass_right()

    def middle_left(self):
        landing = self.landing
        self.wait_left()
        landing[3] = landing[3] + self.part(self.left, 1)[...]
        self.pass_left()

    def finish(self):
        self.comm.wait_recv(self.landing.at[pl.ds(0, 4)], self.sems[2])

    def sent(self):
        self.first.wait()
        self.rest.wait()

    def sums(self):
        landing = self.landing
        return (self.part(self.me, 0)[...] + landing[2] + landing[4],
                self.part(self.me, 1)[...] + landing[1] + landing[5])


class PlaneGather:
    def __init__(self, comm, dims, first, full, cols):
        self.comm = comm
        c = comm.c
        lead = dims[0] == first
        second = dims.replace(first, '')
        b = comm.pos(second)
        half_rows = full.shape[3] // 2
        rows = lambda h: pl.ds(h * half_rows, half_rows)
        pair = lambda h: pl.ds(2 * h, 2)
        self.b = b
        every, three, own = slice(None), pl.ds(0, 3), comm.pos(first)
        at = lambda p, q, r: full.at[(p, q, c, r, cols) if lead else (q, p, c, r, cols)]
        slot1 = lambda p, h: at(p, b, rows(h))
        slot2 = lambda p, h: at(pair(h), p, every)
        self.ring1 = RingGather(comm, first, lambda h: slot1(own, h), slot1, at(own, b, every), at(three, b, every))
        self.ring2 = RingGather(comm, second, lambda h: slot2(b, h), slot2, at(every, b, every), at(every, three, every))
        self.line = lambda p: at(every, p, every)
        whole = at(every, every, every)
        self.group, self.sem, self.whole = Sends(comm, whole), comm.recv_sem(), whole

    def push(self, p):
        self.comm.send(self.line(p), self.line(p), self.comm.partner, self.group, self.sem)

    def start1(self):
        self.ring1.start()

    def forward1(self):
        self.ring1.forward()

    def start2(self):
        self.ring1.near()
        self.ring1.finish()
        self.ring2.start()
        self.push(self.b)

    def forward2(self):
        self.ring2.forward()

    def near2(self):
        self.ring2.near()
        self.push(self.ring2.left)
        self.push(self.ring2.right)

    def finish2(self):
        self.ring2.finish()
        self.push(self.ring2.far)

    def arrived(self):
        self.comm.wait_recv(self.whole, self.sem)

    def sent(self):
        self.ring1.sent()
        self.ring2.sent()
        self.group.wait()


def gathers(comm, dims, full, pieces):
    width = full.shape[4] // pieces
    out = [PlaneGather(comm, dims, dims[k % 2], full, pl.ds(k * width, width)) for k in range(pieces)]
    return [Every(out[k:k + 2]) for k in range(0, pieces, 2)]


def own_blocks(comm, w_in, w_out, layer, w1, w2):
    z, y, x, c = comm.z, comm.y, comm.x, comm.c
    width = w_in.shape[2] // 64
    rows1, rows2 = w1.shape[3], w2.shape[3]
    own = w1.at[z, y, c]
    k = comm.local_count
    comm.local_count += 1
    for j in range(16):
        start = (4 * (j % 4) + j // 4) * 4 * width + x * width
        pltpu.make_async_copy(w_in.at[layer, pl.ds(c * rows1, rows1), pl.ds(pl.multiple_of(start, width), width)],
                              own.at[:, pl.ds(j * width, width)], comm.local_sems.at[k]).start()
    start = (x * 2 + c) * rows2
    copies = comm.local((w_out.at[layer, pl.ds(pl.multiple_of(start, rows2), rows2)], w2.at[y, z, c]))
    return [pltpu.make_async_copy(own, own, comm.local_sems.at[k])] + copies


def ring_of_tokens(comm, full):
    n = full.shape[1] // 2
    slot = lambda p, h: full.at[p, pl.ds(h * n, n)]
    return RingGather(comm, 'x', lambda h: slot(comm.x, h), slot, full.at[0], full.at[pl.ds(0, 3)])


def token_sums(comm, part, landing, tokens):
    width = part.shape[1] // 2
    block = lambda pos, half: part.at[pl.ds(pl.multiple_of(pos * tokens, tokens), tokens), pl.ds(half * width, width)]
    return RingReduce(comm, 'x', block, landing)


def norm_rows(x):
    return x * lax.rsqrt(jnp.mean(x * x, axis=-1, keepdims=True) + EPSILON)


def norm_rows_vjp(x, g):
    r = lax.rsqrt(jnp.mean(x * x, axis=-1, keepdims=True) + EPSILON)
    dot = jnp.mean(x * g, axis=-1, keepdims=True)
    return r * g - x * (r * r * r * dot)


def gelu(x):
    t = jnp.tanh(GELU_SCALE * (x + GELU_CUBE * (x * x * x)))
    return x * (0.5 * (1.0 + t))


def gelu_grad(x):
    x2 = x * x
    t = jnp.tanh(GELU_SCALE * (x + GELU_CUBE * (x2 * x)))
    return 0.5 * (1.0 + t) + (0.5 * x) * (1.0 - t * t) * (GELU_SCALE * (1.0 + (3.0 * GELU_CUBE) * x2))


def dot(a, b):
    return lax.dot_general(a, b, (((1,), (0,)), ((), ())), preferred_element_type=F32)


def dot_bt(a, b):
    return lax.dot_general(a, b, (((1,), (1,)), ((), ())), preferred_element_type=F32)


def flat(value):
    return value.reshape(-1, value.shape[-1])


def tiles(n, step, tile=256):
    t = min(tile, n)

    def run(i, _):
        step(pl.ds(pl.multiple_of(i * t, t), t))
        return 0

    lax.fori_loop(0, n // t, run, 0)


def forward_acts(u, w1, a, s, st):
    def step(cols):
        acc = dot(flat(u[...]), flat(w1[:, :, :, :, cols])).astype(BF16)
        a[:, cols] = acc
        value = gelu(acc.astype(F32)).astype(BF16)
        s[:, cols] = value
        st[cols, :] = value.T

    tiles(a.shape[1], step)


def transposed(u, ut):
    def step(cols):
        ut[cols, :] = flat(u[:, :, cols]).T

    tiles(ut.shape[0], step)


def forward_part(s, w2, part, half):
    width = part.shape[1] // 2
    t = min(256, width)

    def run(i, _):
        cols = pl.ds(pl.multiple_of(half * width + i * t, t), t)
        part[:, cols] = dot(s[...], flat(w2[:, :, :, :, cols]))
        return 0

    lax.fori_loop(0, width // t, run, 0)


def row_tile(w, i):
    return flat(w[i // 2, pl.ds((i % 2) * 2, 2)])


def backward_acts(d, tile_product, a, q):
    rows = a.shape[1] // 8

    def step(i, _):
        cols = pl.ds(pl.multiple_of(i * rows, rows), rows)
        q[:, cols] = (tile_product(i) * gelu_grad(a[:, cols].astype(F32))).astype(BF16)
        return 0

    lax.fori_loop(0, 8, step, 0)


def backward_part(tile_product, part, half):
    rows = part.shape[1] // 8

    def step(j, _):
        i = half * 4 + j
        part[:, pl.ds(pl.multiple_of(i * rows, rows), rows)] = tile_product(i)
        return 0

    lax.fori_loop(0, 4, step, 0)


def last_dim_half(ref, k):
    width = ref.shape[-1] // 2
    return ref.at[..., pl.ds(pl.multiple_of(k * width, width), width)]


def upper_half(x0, cot, w_in, w_out,
               x1, e1, d0, part_out, a_low, ut_low, st_low, ut_top, st_top, q_top, d_top, w1_low, w2_low,
               p1, p2, q1, q2, uf, df, a, s, q, ut, st, part, landing,
               send_sems, recv_sems, local_sems, credits):
    comm = Comm(send_sems, recv_sems, local_sems)
    tokens = x0.shape[0]
    x, c = comm.x, comm.c
    p_free, q_free = credits.at[0], credits.at[1]

    own0 = own_blocks(comm, w_in, w_out, 0, p1, p2)
    own1 = own_blocks(comm, w_in, w_out, 1, q1, q2)
    uf[x] = norm_rows(x0[...].astype(F32)).astype(BF16)
    df[x] = cot[...]
    comm.barrier('xyzc')

    gather_u = ring_of_tokens(comm, uf)
    gather_d = ring_of_tokens(comm, df)
    g1, = gathers(comm, 'zy', p1, 2)
    g2, g3 = gathers(comm, 'yz', p2, 4)
    n1, = gathers(comm, 'zy', q1, 2)
    n2, = gathers(comm, 'yz', q2, 2)
    done(own0)
    g1.start1()
    g2.start1()
    gather_u.start()
    g1.forward1()
    g3.start1()
    g2.forward1()
    g1.start2()
    gather_u.forward()
    gather_d.start()
    g1.forward2()
    g3.forward1()
    gather_u.near()
    g2.start2()
    done(own1)
    n1.start1()
    gather_u.finish()
    transposed(uf, ut)
    pushed = [comm.push(ut, ut_low.at[1])]
    kept = comm.local((ut, ut_low.at[0]))
    g1.near2()
    gather_d.forward()
    g1.finish2()
    g1.arrived()
    g2.forward2()
    g3.start2()
    forward_acts(uf, p1, a, s, st)
    g2.near2()
    g2.finish2()
    n1.forward1()
    g3.forward2()
    n2.start1()
    pushed += [comm.push(st, st_low.at[1])]
    kept += comm.local((st, st_low.at[0]), (a, a_low))
    g2.arrived()
    gather_u.sent()
    ring = token_sums(comm, part, landing, tokens)
    forward_part(s, p2, part, 0)
    ring.start_half(0)
    g3.near2()
    n1.start2()
    g3.finish2()
    g3.arrived()
    forward_part(s, p2, part, 1)
    ring.start_half(1)
    n2.forward1()
    gather_d.near()
    gather_d.finish()
    pushed += [comm.push(last_dim_half(df, 1 - c), d_top.at[1])]
    kept_d = comm.local((last_dim_half(df, c), d_top.at[0]))
    g1.sent()
    g2.sent()
    g3.sent()
    comm.signal(p_free, 'yzc')
    own2 = own_blocks(comm, w_in, w_out, 1, p1, p2)
    b1, = gathers(comm, 'zy', p1, 2)
    b2, = gathers(comm, 'yz', p2, 2)
    n1.forward2()
    ring.middle_right()
    n1.near2()
    n2.start2()
    done(own2)
    comm.wait(p_free, 'yzc')
    b2.start1()
    b1.start1()
    ring.middle_left()
    n1.finish2()
    n2.forward2()
    ring.finish()
    x_next = (x0[...].astype(F32) + jnp.concatenate(ring.sums(), axis=1)).astype(BF16)
    x1[...] = x_next
    uf[x] = norm_rows(x_next.astype(F32)).astype(BF16)
    ring.sent()
    gather_v = ring_of_tokens(comm, uf)
    gather_v.start()
    b2.forward1()
    b1.forward1()
    n2.near2()
    n1.arrived()
    b2.start2()
    n2.finish2()
    gather_v.forward()
    n2.arrived()
    done(kept)
    pushed[0][0].wait()
    pushed[1][0].wait()
    b2.forward2()
    gather_v.near()
    b1.start2()
    gather_v.finish()
    forward_acts(uf, q1, a, s, st)
    b2.near2()
    b2.finish2()
    forward_part(s, q2, part, 0)
    forward_part(s, q2, part, 1)
    keep_part = comm.local((part, part_out))
    n1.sent()
    n2.sent()
    comm.signal(q_free, 'yzc')
    own3 = own_blocks(comm, w_in, w_out, 0, q1, q2)
    l1, = gathers(comm, 'zy', q1, 2)
    l2, = gathers(comm, 'yz', q2, 2)
    b2.arrived()
    b1.forward2()
    transposed(uf, ut)
    pushed += [comm.push(ut, ut_top.at[1]), comm.push(st, st_top.at[1])]
    kept = kept_d + comm.local((ut, ut_top.at[0]), (st, st_top.at[0]))
    done(own3)
    comm.wait(q_free, 'yzc')
    l1.start1()
    b1.near2()
    backward_acts(df, lambda i: dot_bt(flat(df[...]), row_tile(p2, i)), a, q)
    b1.finish2()
    l1.forward1()
    l2.start1()
    b1.arrived()
    done(keep_part)
    ring = token_sums(comm, part, landing, tokens)
    product = lambda i: dot_bt(q[...], row_tile(p1, i))
    backward_part(product, part, 0)
    ring.start_half(0)
    l2.forward1()
    l1.start2()
    backward_part(product, part, 1)
    ring.start_half(1)
    pushed += [comm.push(last_dim_half(q, 1 - c), q_top.at[1])]
    kept += comm.local((last_dim_half(q, c), q_top.at[0]))
    l1.forward2()
    l2.start2()
    ring.middle_right()
    l1.near2()
    l1.finish2()
    l2.forward2()
    ring.middle_left()
    l1.arrived()
    kept += comm.local((q1, w1_low))
    l2.near2()
    l2.finish2()
    ring.finish()
    g = jnp.concatenate(ring.sums(), axis=1)
    e = cot[...].astype(F32) + norm_rows_vjp(x1[...].astype(F32), g)
    e1[...] = e
    d0[...] = e.astype(BF16)
    l2.arrived()
    kept += comm.local((q2, w2_low))
    for _, arrived in pushed:
        arrived()
    done(kept)
    comm.end()


def sds(shape, dtype):
    return jax.ShapeDtypeStruct(shape, dtype)


def sems(n):
    return pltpu.SemaphoreType.DMA((n,))


def spaces(kinds):
    return [pl.BlockSpec(memory_space=VMEM if k == 'v' else HBM) for k in kinds]


def call(kernel, ins, in_kinds, outs, out_kinds, scratch, copies, credits, collective_id, flops):
    return pl.pallas_call(
        kernel,
        name=kernel.__name__,
        out_shape=tuple(outs),
        in_specs=spaces(in_kinds),
        out_specs=tuple(spaces(out_kinds)),
        scratch_shapes=scratch + [sems(copies[0][0]), sems(copies[0][1]), sems(copies[1]),
                                  pltpu.SemaphoreType.REGULAR((credits,))],
        compiler_params=pltpu.CompilerParams(collective_id=collective_id, has_side_effects=True,
                                             vmem_limit_bytes=VMEM_BYTES),
        cost_estimate=pl.CostEstimate(flops=flops, bytes_accessed=1 << 24, transcendentals=0),
    )(*ins)


def call_upper_half(x0, cot, w_in, w_out):
    tokens, width = x0.shape
    inner = w_in.shape[2]
    group, slice_ = 4 * tokens, inner // 4
    w1 = (4, 4, 2, width // 32, slice_)
    w2 = (4, 4, 2, inner // 128, width)
    block = sds((tokens, width), BF16)
    acts = (group, slice_)
    ut, st = (width, group), (slice_, group)
    pair = lambda shape: sds((2,) + shape, BF16)
    outs = [block, sds((tokens, width), F32), block, sds((group, width), F32), sds(acts, BF16),
            pair(ut), pair(st), pair(ut), pair(st), pair((group, slice_ // 2)), pair((4, tokens, width // 2)),
            sds(w1, BF16), sds(w2, BF16)]
    tok = (4, tokens, width)
    scratch = [VMEM(shape, BF16) for shape in (w1, w2, w1, w2, tok, tok, acts, acts, acts, ut, st)]
    scratch += [VMEM((group, width), F32), VMEM((6, tokens, width // 2), F32)]
    return call(upper_half, (x0, cot, w_in, w_out), 'vvhh', outs, 'vvv' + 'h' * 10, scratch, (UPPER, 18), 2, 1,
                16 * group * width * slice_)


class GradReduce:
    def __init__(self, comm, axes, operands, column, sends, landing1, landing2, result, credits, before=None):
        self.comm, self.axes, self.operands, self.column = comm, axes, operands, column
        self.sends, self.landing1, self.landing2, self.result = sends, landing1, landing2, result
        self.credits, self.before = credits, before
        self.ring = RingReduce(comm, axes[0], None, landing1, before and before.ring)
        rows = sends.shape[1] // 2
        half = sends.shape[2] // 2
        self.block = lambda pos, h: sends.at[pos // 2, pl.ds(pl.multiple_of((pos % 2) * rows, rows), rows),
                                             pl.ds(h * half, half)]
        self.ring2 = RingReduce(comm, axes[1], self.block, landing2, before and before.ring2)

    def products(self, count, where, store):
        rows, width = self.sends.shape[1:]
        t = min(128, rows)
        per = rows // t

        def step(n, _):
            i, j = n // per, n % per
            pos, half = where(i)
            start = pl.multiple_of((pos * 2 + half) * rows + j * t, t)
            value = None
            for at, b in self.operands:
                term = dot(at[pl.ds(start, t)], b(pl.ds(self.column, width)))
                value = term if value is None else value + term
            store(i, pl.ds(pl.multiple_of(j * t, t), t), value)
            return 0

        lax.fori_loop(0, count * per, step, 0)

    def start(self):
        me, sends = self.ring.me, self.sends
        if self.before:
            self.before.sent()
            self.comm.wait(self.credits.at[0], self.axes[0])

        def where(i):
            return (me + jnp.where(i < 2, 2, 2 * i - 3)) % 4, ((i + 1) // 2) % 2

        def store(i, rows, value):
            sends[i, rows] = value

        self.products(4, where, store)
        self.ring.start(*[sends.at[k] for k in range(4)])

    def middle(self):
        me, landing = self.ring.me, self.landing1
        self.ring.wait_right()
        self.ring.wait_left()

        def store(i, rows, value):
            landing[3 * i, rows] = landing[3 * i, rows] + value

        self.products(2, lambda i: ((me + 1 + 2 * i) % 4, i), store)
        self.ring.pass_right()
        self.ring.pass_left()

    def turn(self):
        me, landing, sends = self.ring.me, self.landing1, self.sends
        self.ring.finish()
        self.ring.first.wait()

        def store(i, rows, value):
            sends[i, rows] = value + landing[2 - i, rows] + landing[4 + i, rows]

        self.products(2, lambda i: (me, i), store)
        if self.before:
            self.comm.wait(self.credits.at[1], self.axes[1])
        self.ring2.start_all()

    def free1(self):
        self.ring.sent()
        self.comm.signal(self.credits.at[0], self.axes[0])

    def middle2(self):
        self.ring2.middle_right()
        self.ring2.middle_left()

    def finish(self):
        self.ring2.finish()
        w = self.sends.shape[2] // 2
        self.result[:, 0:w], self.result[:, w:2 * w] = self.ring2.sums()

    def sent(self):
        self.ring2.sent()

    def free2(self):
        self.sent()
        self.comm.signal(self.credits.at[1], self.axes[1])


CHUNKS = 4


def grad_buffers(width, slice_):
    out = []
    for rows, cols in ((width // 8, slice_ // 2), (slice_ // 8, width // 2)):
        w = cols // CHUNKS
        out += [VMEM((CHUNKS, 4, rows, w), F32), VMEM((CHUNKS, 6, rows, w), F32),
                VMEM((CHUNKS, 6, rows // 2, w // 2), F32)]
    return out


def result_shapes(width, slice_):
    return [(CHUNKS, width // 16, slice_ // 2 // CHUNKS), (CHUNKS, slice_ // 16, width // 2 // CHUNKS)]


def grad_chunks(comm, operands, bufs, results, credits, before=None):
    out = []
    for k in range(CHUNKS):
        both = []
        for i, axes in enumerate(('zy', 'yz')):
            sends, land1, land2 = bufs[3 * i:3 * i + 3]
            both.append(GradReduce(comm, axes, operands[i], k * sends.shape[3], sends.at[k], land1.at[k], land2.at[k],
                                   results[i].at[k], credits.at[2 * k + i],
                                   before[k].things[i] if before else None))
        out.append(Every(both))
    return out


class BlockGather:
    def __init__(self, comm, own, out):
        self.comm, self.own, self.out = comm, own, out
        c = comm.c
        n = own.shape[0] // 2
        half = lambda h: pl.ds(h * n, n)
        self.ring = RingGather(comm, 'x', lambda h: own.at[half(h)], lambda p, h: out.at[p, c, half(h)],
                               own, out.at[pl.ds(0, 3), c])
        self.four = out.at[:, c]
        self.group, self.sem = Sends(comm, self.four), comm.recv_sem()

    def push(self, pos, src):
        c = self.comm
        c.send(src, self.out.at[pos, c.c], c.partner, self.group, self.sem)

    def start(self):
        self.ring.start()
        self.push(self.ring.me, self.own)
        self.kept = self.comm.local((self.own, self.out.at[self.ring.me, self.comm.c]))

    def forward(self):
        self.ring.forward()

    def near(self):
        ring, c = self.ring, self.comm.c
        ring.near()
        self.push(ring.left, self.out.at[ring.left, c])
        self.push(ring.right, self.out.at[ring.right, c])

    def finish(self):
        ring, c = self.ring, self.comm.c
        ring.finish()
        self.push(ring.far, self.out.at[ring.far, c])

    def arrived(self):
        self.comm.wait_recv(self.four, self.sem)
        done(self.kept)


def lower_half(x0, x1, e1, d0, part_hbm, w1_hbm, w2_hbm, a_hbm, ut_low, st_low, ut_top, st_top, q_top, d_top,
               grad, x2, q_low, d_low, top_all_in, top_all_out, low_all_in, low_all_out,
               w, df, a, q, part, landing, gut, gst, gq, gd, top_in, top_out, low_in, low_out, *rest):
    bufs, (send_sems, recv_sems, local_sems, credits, x_free) = rest[:6], rest[6:]
    comm = Comm(send_sems, recv_sems, local_sems)
    tokens = x0.shape[0]
    x, c = comm.x, comm.c
    group = a.shape[0]
    load_d = comm.local((d0, df.at[x]))
    loads = comm.local((ut_top, gut), (q_top, gq), (st_top, gst), (d_top, gd))
    columns = lambda ref, j: ref.at[:, pl.ds(j * group, group)]
    load_w = lambda ref: comm.local(*[(columns(ref, j), w.at[j]) for j in range(4)])
    load2 = load_w(w2_hbm) + comm.local((a_hbm, a))
    comm.barrier('xyzc')

    gather_d = ring_of_tokens(comm, df)
    done(load_d)
    gather_d.start()
    done(loads)
    own_b = lambda ref: lambda cols: flat(ref[..., cols])
    top = [[(gut.at[k], own_b(gq.at[k])) for k in (0, 1)], [(gst.at[k], own_b(gd.at[k])) for k in (0, 1)]]
    upper = grad_chunks(comm, top, bufs, (top_in, top_out), credits)
    t0, t1, t2, t3 = upper

    def by_columns(left):
        rows = w.shape[1] // 8

        def product(i):
            value = None
            for j in range(4):
                term = dot_bt(flat(left[..., j * group:(j + 1) * group]),
                              w[j, pl.ds(pl.multiple_of(i * rows, rows), rows)])
                value = term if value is None else value + term
            return value

        return product

    t0.start()
    t1.start()
    t2.start()
    gather_d.forward()
    t0.middle()
    gather_d.near()
    gather_d.finish()
    done(load2)
    backward_acts(df, by_columns(df), a, q)
    load1 = load_w(w1_hbm)
    _, d_arrived = comm.push(last_dim_half(df, 1 - c), d_low)
    _, q_arrived = comm.push(last_dim_half(q, 1 - c), q_low)
    done(load1)
    ring = token_sums(comm, part, landing, tokens)
    product = by_columns(q)
    backward_part(product, part, 0)
    ring.start_half(0)
    backward_part(product, part, 1)
    ring.start_half(1)
    d_arrived()
    q_arrived()
    half = a.shape[1] // 2
    loads = comm.local(*[(ut_low.at[k], w.at[k]) for k in (0, 1)], *[(st_low.at[k], w.at[2 + k]) for k in (0, 1)],
                       (q_low, a.at[:, pl.ds(0, half)]))
    loads += comm.local(*[(d_low.at[k], a.at[pl.ds(k * tokens, tokens), pl.ds(half, half)]) for k in range(4)])
    t1.middle()
    t3.start()
    t0.turn()
    t2.middle()
    ring.middle_right()
    t1.turn()
    t3.middle()
    ring.middle_left()
    t0.middle2()
    t2.turn()
    ring.finish()
    g = jnp.concatenate(ring.sums(), axis=1)
    grad[...] = (e1[...] + norm_rows_vjp(x0[...].astype(F32), g)).astype(BF16)
    ring.sent()
    comm.signal(x_free, 'x')
    load_part = comm.local((part_hbm, part))
    t1.middle2()
    t0.free1()
    t1.free1()
    comm.wait(x_free, 'x')
    done(load_part)
    ring = token_sums(comm, part, landing, tokens)
    ring.start_all()
    t3.turn()
    t0.finish()
    t0.free2()
    t2.middle2()
    done(loads)
    mine = lambda ref: lambda cols: flat(ref[..., pl.ds(pl.multiple_of(c * half + cols.start, cols.size), cols.size)])
    other = lambda first: lambda cols: a[:, pl.ds(first + cols.start, cols.size)]
    low = [[(w.at[0], mine(q)), (w.at[1], other(0))], [(w.at[2], mine(df)), (w.at[3], other(half))]]
    g0, g1, g2, g3 = grad_chunks(comm, low, bufs, (low_in, low_out), credits, upper)
    g0.start()
    t1.finish()
    t1.free2()
    t2.free1()
    t3.middle2()
    t2.finish()
    t2.free2()
    t3.free1()
    ring.middle_right()
    ring.middle_left()
    g0.middle()
    g1.start()
    t3.finish()
    t3.free2()
    top = Every([BlockGather(comm, top_in, top_all_in), BlockGather(comm, top_out, top_all_out)])
    low = [Every([BlockGather(comm, low_in.at[k], low_all_in.at[k]), BlockGather(comm, low_out.at[k], low_all_out.at[k])])
           for k in range(CHUNKS)]
    low0, low1, low2, low3 = low
    top.start()
    g0.turn()
    g1.middle()
    ring.finish()
    x2[...] = (x1[...].astype(F32) + jnp.concatenate(ring.sums(), axis=1)).astype(BF16)
    g0.middle2()
    g2.start()
    g1.turn()
    g0.finish()
    top.forward()
    low0.start()
    g2.middle()
    top.near()
    g1.middle2()
    g3.start()
    g2.turn()
    g1.finish()
    low1.start()
    top.finish()
    low0.forward()
    low0.near()
    g3.middle()
    low1.forward()
    low1.near()
    low0.finish()
    g2.middle2()
    low1.finish()
    g3.turn()
    g2.finish()
    low2.start()
    g3.middle2()
    low2.forward()
    g3.finish()
    low3.start()
    low2.near()
    low2.finish()
    low3.forward()
    low3.near()
    low3.finish()
    for pair in [top] + low:
        pair.arrived()
    comm.end()


def call_lower_half(x0, x1, e1, d0, part_hbm, w1_hbm, w2_hbm, a_hbm, ut_low, st_low, ut_top, st_top, q_top, d_top):
    tokens, width = x0.shape
    group, slice_ = a_hbm.shape
    shapes = result_shapes(width, slice_)
    tops = [(4, 2) + shape for shape in shapes]
    lows = [(CHUNKS, 4, 2) + shape[1:] for shape in shapes]
    block = sds((tokens, width), BF16)
    outs = [block, block, sds(q_top.shape[1:], BF16), sds(d_top.shape[1:], BF16)] + [sds(s, F32) for s in tops + lows]
    acts = VMEM((group, slice_), BF16)
    scratch = [VMEM((4, width, group), BF16), VMEM((4, tokens, width), BF16), acts, acts, VMEM((group, width), F32),
               VMEM((6, tokens, width // 2), F32)]
    scratch += [VMEM(r.shape, BF16) for r in (ut_top, st_top, q_top, d_top)] + [VMEM(s, F32) for s in shapes + shapes]
    scratch += grad_buffers(width, slice_)
    ins = (x0, x1, e1, d0, part_hbm, w1_hbm.reshape(width, slice_), w2_hbm.reshape(slice_, width), a_hbm,
           ut_low, st_low, ut_top, st_top, q_top, d_top)
    return pl.pallas_call(
        lower_half,
        name='lower_half',
        out_shape=tuple(outs),
        in_specs=spaces('vvv' + 'h' * 11),
        out_specs=tuple(spaces('vv' + 'h' * 6)),
        scratch_shapes=scratch + [sems(LOWER[0]), sems(LOWER[1]), sems(LOWER[2]), pltpu.SemaphoreType.REGULAR((2 * CHUNKS, 2)),
                                  pltpu.SemaphoreType.REGULAR],
        compiler_params=pltpu.CompilerParams(collective_id=2, has_side_effects=True, vmem_limit_bytes=VMEM_BYTES),
        cost_estimate=pl.CostEstimate(flops=16 * group * width * slice_, bytes_accessed=1 << 24, transcendentals=0),
    )(*ins)


def assemble(top_in, top_out, low_in, low_out, grad_in, grad_out, v_top_in, v_top_out, v_low_in, v_low_out,
             load_sems, store_sems):
    loads = []
    refs = (v_low_in, v_low_out, v_top_in, v_top_out)
    for i, src in enumerate((low_in, low_out, top_in, top_out)):
        copy = pltpu.make_async_copy(src, refs[i], load_sems.at[i])
        copy.start()
        loads.append(copy)
    strip = grad_in.shape[2] // 64
    rows, width = low_in.shape[3:]
    width_out = low_out.shape[4]
    per = width // strip
    for i, ref in enumerate(refs):
        loads[i].wait()
        layer = i // 2
        for k in range(CHUNKS):
            for x in range(4):
                for c in range(2):
                    src = ref.at[x, c, k] if layer else ref.at[k, x, c]
                    if i % 2:
                        dst = grad_out.at[layer, pl.ds(x * src.shape[0], src.shape[0]),
                                          pl.ds((c * CHUNKS + k) * width_out, width_out)]
                        pltpu.make_async_copy(src, dst, store_sems.at[1]).start()
                        continue
                    for j in range(per):
                        y, z = (c * 8 + k * per + j) // 4, (k * per + j) % 4
                        dst = grad_in.at[layer, :, pl.ds(((4 * z + y) * 4 + x) * strip, strip)]
                        pltpu.make_async_copy(src.at[:, pl.ds(j * strip, strip)], dst, store_sems.at[0]).start()
    pltpu.make_async_copy(grad_in, grad_in, store_sems.at[0]).wait()
    pltpu.make_async_copy(grad_out, grad_out, store_sems.at[1]).wait()


def call_assemble(ins, in_shape, out_shape):
    return pl.pallas_call(
        assemble,
        name='assemble',
        out_shape=(sds(in_shape, F32), sds(out_shape, F32)),
        in_specs=spaces('hhhh'),
        out_specs=tuple(spaces('hh')),
        scratch_shapes=[VMEM(r.shape, F32) for r in ins] + [sems(4), sems(2)],
        compiler_params=pltpu.CompilerParams(vmem_limit_bytes=VMEM_BYTES),
        cost_estimate=pl.CostEstimate(flops=1 << 30, bytes_accessed=1 << 25, transcendentals=0),
    )(*ins)


def solution(mesh):
    tok_spec = P(('local', 'data'), None)
    w_spec = P(None, 'local', None)

    def device_step(tokens, cotangent, w_in, w_out):
        (x1, e1, d0, part_out, a_low, ut_low, st_low, ut_top, st_top, q_top, d_top, w1_low, w2_low) = call_upper_half(
            tokens, cotangent, w_in, w_out)
        grad, x2, _, _, *gathered = call_lower_half(
            tokens, x1, e1, d0, part_out, w1_low, w2_low, a_low, ut_low, st_low, ut_top, st_top, q_top, d_top)
        grad_in, grad_out = call_assemble(gathered, w_in.shape, w_out.shape)
        return x2, grad_in, grad_out, grad

    return jax.shard_map(device_step, mesh=mesh, in_specs=(tok_spec, tok_spec, w_spec, w_spec),
                         out_specs=(tok_spec, w_spec, w_spec, tok_spec), check_vma=False)
```

time: 2550 us -> 411 us (0.16)
  waiting for transfers between devices: 2260 us -> 0 us
  Pallas kernels: 0 us -> 407 us
  matrix products: 238 us -> 0 us
    reduce_scatter x4 -> x0, waiting for transfers between devices: 1370 us -> none  [reduce_grad(): lax.psum_scatter(grad_full, 'local', scatter_dimension=0, tiled=True)]
    all_gather x4 -> x0, waiting for transfers between devices: 741 us -> none  [the longest x2 378 us: device_step(): w_first = lax.all_gather(w_in[layer_idx], 'local', axis=0, tiled=True)]
    pallas_call x0 -> x3, Pallas kernels: none -> 407 us  [the longest x1 202 us: call_lower_half(): pl.pallas_call(lower_half, name='lower_half', out_shape=tuple(outs), in_s...]
    dot_general x12 -> x0, matrix products: 238 us -> none  [the longest x2 49.8 us: layer_backward(): lax.dot_general(hidden, grad_b, (((0,), (0,)), ((), ())), preferred_eleme...]
    psum x1 -> x0, waiting for transfers between devices: 148 us -> none  [reduce_grad(): return lax.psum(grad_part, 'data')]
  transfers between devices with their start and end apart: 9 -> 0, of which waited for: 9 -> 0; matrix products, arithmetic and copies ran while one was open for 7% -> 0% of each run, Pallas kernels for 0% -> 0%
where the time goes in v3:
time: 411 us
  Pallas kernels  407 us (99%)
    pallas_call x1, Pallas kernels, call_lower_half(): pl.pallas_call(lower_half, name='lower_half', out_shape=tuple(outs), in_s...  202 us
    pallas_call x1, Pallas kernels, call(): pl.pallas_call(kernel, name=kernel.__name__, out_shape=tuple(outs), in_sp...  193 us
    pallas_call x1, Pallas kernels, call_assemble(): pl.pallas_call(assemble, name='assemble', out_shape=(sds(in_shape, F32),...  11 us

profile of v3, /device:TPU:1, one launch (start us, length us, event | category | flops | bytes accessed | tf_op | source)
XLA Modules:
  0.0 411.1 jit_solution(12939625964670970275)
XLA Ops:
  0.6 193.3 %upper_half.1 = (bf16[128,2048]{1,0:T(8,128)(2,1)}, f32[128,2048]{1,0:T(8,128)}, bf16[128,2048]{1,0:T(8,128)(2,1)}, f32[512,2048]{1,0:T(8,128)}, bf16[512,2048]{...) custom-call(bf16[128,2048]{1,0:T(8,128)(2,1)} %x0.3, ...), custom_call_target="tpu_custom_call" | custom-call | flops 34359738368 | bytes 16777216 | tf_op jit(solution)/shard_map/upper_half/pallas_call | solution.py:613
  194.0 202.3 %lower_half.1 = (bf16[128,2048]{1,0:T(8,128)(2,1)}, bf16[128,2048]{1,0:T(8,128)(2,1)}, bf16[512,1024]{1,0:T(8,128)(2,1)}, bf16[4,128,1024]{2,1,0:T(8,128)(2,1)},...) custom-call(bf16[128,2048]{1,0:T(8,128)(2,1)} %x0.3, ...), custom_call_target="tpu_custom_call" | custom-call | flops 34359738368 | bytes 16777216 | tf_op jit(solution)/shard_map/lower_half/pallas_call | solution.py:977
  396.3 11.0 %assemble.1 = (f32[2,128,8192]{2,1,0:T(8,128)}, f32[2,512,2048]{2,1,0:T(8,128)}) custom-call(f32[4,2,4,128,256]{4,3,2,1,0:T(8,128)} %get-tuple-element.39.top_in, f32[4,2,4,128,256]{4,3,2,1,0:T(8,128)} %get-tuple-element.40.top_out, f32[4,4,2,128,256]{4,3,2,1,0:T(8,128)} %get-tuple-element.41.low_in, f32[4,4,2,128,256]{4,3,2,1,0:T(8,128)} %get-tuple-element.42.low_out), custom_call_target="tpu_custom_call" | custom-call | flops 1073741824 | bytes 33554432 | tf_op jit(solution)/shard_map/assemble/pallas_call | solution.py:1023
  407.3 1.9 copy.10
  409.2 1.9 copy.11

commit v4 on v3

--- a/solution.py
+++ b/solution.py
@@ -16,8 +16,8 @@
 HBM = pltpu.HBM
 VMEM = pltpu.VMEM
 VMEM_BYTES = 67043328
-UPPER = (67, 147)
-LOWER = (59, 99, 34)
+UPPER = (40, 95)
+LOWER = (69, 116, 41)
 
 
 class Comm:
@@ -55,10 +55,11 @@
     def wait(self, sem, axes):
         pl.semaphore_wait(sem, len(self.peers(axes)))
 
-    def barrier(self, axes):
-        sem = pltpu.get_barrier_semaphore()
-        self.signal(sem, axes)
-        self.wait(sem, axes)
+    def arrive(self, axes):
+        self.signal(pltpu.get_barrier_semaphore(), axes)
+
+    def meet(self, axes):
+        self.wait(pltpu.get_barrier_semaphore(), axes)
 
     def send_sem(self):
         self.sends += 1
@@ -127,13 +128,13 @@
 
 
 class RingGather:
-    def __init__(self, comm, axis, own, slot, block, three):
+    def __init__(self, comm, axis, own, slot, block, three, before=None):
         self.comm, self.own, self.slot, self.block = comm, own, slot, block
         self.me = comm.pos(axis)
         self.right, self.far, self.left = [(self.me + k) % 4 for k in (1, 2, 3)]
         self.to_right, self.to_left = comm.neighbor(axis, 1), comm.neighbor(axis, 3)
-        self.group = Sends(comm, three)
-        self.sems = [comm.recv_sem() for _ in range(3)]
+        self.group = Sends(comm, three, before and before.group.sem)
+        self.sems = before.sems if before else [comm.recv_sem() for _ in range(3)]
 
     def both(self, k, right, right_slot, left, left_slot):
         self.comm.send(right, right_slot, self.to_right, self.group, self.sems[k])
@@ -231,7 +232,7 @@
 
 
 class PlaneGather:
-    def __init__(self, comm, dims, first, full, cols):
+    def __init__(self, comm, dims, first, full, cols, before=None):
         self.comm = comm
         c = comm.c
         lead = dims[0] == first
@@ -245,14 +246,19 @@
         at = lambda p, q, r: full.at[(p, q, c, r, cols) if lead else (q, p, c, r, cols)]
         slot1 = lambda p, h: at(p, b, rows(h))
         slot2 = lambda p, h: at(pair(h), p, every)
-        self.ring1 = RingGather(comm, first, lambda h: slot1(own, h), slot1, at(own, b, every), at(three, b, every))
-        self.ring2 = RingGather(comm, second, lambda h: slot2(b, h), slot2, at(every, b, every), at(every, three, every))
+        self.ring1 = RingGather(comm, first, lambda h: slot1(own, h), slot1, at(own, b, every), at(three, b, every),
+                                before and before.ring1)
+        self.ring2 = RingGather(comm, second, lambda h: slot2(b, h), slot2, at(every, b, every), at(every, three, every),
+                                before and before.ring2)
         self.line = lambda p: at(every, p, every)
-        whole = at(every, every, every)
-        self.group, self.sem, self.whole = Sends(comm, whole), comm.recv_sem(), whole
-
-    def push(self, p):
-        self.comm.send(self.line(p), self.line(p), self.comm.partner, self.group, self.sem)
+        self.both_cores = lambda p, ref: ref.at[(every, p, every, every, cols) if lead else (p, every, every, every, cols)]
+        self.whole, self.near_lines = at(every, every, every), at(every, three, every)
+        self.group = Sends(comm, self.whole, before and before.group.sem)
+        self.sems = before.sems if before else [comm.recv_sem(), comm.recv_sem()]
+        self.full = full
+
+    def push(self, p, k=0):
+        self.comm.send(self.line(p), self.line(p), self.comm.partner, self.group, self.sems[k])
 
     def start1(self):
         self.ring1.start()
@@ -276,10 +282,29 @@
 
     def finish2(self):
         self.ring2.finish()
-        self.push(self.ring2.far)
+        self.push(self.ring2.far, 1)
+
+    def arrived_near(self):
+        self.comm.wait_recv(self.near_lines, self.sems[0])
+
+    def arrived_far(self):
+        self.comm.wait_recv(self.line(self.b), self.sems[1])
 
     def arrived(self):
-        self.comm.wait_recv(self.whole, self.sem)
+        self.arrived_near()
+        self.arrived_far()
+
+    def copy_out(self, out, positions, kept):
+        both = self.both_cores
+        kept += self.comm.local(*[(both(p, self.full), both(p, out)) for p in positions])
+
+    def near_out(self, out, kept):
+        self.arrived_near()
+        self.copy_out(out, (self.b, self.ring2.left, self.ring2.right), kept)
+
+    def far_out(self, out, kept):
+        self.arrived_far()
+        self.copy_out(out, (self.ring2.far,), kept)
 
     def sent(self):
         self.ring1.sent()
@@ -287,9 +312,10 @@
         self.group.wait()
 
 
-def gathers(comm, dims, full, pieces):
+def gathers(comm, dims, full, pieces, before=None):
     width = full.shape[4] // pieces
-    out = [PlaneGather(comm, dims, dims[k % 2], full, pl.ds(k * width, width)) for k in range(pieces)]
+    out = [PlaneGather(comm, dims, dims[k % 2], full, pl.ds(k * width, width), before and before.things[k])
+           for k in range(pieces)]
     return [Every(out[k:k + 2]) for k in range(0, pieces, 2)]
 
 
@@ -309,16 +335,16 @@
     return [pltpu.make_async_copy(own, own, comm.local_sems.at[k])] + copies
 
 
-def ring_of_tokens(comm, full):
+def ring_of_tokens(comm, full, before=None):
     n = full.shape[1] // 2
     slot = lambda p, h: full.at[p, pl.ds(h * n, n)]
-    return RingGather(comm, 'x', lambda h: slot(comm.x, h), slot, full.at[0], full.at[pl.ds(0, 3)])
-
-
-def token_sums(comm, part, landing, tokens):
+    return RingGather(comm, 'x', lambda h: slot(comm.x, h), slot, full.at[0], full.at[pl.ds(0, 3)], before)
+
+
+def token_sums(comm, part, landing, tokens, before=None):
     width = part.shape[1] // 2
     block = lambda pos, half: part.at[pl.ds(pl.multiple_of(pos * tokens, tokens), tokens), pl.ds(half * width, width)]
-    return RingReduce(comm, 'x', block, landing)
+    return RingReduce(comm, 'x', block, landing, before)
 
 
 def norm_rows(x):
@@ -426,8 +452,8 @@
 
 
 def upper_half(x0, cot, w_in, w_out,
-               x1, e1, d0, part_out, a_low, ut_low, st_low, ut_top, st_top, q_top, d_top, w1_low, w2_low,
-               p1, p2, q1, q2, uf, df, a, s, q, ut, st, part, landing,
+               x1_out, e1_out, d0_out, part_out, a_low, ut_low, st_low, ut_top, st_top, q_top, d_top, w1_low, w2_low,
+               p1, p2, q1, q2, uf, df, a, s, q, ut, st, x1, d0, part, landing, e1,
                send_sems, recv_sems, local_sems, credits):
     comm = Comm(send_sems, recv_sems, local_sems)
     tokens = x0.shape[0]
@@ -436,9 +462,10 @@
 
     own0 = own_blocks(comm, w_in, w_out, 0, p1, p2)
     own1 = own_blocks(comm, w_in, w_out, 1, q1, q2)
+    comm.arrive('xyzc')
     uf[x] = norm_rows(x0[...].astype(F32)).astype(BF16)
     df[x] = cot[...]
-    comm.barrier('xyzc')
+    comm.meet('xyzc')
 
     gather_u = ring_of_tokens(comm, uf)
     gather_d = ring_of_tokens(comm, df)
@@ -447,112 +474,110 @@
     n1, = gathers(comm, 'zy', q1, 2)
     n2, = gathers(comm, 'yz', q2, 2)
     done(own0)
-    g1.start1()
     g2.start1()
     gather_u.start()
+    gather_d.start()
+    done(own1)
+    g1.start1()
+    g2.forward1()
+    g3.start1()
     g1.forward1()
-    g3.start1()
-    g2.forward1()
+    g2.start2()
+    gather_u.forward()
+    g3.forward1()
     g1.start2()
-    gather_u.forward()
-    gather_d.start()
+    gather_u.near()
+    gather_d.forward()
     g1.forward2()
-    g3.forward1()
-    gather_u.near()
-    g2.start2()
-    done(own1)
+    g2.forward2()
     n1.start1()
+    g3.start2()
+    n2.start1()
+    g2.near2()
+    gather_d.near()
+    g1.near2()
+    g1.finish2()
     gather_u.finish()
     transposed(uf, ut)
     pushed = [comm.push(ut, ut_low.at[1])]
     kept = comm.local((ut, ut_low.at[0]))
-    g1.near2()
-    gather_d.forward()
-    g1.finish2()
+    gather_d.finish()
+    g2.finish2()
     g1.arrived()
-    g2.forward2()
-    g3.start2()
     forward_acts(uf, p1, a, s, st)
-    g2.near2()
-    g2.finish2()
+    g2.arrived()
     n1.forward1()
     g3.forward2()
-    n2.start1()
-    pushed += [comm.push(st, st_low.at[1])]
-    kept += comm.local((st, st_low.at[0]), (a, a_low))
-    g2.arrived()
     gather_u.sent()
     ring = token_sums(comm, part, landing, tokens)
     forward_part(s, p2, part, 0)
     ring.start_half(0)
     g3.near2()
+    pushed += [comm.push(st, st_low.at[1])]
+    kept += comm.local((st, st_low.at[0]), (a, a_low))
+    pushed += [comm.push(last_dim_half(df, 1 - c), d_top.at[1])]
+    kept_d = comm.local((last_dim_half(df, c), d_top.at[0]))
+    n2.forward1()
     n1.start2()
     g3.finish2()
     g3.arrived()
     forward_part(s, p2, part, 1)
     ring.start_half(1)
-    n2.forward1()
-    gather_d.near()
-    gather_d.finish()
-    pushed += [comm.push(last_dim_half(df, 1 - c), d_top.at[1])]
-    kept_d = comm.local((last_dim_half(df, c), d_top.at[0]))
     g1.sent()
     g2.sent()
     g3.sent()
     comm.signal(p_free, 'yzc')
     own2 = own_blocks(comm, w_in, w_out, 1, p1, p2)
-    b1, = gathers(comm, 'zy', p1, 2)
-    b2, = gathers(comm, 'yz', p2, 2)
-    n1.forward2()
-    ring.middle_right()
-    n1.near2()
-    n2.start2()
+    b1, = gathers(comm, 'zy', p1, 2, g1)
+    b2, = gathers(comm, 'yz', p2, 2, g2)
     done(own2)
     comm.wait(p_free, 'yzc')
     b2.start1()
+    n1.forward2()
+    n2.start2()
     b1.start1()
+    ring.middle_right()
+    n1.near2()
     ring.middle_left()
     n1.finish2()
+    b2.forward1()
     n2.forward2()
+    n1.arrived()
+    n2.near2()
+    b1.forward1()
     ring.finish()
     x_next = (x0[...].astype(F32) + jnp.concatenate(ring.sums(), axis=1)).astype(BF16)
     x1[...] = x_next
+    keep_x = comm.local((x1, x1_out))
     uf[x] = norm_rows(x_next.astype(F32)).astype(BF16)
     ring.sent()
-    gather_v = ring_of_tokens(comm, uf)
+    gather_v = ring_of_tokens(comm, uf, gather_u)
     gather_v.start()
-    b2.forward1()
-    b1.forward1()
-    n2.near2()
-    n1.arrived()
+    done(kept)
+    pushed[0][0].wait()
+    pushed[1][0].wait()
     b2.start2()
     n2.finish2()
     gather_v.forward()
-    n2.arrived()
-    done(kept)
-    pushed[0][0].wait()
-    pushed[1][0].wait()
     b2.forward2()
     gather_v.near()
     b1.start2()
+    n2.arrived()
+    b2.near2()
     gather_v.finish()
     forward_acts(uf, q1, a, s, st)
-    b2.near2()
     b2.finish2()
     forward_part(s, q2, part, 0)
     forward_part(s, q2, part, 1)
     keep_part = comm.local((part, part_out))
+    b1.forward2()
     n1.sent()
     n2.sent()
     comm.signal(q_free, 'yzc')
     own3 = own_blocks(comm, w_in, w_out, 0, q1, q2)
-    l1, = gathers(comm, 'zy', q1, 2)
-    l2, = gathers(comm, 'yz', q2, 2)
+    l1, = gathers(comm, 'zy', q1, 2, n1)
+    l2, = gathers(comm, 'yz', q2, 2, n2)
     b2.arrived()
-    b1.forward2()
-    transposed(uf, ut)
-    pushed += [comm.push(ut, ut_top.at[1]), comm.push(st, st_top.at[1])]
-    kept = kept_d + comm.local((ut, ut_top.at[0]), (st, st_top.at[0]))
     done(own3)
     comm.wait(q_free, 'yzc')
     l1.start1()
@@ -560,10 +585,13 @@
     backward_acts(df, lambda i: dot_bt(flat(df[...]), row_tile(p2, i)), a, q)
     b1.finish2()
     l1.forward1()
+    transposed(uf, ut)
+    pushed += [comm.push(ut, ut_top.at[1]), comm.push(st, st_top.at[1])]
+    kept = kept_d + comm.local((ut, ut_top.at[0]), (st, st_top.at[0]))
     l2.start1()
     b1.arrived()
     done(keep_part)
-    ring = token_sums(comm, part, landing, tokens)
+    ring = token_sums(comm, part, landing, tokens, ring)
     product = lambda i: dot_bt(q[...], row_tile(p1, i))
     backward_part(product, part, 0)
     ring.start_half(0)
@@ -573,24 +601,25 @@
     ring.start_half(1)
     pushed += [comm.push(last_dim_half(q, 1 - c), q_top.at[1])]
     kept += comm.local((last_dim_half(q, c), q_top.at[0]))
+    l2.start2()
     l1.forward2()
-    l2.start2()
+    l1.near2()
     ring.middle_right()
-    l1.near2()
-    l1.finish2()
+    l1.near_out(w1_low, kept)
     l2.forward2()
     ring.middle_left()
-    l1.arrived()
-    kept += comm.local((q1, w1_low))
     l2.near2()
+    l1.finish2()
+    l2.near_out(w2_low, kept)
+    l1.far_out(w1_low, kept)
     l2.finish2()
     ring.finish()
     g = jnp.concatenate(ring.sums(), axis=1)
     e = cot[...].astype(F32) + norm_rows_vjp(x1[...].astype(F32), g)
     e1[...] = e
     d0[...] = e.astype(BF16)
-    l2.arrived()
-    kept += comm.local((q2, w2_low))
+    kept += keep_x + comm.local((e1, e1_out), (d0, d0_out))
+    l2.far_out(w2_low, kept)
     for _, arrived in pushed:
         arrived()
     done(kept)
@@ -638,9 +667,10 @@
             pair(ut), pair(st), pair(ut), pair(st), pair((group, slice_ // 2)), pair((4, tokens, width // 2)),
             sds(w1, BF16), sds(w2, BF16)]
     tok = (4, tokens, width)
-    scratch = [VMEM(shape, BF16) for shape in (w1, w2, w1, w2, tok, tok, acts, acts, acts, ut, st)]
-    scratch += [VMEM((group, width), F32), VMEM((6, tokens, width // 2), F32)]
-    return call(upper_half, (x0, cot, w_in, w_out), 'vvhh', outs, 'vvv' + 'h' * 10, scratch, (UPPER, 18), 2, 1,
+    scratch = [VMEM(shape, BF16) for shape in (w1, w2, w1, w2, tok, tok, acts, acts, acts, ut, st, block.shape,
+                                            block.shape)]
+    scratch += [VMEM((group, width), F32), VMEM((6, tokens, width // 2), F32), VMEM(block.shape, F32)]
+    return call(upper_half, (x0, cot, w_in, w_out), 'vvhh', outs, 'h' * 13, scratch, (UPPER, 35), 2, 1,
                 16 * group * width * slice_)
 
 
@@ -650,10 +680,8 @@
         self.sends, self.landing1, self.landing2, self.result = sends, landing1, landing2, result
         self.credits, self.before = credits, before
         self.ring = RingReduce(comm, axes[0], None, landing1, before and before.ring)
-        rows = sends.shape[1] // 2
-        half = sends.shape[2] // 2
-        self.block = lambda pos, h: sends.at[pos // 2, pl.ds(pl.multiple_of((pos % 2) * rows, rows), rows),
-                                             pl.ds(h * half, half)]
+        rows = sends.shape[1] // 4
+        self.block = lambda pos, h: sends.at[pos // 2, pl.ds(pl.multiple_of(((pos % 2) * 2 + h) * rows, rows), rows)]
         self.ring2 = RingReduce(comm, axes[1], self.block, landing2, before and before.ring2)
 
     def products(self, count, where, store):
@@ -724,8 +752,8 @@
 
     def finish(self):
         self.ring2.finish()
-        w = self.sends.shape[2] // 2
-        self.result[:, 0:w], self.result[:, w:2 * w] = self.ring2.sums()
+        n = self.result.shape[0] // 2
+        self.result[0:n], self.result[n:2 * n] = self.ring2.sums()
 
     def sent(self):
         self.ring2.sent()
@@ -743,7 +771,7 @@
     for rows, cols in ((width // 8, slice_ // 2), (slice_ // 8, width // 2)):
         w = cols // CHUNKS
         out += [VMEM((CHUNKS, 4, rows, w), F32), VMEM((CHUNKS, 6, rows, w), F32),
-                VMEM((CHUNKS, 6, rows // 2, w // 2), F32)]
+                VMEM((CHUNKS, 6, rows // 4, w), F32)]
     return out
 
 
@@ -754,13 +782,17 @@
 def grad_chunks(comm, operands, bufs, results, credits, before=None):
     out = []
     for k in range(CHUNKS):
-        both = []
-        for i, axes in enumerate(('zy', 'yz')):
-            sends, land1, land2 = bufs[3 * i:3 * i + 3]
-            both.append(GradReduce(comm, axes, operands[i], k * sends.shape[3], sends.at[k], land1.at[k], land2.at[k],
-                                   results[i].at[k], credits.at[2 * k + i],
-                                   before[k].things[i] if before else None))
-        out.append(Every(both))
+        pieces = 2 if before and k == CHUNKS - 1 else 1
+        for piece in range(pieces):
+            both = []
+            for i, axes in enumerate(('zy', 'yz')):
+                width = bufs[3 * i].shape[3] // pieces
+                cols = pl.ds(piece * width, width)
+                sends, land1, land2 = [ref.at[k, :, :, cols] for ref in bufs[3 * i:3 * i + 3]]
+                both.append(GradReduce(comm, axes, operands[i], (k * pieces + piece) * width, sends, land1, land2,
+                                       results[i].at[k, :, cols], credits.at[2 * k + i],
+                                       before[k].things[i] if before and piece == 0 else None))
+            out.append(Every(both))
     return out
 
 
@@ -803,25 +835,28 @@
         done(self.kept)
 
 
-def lower_half(x0, x1, e1, d0, part_hbm, w1_hbm, w2_hbm, a_hbm, ut_low, st_low, ut_top, st_top, q_top, d_top,
-               grad, x2, q_low, d_low, top_all_in, top_all_out, low_all_in, low_all_out,
-               w, df, a, q, part, landing, gut, gst, gq, gd, top_in, top_out, low_in, low_out, *rest):
+def lower_half(x0_hbm, x1_hbm, e1_hbm, d0, part_hbm, w1_hbm, w2_hbm, a_hbm, ut_low, st_low, ut_top, st_top, q_top, d_top,
+               grad_out, x2_out, q_low, d_low, top_all_in, top_all_out, low_all_in, low_all_out,
+               w, df, a, q, x0, x1, grad, x2, e1, part, landing, gut, gst, gq, gd,
+               top_in, top_out, low_in, low_out, *rest):
     bufs, (send_sems, recv_sems, local_sems, credits, x_free) = rest[:6], rest[6:]
     comm = Comm(send_sems, recv_sems, local_sems)
     tokens = x0.shape[0]
     x, c = comm.x, comm.c
     group = a.shape[0]
     load_d = comm.local((d0, df.at[x]))
-    loads = comm.local((ut_top, gut), (q_top, gq), (st_top, gst), (d_top, gd))
+    loads_in = comm.local((ut_top, gut), (q_top, gq))
+    comm.arrive('xyzc')
+    loads_out = comm.local((st_top, gst), (d_top, gd))
     columns = lambda ref, j: ref.at[:, pl.ds(j * group, group)]
     load_w = lambda ref: comm.local(*[(columns(ref, j), w.at[j]) for j in range(4)])
-    load2 = load_w(w2_hbm) + comm.local((a_hbm, a))
-    comm.barrier('xyzc')
+    comm.meet('xyzc')
 
     gather_d = ring_of_tokens(comm, df)
     done(load_d)
     gather_d.start()
-    done(loads)
+    load2 = load_w(w2_hbm) + comm.local((a_hbm, a))
+    load_x = comm.local((x0_hbm, x0), (e1_hbm, e1), (x1_hbm, x1))
     own_b = lambda ref: lambda cols: flat(ref[..., cols])
     top = [[(gut.at[k], own_b(gq.at[k])) for k in (0, 1)], [(gst.at[k], own_b(gd.at[k])) for k in (0, 1)]]
     upper = grad_chunks(comm, top, bufs, (top_in, top_out), credits)
@@ -840,12 +875,22 @@
 
         return product
 
-    t0.start()
+    done(loads_in)
+    t0.things[0].start()
+    done(loads_out)
+    t0.things[1].start()
+    top = Every([BlockGather(comm, top_in, top_all_in), BlockGather(comm, top_out, top_all_out)])
+    w_in, w_out = low_in.shape[2] // 2, low_out.shape[2] // 2
+    low = [(k, slice(None), slice(None)) for k in range(CHUNKS - 1)]
+    low += [(CHUNKS - 1, pl.ds(h * w_in, w_in), pl.ds(h * w_out, w_out)) for h in (0, 1)]
+    low = [Every([BlockGather(comm, low_in.at[k, :, i], low_all_in.at[k, :, :, :, i]),
+                  BlockGather(comm, low_out.at[k, :, o], low_all_out.at[k, :, :, :, o])]) for k, i, o in low]
+    low0, low1, low2, low3, low4 = low
     t1.start()
-    t2.start()
     gather_d.forward()
     t0.middle()
     gather_d.near()
+    t2.start()
     gather_d.finish()
     done(load2)
     backward_acts(df, by_columns(df), a, q)
@@ -865,97 +910,106 @@
     loads = comm.local(*[(ut_low.at[k], w.at[k]) for k in (0, 1)], *[(st_low.at[k], w.at[2 + k]) for k in (0, 1)],
                        (q_low, a.at[:, pl.ds(0, half)]))
     loads += comm.local(*[(d_low.at[k], a.at[pl.ds(k * tokens, tokens), pl.ds(half, half)]) for k in range(4)])
+    done(loads)
+    mine = lambda ref: lambda cols: flat(ref[..., pl.ds(pl.multiple_of(c * half + cols.start, cols.size), cols.size)])
+    other = lambda first: lambda cols: a[:, pl.ds(first + cols.start, cols.size)]
+    operands = [[(w.at[0], mine(q)), (w.at[1], other(0))], [(w.at[2], mine(df)), (w.at[3], other(half))]]
+    g0, g1, g2, g3, g4 = grad_chunks(comm, operands, bufs, (low_in, low_out), credits, upper)
+    t0.turn()
+    t0.free1()
+    t2.middle()
+    ring.middle_right()
+    t0.middle2()
     t1.middle()
     t3.start()
-    t0.turn()
-    t2.middle()
-    ring.middle_right()
+    t2.turn()
+    t0.finish()
+    ring.middle_left()
+    t0.free2()
+    t2.free1()
     t1.turn()
+    t1.free1()
     t3.middle()
-    ring.middle_left()
-    t0.middle2()
-    t2.turn()
     ring.finish()
     g = jnp.concatenate(ring.sums(), axis=1)
+    done(load_x)
     grad[...] = (e1[...] + norm_rows_vjp(x0[...].astype(F32), g)).astype(BF16)
+    keep = comm.local((grad, grad_out))
     ring.sent()
     comm.signal(x_free, 'x')
     load_part = comm.local((part_hbm, part))
-    t1.middle2()
-    t0.free1()
-    t1.free1()
     comm.wait(x_free, 'x')
     done(load_part)
-    ring = token_sums(comm, part, landing, tokens)
+    ring = token_sums(comm, part, landing, tokens, ring)
     ring.start_all()
+    t2.middle2()
+    t1.middle2()
+    g0.start()
     t3.turn()
-    t0.finish()
-    t0.free2()
-    t2.middle2()
-    done(loads)
-    mine = lambda ref: lambda cols: flat(ref[..., pl.ds(pl.multiple_of(c * half + cols.start, cols.size), cols.size)])
-    other = lambda first: lambda cols: a[:, pl.ds(first + cols.start, cols.size)]
-    low = [[(w.at[0], mine(q)), (w.at[1], other(0))], [(w.at[2], mine(df)), (w.at[3], other(half))]]
-    g0, g1, g2, g3 = grad_chunks(comm, low, bufs, (low_in, low_out), credits, upper)
-    g0.start()
+    t3.free1()
     t1.finish()
+    t2.finish()
+    ring.middle_left()
+    ring.middle_right()
+    g0.middle()
     t1.free2()
-    t2.free1()
+    t2.free2()
     t3.middle2()
-    t2.finish()
-    t2.free2()
-    t3.free1()
-    ring.middle_right()
-    ring.middle_left()
-    g0.middle()
     g1.start()
     t3.finish()
+    top.start()
     t3.free2()
-    top = Every([BlockGather(comm, top_in, top_all_in), BlockGather(comm, top_out, top_all_out)])
-    low = [Every([BlockGather(comm, low_in.at[k], low_all_in.at[k]), BlockGather(comm, low_out.at[k], low_all_out.at[k])])
-           for k in range(CHUNKS)]
-    low0, low1, low2, low3 = low
-    top.start()
     g0.turn()
-    g1.middle()
     ring.finish()
     x2[...] = (x1[...].astype(F32) + jnp.concatenate(ring.sums(), axis=1)).astype(BF16)
+    keep += comm.local((x2, x2_out))
+    g1.middle()
     g0.middle2()
     g2.start()
+    top.forward()
+    g0.finish()
+    top.near()
+    low0.start()
     g1.turn()
-    g0.finish()
-    top.forward()
-    low0.start()
     g2.middle()
-    top.near()
     g1.middle2()
     g3.start()
+    top.finish()
+    low0.forward()
     g2.turn()
     g1.finish()
     low1.start()
-    top.finish()
-    low0.forward()
+    g4.start()
     low0.near()
+    g2.middle2()
     g3.middle()
     low1.forward()
     low1.near()
+    g4.middle()
     low0.finish()
-    g2.middle2()
     low1.finish()
-    g3.turn()
     g2.finish()
     low2.start()
+    g3.turn()
+    g4.turn()
     g3.middle2()
     low2.forward()
+    low2.near()
+    g4.middle2()
     g3.finish()
     low3.start()
-    low2.near()
     low2.finish()
+    g4.finish()
+    low4.start()
     low3.forward()
     low3.near()
+    low4.forward()
+    low4.near()
     low3.finish()
+    low4.finish()
     for pair in [top] + low:
         pair.arrived()
+    done(keep)
     comm.end()
 
 
@@ -968,8 +1022,9 @@
     block = sds((tokens, width), BF16)
     outs = [block, block, sds(q_top.shape[1:], BF16), sds(d_top.shape[1:], BF16)] + [sds(s, F32) for s in tops + lows]
     acts = VMEM((group, slice_), BF16)
-    scratch = [VMEM((4, width, group), BF16), VMEM((4, tokens, width), BF16), acts, acts, VMEM((group, width), F32),
-               VMEM((6, tokens, width // 2), F32)]
+    scratch = [VMEM((4, width, group), BF16), VMEM((4, tokens, width), BF16), acts, acts]
+    scratch += [VMEM(block.shape, BF16) for _ in range(4)] + [VMEM(block.shape, F32), VMEM((group, width), F32),
+                                                              VMEM((6, tokens, width // 2), F32)]
     scratch += [VMEM(r.shape, BF16) for r in (ut_top, st_top, q_top, d_top)] + [VMEM(s, F32) for s in shapes + shapes]
     scratch += grad_buffers(width, slice_)
     ins = (x0, x1, e1, d0, part_hbm, w1_hbm.reshape(width, slice_), w2_hbm.reshape(slice_, width), a_hbm,
@@ -978,8 +1033,8 @@
         lower_half,
         name='lower_half',
         out_shape=tuple(outs),
-        in_specs=spaces('vvv' + 'h' * 11),
-        out_specs=tuple(spaces('vv' + 'h' * 6)),
+        in_specs=spaces('h' * 14),
+        out_specs=tuple(spaces('h' * 8)),
         scratch_shapes=scratch + [sems(LOWER[0]), sems(LOWER[1]), sems(LOWER[2]), pltpu.SemaphoreType.REGULAR((2 * CHUNKS, 2)),
                                   pltpu.SemaphoreType.REGULAR],
         compiler_params=pltpu.CompilerParams(collective_id=2, has_side_effects=True, vmem_limit_bytes=VMEM_BYTES),

time: 411 us -> 399 us (0.971)
  Pallas kernels: 407 us -> 394 us
    pallas_call x1, Pallas kernels: 202 us -> 195 us  [call_lower_half(): pl.pallas_call(lower_half, name='lower_half', out_shape=tuple(outs), in_s...]
    pallas_call x1, Pallas kernels: 193 us -> 188 us  [call(): pl.pallas_call(kernel, name=kernel.__name__, out_shape=tuple(outs), in_sp...]
where the time goes in v4:
time: 399 us; the launch traced here: 398 us
  Pallas kernels  394 us (99%)
    pallas_call x1, Pallas kernels, call_lower_half(): pl.pallas_call(lower_half, name='lower_half', out_shape=tuple(outs), in_s...  195 us
    pallas_call x1, Pallas kernels, call(): pl.pallas_call(kernel, name=kernel.__name__, out_shape=tuple(outs), in_sp...  188 us
    pallas_call x1, Pallas kernels, call_assemble(): pl.pallas_call(assemble, name='assemble', out_shape=(sds(in_shape, F32),...  11 us

profile of v4, /device:TPU:1, one launch (start us, length us, event | category | flops | bytes accessed | tf_op | source)
XLA Modules:
  0.0 398.3 jit_solution(8211606010652320627)
XLA Ops:
  0.6 187.8 %upper_half.1 = (bf16[128,2048]{1,0:T(8,128)(2,1)}, f32[128,2048]{1,0:T(8,128)}, bf16[128,2048]{1,0:T(8,128)(2,1)}, f32[512,2048]{1,0:T(8,128)}, bf16[512,2048]{...) custom-call(bf16[128,2048]{1,0:T(8,128)(2,1)} %x0_hbm.1, ...), custom_call_target="tpu_custom_call" | custom-call | flops 34359738368 | bytes 16777216 | tf_op jit(solution)/shard_map/upper_half/pallas_call | solution.py:642
  188.5 195.0 %lower_half.1 = (bf16[128,2048]{1,0:T(8,128)(2,1)}, bf16[128,2048]{1,0:T(8,128)(2,1)}, bf16[512,1024]{1,0:T(8,128)(2,1)}, bf16[4,128,1024]{2,1,0:T(8,128)(2,1)},...) custom-call(bf16[128,2048]{1,0:T(8,128)(2,1)} %x0_hbm.1, ...), custom_call_target="tpu_custom_call" | custom-call | flops 34359738368 | bytes 16777216 | tf_op jit(solution)/shard_map/lower_half/pallas_call | solution.py:1032
  383.5 11.0 %assemble.1 = (f32[2,128,8192]{2,1,0:T(8,128)}, f32[2,512,2048]{2,1,0:T(8,128)}) custom-call(f32[4,2,4,128,256]{4,3,2,1,0:T(8,128)} %get-tuple-element.39.top_in, f32[4,2,4,128,256]{4,3,2,1,0:T(8,128)} %get-tuple-element.40.top_out, f32[4,4,2,128,256]{4,3,2,1,0:T(8,128)} %get-tuple-element.41.low_in, f32[4,4,2,128,256]{4,3,2,1,0:T(8,128)} %get-tuple-element.42.low_out), custom_call_target="tpu_custom_call" | custom-call | flops 1073741824 | bytes 33554432 | tf_op jit(solution)/shard_map/assemble/pallas_call | solution.py:1078
  394.5 1.9 copy.10
  396.4 1.9 copy.11

commit v5 on v4

--- a/solution.py
+++ b/solution.py
@@ -176,15 +176,18 @@
     def left_to(self, k, src, group, sem):
         self.comm.send(src, self.landing.at[k], self.to_left, group, sem)
 
-    def start(self, far0, far1, right1, left0):
+    def start_far(self, far0, far1):
         self.right_to(0, far0, self.first, self.sems[0])
         self.left_to(3, far1, self.first, self.sems[1])
+
+    def start_near(self, right1, left0):
         self.right_to(1, right1, self.rest, self.sems[2])
         self.left_to(4, left0, self.rest, self.sems[2])
 
     def start_all(self):
         part = self.part
-        self.start(part(self.far, 0), part(self.far, 1), part(self.right, 1), part(self.left, 0))
+        self.start_far(part(self.far, 0), part(self.far, 1))
+        self.start_near(part(self.right, 1), part(self.left, 0))
 
     def start_half(self, half):
         if half == 0:
@@ -702,20 +705,30 @@
 
         lax.fori_loop(0, count * per, step, 0)
 
-    def start(self):
+    def start_far(self):
         me, sends = self.ring.me, self.sends
         if self.before:
             self.before.sent()
             self.comm.wait(self.credits.at[0], self.axes[0])
 
-        def where(i):
-            return (me + jnp.where(i < 2, 2, 2 * i - 3)) % 4, ((i + 1) // 2) % 2
-
         def store(i, rows, value):
             sends[i, rows] = value
 
-        self.products(4, where, store)
-        self.ring.start(*[sends.at[k] for k in range(4)])
+        self.products(2, lambda i: ((me + 2) % 4, i), store)
+        self.ring.start_far(sends.at[0], sends.at[1])
+
+    def start_near(self):
+        me, sends = self.ring.me, self.sends
+
+        def store(i, rows, value):
+            sends[2 + i, rows] = value
+
+        self.products(2, lambda i: ((me + 1 + 2 * i) % 4, 1 - i), store)
+        self.ring.start_near(sends.at[2], sends.at[3])
+
+    def start(self):
+        self.start_far()
+        self.start_near()
 
     def middle(self):
         me, landing = self.ring.me, self.landing1
@@ -860,7 +873,7 @@
     own_b = lambda ref: lambda cols: flat(ref[..., cols])
     top = [[(gut.at[k], own_b(gq.at[k])) for k in (0, 1)], [(gst.at[k], own_b(gd.at[k])) for k in (0, 1)]]
     upper = grad_chunks(comm, top, bufs, (top_in, top_out), credits)
-    t0, t1, t2, t3 = upper
+    (t0i, t0o), (t1i, t1o), (t2i, t2o), (t3i, t3o) = [pair.things for pair in upper]
 
     def by_columns(left):
         rows = w.shape[1] // 8
@@ -876,21 +889,27 @@
         return product
 
     done(loads_in)
-    t0.things[0].start()
+    t0i.start_far()
     done(loads_out)
-    t0.things[1].start()
+    t0o.start_far()
+    t0i.start_near()
+    t0o.start_near()
     top = Every([BlockGather(comm, top_in, top_all_in), BlockGather(comm, top_out, top_all_out)])
     w_in, w_out = low_in.shape[2] // 2, low_out.shape[2] // 2
     low = [(k, slice(None), slice(None)) for k in range(CHUNKS - 1)]
     low += [(CHUNKS - 1, pl.ds(h * w_in, w_in), pl.ds(h * w_out, w_out)) for h in (0, 1)]
     low = [Every([BlockGather(comm, low_in.at[k, :, i], low_all_in.at[k, :, :, :, i]),
                   BlockGather(comm, low_out.at[k, :, o], low_all_out.at[k, :, :, :, o])]) for k, i, o in low]
-    low0, low1, low2, low3, low4 = low
-    t1.start()
+    (low0i, low0o), (low1i, low1o), (low2i, low2o), (low3i, low3o), (low4i, low4o) = [pair.things for pair in low]
+    t3i.start()
+    t1i.start()
     gather_d.forward()
-    t0.middle()
+    t1o.start()
+    t0o.middle()
+    t0i.middle()
+    t3o.start()
     gather_d.near()
-    t2.start()
+    t2o.start()
     gather_d.finish()
     done(load2)
     backward_acts(df, by_columns(df), a, q)
@@ -904,6 +923,8 @@
     ring.start_half(0)
     backward_part(product, part, 1)
     ring.start_half(1)
+    t1o.middle()
+    t0o.turn()
     d_arrived()
     q_arrived()
     half = a.shape[1] // 2
@@ -914,22 +935,29 @@
     mine = lambda ref: lambda cols: flat(ref[..., pl.ds(pl.multiple_of(c * half + cols.start, cols.size), cols.size)])
     other = lambda first: lambda cols: a[:, pl.ds(first + cols.start, cols.size)]
     operands = [[(w.at[0], mine(q)), (w.at[1], other(0))], [(w.at[2], mine(df)), (w.at[3], other(half))]]
-    g0, g1, g2, g3, g4 = grad_chunks(comm, operands, bufs, (low_in, low_out), credits, upper)
-    t0.turn()
-    t0.free1()
-    t2.middle()
+    lower = grad_chunks(comm, operands, bufs, (low_in, low_out), credits, upper)
+    (g0i, g0o), (g1i, g1o), (g2i, g2o), (g3i, g3o), (g4i, g4o) = [pair.things for pair in lower]
+    t0o.free1()
+    t2i.start()
+    t1i.middle()
+    t0i.turn()
+    t0i.free1()
+    t3o.middle()
+    t0o.middle2()
     ring.middle_right()
-    t0.middle2()
-    t1.middle()
-    t3.start()
-    t2.turn()
-    t0.finish()
+    t2i.middle()
+    t3i.middle()
+    t2o.middle()
     ring.middle_left()
-    t0.free2()
-    t2.free1()
-    t1.turn()
-    t1.free1()
-    t3.middle()
+    t0i.middle2()
+    t1i.turn()
+    t1o.turn()
+    t0o.finish()
+    t1i.free1()
+    t1o.free1()
+    t3o.turn()
+    t2i.turn()
+    t2i.free1()
     ring.finish()
     g = jnp.concatenate(ring.sums(), axis=1)
     done(load_x)
@@ -942,71 +970,131 @@
     done(load_part)
     ring = token_sums(comm, part, landing, tokens, ring)
     ring.start_all()
-    t2.middle2()
-    t1.middle2()
-    g0.start()
-    t3.turn()
-    t3.free1()
-    t1.finish()
-    t2.finish()
+    t2o.turn()
+    t0i.finish()
+    t0i.free2()
+    t3i.turn()
+    t0o.free2()
+    t3i.free1()
+    t2o.free1()
+    t1i.middle2()
+    t3o.middle2()
+    t1o.middle2()
+    t2i.middle2()
+    t2o.middle2()
+    t3o.free1()
+    g0i.start()
+    t3i.middle2()
+    t3o.finish()
+    g0o.start()
+    t1i.finish()
+    t2i.finish()
+    t2o.finish()
+    t2o.free2()
+    t1o.finish()
+    t3o.free2()
+    t2i.free2()
+    t1i.free2()
+    t3i.finish()
+    t3i.free2()
+    t1o.free2()
+    ring.middle_right()
     ring.middle_left()
-    ring.middle_right()
-    g0.middle()
-    t1.free2()
-    t2.free2()
-    t3.middle2()
-    g1.start()
-    t3.finish()
+    g0i.middle()
     top.start()
-    t3.free2()
-    g0.turn()
+    g0o.middle()
+    g2o.start()
+    g2i.start()
+    g0i.turn()
+    g0o.turn()
+    g1i.start()
+    g1o.start()
+    g0o.middle2()
     ring.finish()
     x2[...] = (x1[...].astype(F32) + jnp.concatenate(ring.sums(), axis=1)).astype(BF16)
     keep += comm.local((x2, x2_out))
-    g1.middle()
-    g0.middle2()
-    g2.start()
+    g0i.middle2()
+    g2o.middle()
+    g2i.middle()
+    g1i.middle()
+    g1o.middle()
+    g3i.start()
+    g0o.finish()
+    low0o.start()
+    g0i.finish()
+    low0i.start()
     top.forward()
-    g0.finish()
     top.near()
-    low0.start()
-    g1.turn()
-    g2.middle()
-    g1.middle2()
-    g3.start()
+    low0o.forward()
+    g2o.turn()
+    g2i.turn()
+    low0i.forward()
+    g1i.turn()
+    low0o.near()
+    low0i.near()
+    g2i.middle2()
+    g1o.turn()
+    g1i.middle2()
+    g3o.start()
+    g2o.middle2()
+    g1i.finish()
+    g2i.finish()
+    low2i.start()
+    g1o.middle2()
+    low1i.start()
+    g4i.start()
+    g3o.middle()
+    g2o.finish()
+    g1o.finish()
+    g4o.start()
+    low1o.start()
+    low0o.finish()
+    g3i.middle()
     top.finish()
-    low0.forward()
-    g2.turn()
-    g1.finish()
-    low1.start()
-    g4.start()
-    low0.near()
-    g2.middle2()
-    g3.middle()
-    low1.forward()
-    low1.near()
-    g4.middle()
-    low0.finish()
-    low1.finish()
-    g2.finish()
-    low2.start()
-    g3.turn()
-    g4.turn()
-    g3.middle2()
-    low2.forward()
-    low2.near()
-    g4.middle2()
-    g3.finish()
-    low3.start()
-    low2.finish()
-    g4.finish()
-    low4.start()
-    low3.forward()
-    low3.near()
-    low4.forward()
-    low4.near()
-    low3.finish()
-    low4.finish()
+    low2o.start()
+    low0i.finish()
+    low2i.forward()
+    low2i.near()
+    low1i.forward()
+    low1i.near()
+    g4i.middle()
+    g3o.turn()
+    low1o.forward()
+    g4o.middle()
+    g3i.turn()
+    low2o.forward()
+    low2o.near()
+    g4i.turn()
+    g3o.middle2()
+    g4o.turn()
+    g3i.middle2()
+    g4i.middle2()
+    g3o.finish()
+    low3o.start()
+    low2i.finish()
+    g4o.middle2()
+    g3i.finish()
+    low1o.near()
+    low3i.start()
+    g4i.finish()
+    low4i.start()
+    g4o.finish()
+    low4o.start()
+    low3o.forward()
+    low3o.near()
+    low2o.finish()
+    low3i.forward()
+    low3i.near()
+    low4i.forward()
+    low1i.finish()
+    low4i.near()
+    low1o.finish()
+    low4o.forward()
+    low3o.finish()
+    low3i.finish()
+    low4i.finish()
+    low4o.near()
+    low4o.finish()
     for pair in [top] + low:
         pair.arrived()
     done(keep)

time: 399 us -> 396 us (level)
  no operation moved by 1% of the time
where the time goes in v5:
time: 396 us
  Pallas kernels  391 us (99%)
    pallas_call x1, Pallas kernels, call_lower_half(): pl.pallas_call(lower_half, name='lower_half', out_shape=tuple(outs), in_s...  192 us
    pallas_call x1, Pallas kernels, call(): pl.pallas_call(kernel, name=kernel.__name__, out_shape=tuple(outs), in_sp...  188 us
    pallas_call x1, Pallas kernels, call_assemble(): pl.pallas_call(assemble, name='assemble', out_shape=(sds(in_shape, F32),...  11 us

profile of v5, /device:TPU:1, one launch (start us, length us, event | category | flops | bytes accessed | tf_op | source)
XLA Modules:
  0.0 395.7 jit_solution(17389629040921917677)
XLA Ops:
  0.6 187.8 %upper_half.1 = (bf16[128,2048]{1,0:T(8,128)(2,1)}, f32[128,2048]{1,0:T(8,128)}, bf16[128,2048]{1,0:T(8,128)(2,1)}, f32[512,2048]{1,0:T(8,128)}, bf16[512,2048]{...) custom-call(bf16[128,2048]{1,0:T(8,128)(2,1)} %x0_hbm.1, ...), custom_call_target="tpu_custom_call" | custom-call | flops 34359738368 | bytes 16777216 | tf_op jit(solution)/shard_map/upper_half/pallas_call | solution.py:645
  188.5 192.4 %lower_half.1 = (bf16[128,2048]{1,0:T(8,128)(2,1)}, bf16[128,2048]{1,0:T(8,128)(2,1)}, bf16[512,1024]{1,0:T(8,128)(2,1)}, bf16[4,128,1024]{2,1,0:T(8,128)(2,1)},...) custom-call(bf16[128,2048]{1,0:T(8,128)(2,1)} %x0_hbm.1, ...), custom_call_target="tpu_custom_call" | custom-call | flops 34359738368 | bytes 16777216 | tf_op jit(solution)/shard_map/lower_half/pallas_call | solution.py:1120
  380.9 11.0 %assemble.1 = (f32[2,128,8192]{2,1,0:T(8,128)}, f32[2,512,2048]{2,1,0:T(8,128)}) custom-call(f32[4,2,4,128,256]{4,3,2,1,0:T(8,128)} %get-tuple-element.39.top_in, f32[4,2,4,128,256]{4,3,2,1,0:T(8,128)} %get-tuple-element.40.top_out, f32[4,4,2,128,256]{4,3,2,1,0:T(8,128)} %get-tuple-element.41.low_in, f32[4,4,2,128,256]{4,3,2,1,0:T(8,128)} %get-tuple-element.42.low_out), custom_call_target="tpu_custom_call" | custom-call | flops 1073741824 | bytes 33554432 | tf_op jit(solution)/shard_map/assemble/pallas_call | solution.py:1166
  391.9 1.9 copy.10
  393.8 1.9 copy.11

commit v6 on v5

--- a/solution.py
+++ b/solution.py
@@ -17,7 +17,7 @@
 VMEM = pltpu.VMEM
 VMEM_BYTES = 67043328
 UPPER = (40, 95)
-LOWER = (69, 116, 41)
+LOWER = (69, 116, 49)
 
 
 class Comm:
@@ -235,8 +235,8 @@
 
 
 class PlaneGather:
-    def __init__(self, comm, dims, first, full, cols, before=None):
-        self.comm = comm
+    def __init__(self, comm, dims, first, full, cols, before=None, out=None):
+        self.comm, self.out, self.kept = comm, out, []
         c = comm.c
         lead = dims[0] == first
         second = dims.replace(first, '')
@@ -253,15 +253,17 @@
                                 before and before.ring1)
         self.ring2 = RingGather(comm, second, lambda h: slot2(b, h), slot2, at(every, b, every), at(every, three, every),
                                 before and before.ring2)
-        self.line = lambda p: at(every, p, every)
-        self.both_cores = lambda p, ref: ref.at[(every, p, every, every, cols) if lead else (p, every, every, every, cols)]
+        self.line = lambda p, ref=full: ref.at[(every, p, c, every, cols) if lead else (p, every, c, every, cols)]
         self.whole, self.near_lines = at(every, every, every), at(every, three, every)
         self.group = Sends(comm, self.whole, before and before.group.sem)
         self.sems = before.sems if before else [comm.recv_sem(), comm.recv_sem()]
-        self.full = full
 
     def push(self, p, k=0):
-        self.comm.send(self.line(p), self.line(p), self.comm.partner, self.group, self.sems[k])
+        line = self.line(p)
+        target = line if self.out is None else self.line(p, self.out)
+        self.comm.send(line, target, self.comm.partner, self.group, self.sems[k])
+        if self.out is not None:
+            self.kept += self.comm.local((line, target))
 
     def start1(self):
         self.ring1.start()
@@ -287,27 +289,10 @@
         self.ring2.finish()
         self.push(self.ring2.far, 1)
 
-    def arrived_near(self):
+    def arrived(self):
         self.comm.wait_recv(self.near_lines, self.sems[0])
-
-    def arrived_far(self):
         self.comm.wait_recv(self.line(self.b), self.sems[1])
-
-    def arrived(self):
-        self.arrived_near()
-        self.arrived_far()
-
-    def copy_out(self, out, positions, kept):
-        both = self.both_cores
-        kept += self.comm.local(*[(both(p, self.full), both(p, out)) for p in positions])
-
-    def near_out(self, out, kept):
-        self.arrived_near()
-        self.copy_out(out, (self.b, self.ring2.left, self.ring2.right), kept)
-
-    def far_out(self, out, kept):
-        self.arrived_far()
-        self.copy_out(out, (self.ring2.far,), kept)
+        done(self.kept)
 
     def sent(self):
         self.ring1.sent()
@@ -315,9 +300,9 @@
         self.group.wait()
 
 
-def gathers(comm, dims, full, pieces, before=None):
+def gathers(comm, dims, full, pieces, before=None, out=None):
     width = full.shape[4] // pieces
-    out = [PlaneGather(comm, dims, dims[k % 2], full, pl.ds(k * width, width), before and before.things[k])
+    out = [PlaneGather(comm, dims, dims[k % 2], full, pl.ds(k * width, width), before and before.things[k], out)
            for k in range(pieces)]
     return [Every(out[k:k + 2]) for k in range(0, pieces, 2)]
 
@@ -454,20 +439,22 @@
     return ref.at[..., pl.ds(pl.multiple_of(k * width, width), width)]
 
 
-def upper_half(x0, cot, w_in, w_out,
+def upper_half(x0_hbm, cot, w_in, w_out,
                x1_out, e1_out, d0_out, part_out, a_low, ut_low, st_low, ut_top, st_top, q_top, d_top, w1_low, w2_low,
-               p1, p2, q1, q2, uf, df, a, s, q, ut, st, x1, d0, part, landing, e1,
+               p1, p2, q1, q2, uf, df, a, s, q, ut, st, x0, x1, d0, part, landing, e1,
                send_sems, recv_sems, local_sems, credits):
     comm = Comm(send_sems, recv_sems, local_sems)
     tokens = x0.shape[0]
     x, c = comm.x, comm.c
     p_free, q_free = credits.at[0], credits.at[1]
 
+    comm.arrive('xyzc')
+    load_x = comm.local((x0_hbm, x0))
     own0 = own_blocks(comm, w_in, w_out, 0, p1, p2)
+    load_d = comm.local((cot, df.at[x]))
     own1 = own_blocks(comm, w_in, w_out, 1, q1, q2)
-    comm.arrive('xyzc')
+    done(load_x)
     uf[x] = norm_rows(x0[...].astype(F32)).astype(BF16)
-    df[x] = cot[...]
     comm.meet('xyzc')
 
     gather_u = ring_of_tokens(comm, uf)
@@ -476,52 +463,52 @@
     g2, g3 = gathers(comm, 'yz', p2, 4)
     n1, = gathers(comm, 'zy', q1, 2)
     n2, = gathers(comm, 'yz', q2, 2)
-    done(own0)
+    done(own0 + load_d)
     g2.start1()
     gather_u.start()
-    gather_d.start()
+    g1.start1()
     done(own1)
-    g1.start1()
     g2.forward1()
     g3.start1()
     g1.forward1()
     g2.start2()
+    g3.forward1()
     gather_u.forward()
-    g3.forward1()
+    gather_d.start()
     g1.start2()
     gather_u.near()
-    gather_d.forward()
+    gather_u.finish()
     g1.forward2()
     g2.forward2()
-    n1.start1()
-    g3.start2()
     n2.start1()
     g2.near2()
-    gather_d.near()
-    g1.near2()
-    g1.finish2()
-    gather_u.finish()
+    g3.start2()
+    gather_d.forward()
+    n1.start1()
     transposed(uf, ut)
     pushed = [comm.push(ut, ut_low.at[1])]
     kept = comm.local((ut, ut_low.at[0]))
+    g1.near2()
+    gather_d.near()
+    g1.finish2()
+    g2.finish2()
     gather_d.finish()
-    g2.finish2()
     g1.arrived()
     forward_acts(uf, p1, a, s, st)
+    n2.forward1()
+    g3.forward2()
     g2.arrived()
-    n1.forward1()
-    g3.forward2()
     gather_u.sent()
     ring = token_sums(comm, part, landing, tokens)
     forward_part(s, p2, part, 0)
     ring.start_half(0)
-    g3.near2()
+    n1.forward1()
     pushed += [comm.push(st, st_low.at[1])]
     kept += comm.local((st, st_low.at[0]), (a, a_low))
+    g3.near2()
     pushed += [comm.push(last_dim_half(df, 1 - c), d_top.at[1])]
     kept_d = comm.local((last_dim_half(df, c), d_top.at[0]))
-    n2.forward1()
-    n1.start2()
+    n2.start2()
     g3.finish2()
     g3.arrived()
     forward_part(s, p2, part, 1)
@@ -535,19 +522,17 @@
     b2, = gathers(comm, 'yz', p2, 2, g2)
     done(own2)
     comm.wait(p_free, 'yzc')
+    b1.start1()
     b2.start1()
+    n1.start2()
+    n2.forward2()
+    ring.middle_right()
+    n2.near2()
+    b2.forward1()
+    b1.forward1()
+    ring.middle_left()
     n1.forward2()
-    n2.start2()
-    b1.start1()
-    ring.middle_right()
     n1.near2()
-    ring.middle_left()
-    n1.finish2()
-    b2.forward1()
-    n2.forward2()
-    n1.arrived()
-    n2.near2()
-    b1.forward1()
     ring.finish()
     x_next = (x0[...].astype(F32) + jnp.concatenate(ring.sums(), axis=1)).astype(BF16)
     x1[...] = x_next
@@ -556,16 +541,18 @@
     ring.sent()
     gather_v = ring_of_tokens(comm, uf, gather_u)
     gather_v.start()
+    n2.finish2()
     done(kept)
     pushed[0][0].wait()
     pushed[1][0].wait()
     b2.start2()
-    n2.finish2()
+    n2.arrived()
+    n1.finish2()
     gather_v.forward()
+    n1.arrived()
     b2.forward2()
     gather_v.near()
     b1.start2()
-    n2.arrived()
     b2.near2()
     gather_v.finish()
     forward_acts(uf, q1, a, s, st)
@@ -578,51 +565,49 @@
     n2.sent()
     comm.signal(q_free, 'yzc')
     own3 = own_blocks(comm, w_in, w_out, 0, q1, q2)
-    l1, = gathers(comm, 'zy', q1, 2, n1)
-    l2, = gathers(comm, 'yz', q2, 2, n2)
+    l1, = gathers(comm, 'zy', q1, 2, n1, w1_low)
+    l2, = gathers(comm, 'yz', q2, 2, n2, w2_low)
     b2.arrived()
     done(own3)
     comm.wait(q_free, 'yzc')
-    l1.start1()
+    l2.start1()
     b1.near2()
     backward_acts(df, lambda i: dot_bt(flat(df[...]), row_tile(p2, i)), a, q)
     b1.finish2()
-    l1.forward1()
+    l2.forward1()
+    l1.start1()
     transposed(uf, ut)
     pushed += [comm.push(ut, ut_top.at[1]), comm.push(st, st_top.at[1])]
     kept = kept_d + comm.local((ut, ut_top.at[0]), (st, st_top.at[0]))
-    l2.start1()
+    pushed += [comm.push(last_dim_half(q, 1 - c), q_top.at[1])]
+    kept += comm.local((last_dim_half(q, c), q_top.at[0]))
     b1.arrived()
     done(keep_part)
     ring = token_sums(comm, part, landing, tokens, ring)
     product = lambda i: dot_bt(q[...], row_tile(p1, i))
     backward_part(product, part, 0)
     ring.start_half(0)
-    l2.forward1()
-    l1.start2()
+    l1.forward1()
+    l2.start2()
     backward_part(product, part, 1)
     ring.start_half(1)
-    pushed += [comm.push(last_dim_half(q, 1 - c), q_top.at[1])]
-    kept += comm.local((last_dim_half(q, c), q_top.at[0]))
-    l2.start2()
+    l2.forward2()
+    l1.start2()
+    ring.middle_right()
+    l2.near2()
+    l2.finish2()
+    ring.middle_left()
     l1.forward2()
+    l2.arrived()
     l1.near2()
-    ring.middle_right()
-    l1.near_out(w1_low, kept)
-    l2.forward2()
-    ring.middle_left()
-    l2.near2()
     l1.finish2()
-    l2.near_out(w2_low, kept)
-    l1.far_out(w1_low, kept)
-    l2.finish2()
     ring.finish()
     g = jnp.concatenate(ring.sums(), axis=1)
-    e = cot[...].astype(F32) + norm_rows_vjp(x1[...].astype(F32), g)
+    e = df[x].astype(F32) + norm_rows_vjp(x1[...].astype(F32), g)
     e1[...] = e
     d0[...] = e.astype(BF16)
     kept += keep_x + comm.local((e1, e1_out), (d0, d0_out))
-    l2.far_out(w2_low, kept)
+    l1.arrived()
     for _, arrived in pushed:
         arrived()
     done(kept)
@@ -671,9 +656,9 @@
             sds(w1, BF16), sds(w2, BF16)]
     tok = (4, tokens, width)
     scratch = [VMEM(shape, BF16) for shape in (w1, w2, w1, w2, tok, tok, acts, acts, acts, ut, st, block.shape,
-                                            block.shape)]
+                                            block.shape, block.shape)]
     scratch += [VMEM((group, width), F32), VMEM((6, tokens, width // 2), F32), VMEM(block.shape, F32)]
-    return call(upper_half, (x0, cot, w_in, w_out), 'vvhh', outs, 'h' * 13, scratch, (UPPER, 35), 2, 1,
+    return call(upper_half, (x0, cot, w_in, w_out), 'hhhh', outs, 'h' * 13, scratch, (UPPER, 37), 2, 1,
                 16 * group * width * slice_)
 
 
@@ -848,6 +833,18 @@
         done(self.kept)
 
 
+def rows_from(src, dst, first):
+    n = src.shape[1] // 4
+    rows = [pl.ds(pl.multiple_of((first + k) % 4 * n, n), n) for k in range(4)]
+    pairs = [(src.at[:, r], dst.at[:, r]) for r in rows]
+    return pairs[0], pairs[1:]
+
+
+def columns_from(src, dst):
+    n = src.shape[-1] // CHUNKS
+    return [(src.at[..., cols], dst.at[..., cols]) for cols in (pl.ds(0, n), pl.ds(n, src.shape[-1] - n))]
+
+
 def lower_half(x0_hbm, x1_hbm, e1_hbm, d0, part_hbm, w1_hbm, w2_hbm, a_hbm, ut_low, st_low, ut_top, st_top, q_top, d_top,
                grad_out, x2_out, q_low, d_low, top_all_in, top_all_out, low_all_in, low_all_out,
                w, df, a, q, x0, x1, grad, x2, e1, part, landing, gut, gst, gq, gd,
@@ -858,9 +855,14 @@
     x, c = comm.x, comm.c
     group = a.shape[0]
     load_d = comm.local((d0, df.at[x]))
-    loads_in = comm.local((ut_top, gut), (q_top, gq))
+    far_in, rest_in = rows_from(ut_top, gut, comm.z + 2)
+    far_out, rest_out = rows_from(st_top, gst, comm.y + 2)
+    q_first, q_rest = columns_from(q_top, gq)
+    d_first, d_rest = columns_from(d_top, gd)
+    loads_in = comm.local(far_in, q_first)
+    loads_out = comm.local(far_out, d_first)
     comm.arrive('xyzc')
-    loads_out = comm.local((st_top, gst), (d_top, gd))
+    loads_rest = comm.local(q_rest, d_rest, *rest_in, *rest_out)
     columns = lambda ref, j: ref.at[:, pl.ds(j * group, group)]
     load_w = lambda ref: comm.local(*[(columns(ref, j), w.at[j]) for j in range(4)])
     comm.meet('xyzc')
@@ -892,6 +894,7 @@
     t0i.start_far()
     done(loads_out)
     t0o.start_far()
+    done(loads_rest)
     t0i.start_near()
     t0o.start_near()
     top = Every([BlockGather(comm, top_in, top_all_in), BlockGather(comm, top_out, top_all_out)])

time: 396 us -> 392 us (0.990)
  Pallas kernels: 391 us -> 387 us
where the time goes in v6:
time: 392 us; the launch traced here: 391 us
  Pallas kernels  387 us (99%)
    pallas_call x1, Pallas kernels, call_lower_half(): pl.pallas_call(lower_half, name='lower_half', out_shape=tuple(outs), in_s...  190 us
    pallas_call x1, Pallas kernels, call(): pl.pallas_call(kernel, name=kernel.__name__, out_shape=tuple(outs), in_sp...  186 us
    pallas_call x1, Pallas kernels, call_assemble(): pl.pallas_call(assemble, name='assemble', out_shape=(sds(in_shape, F32),...  11 us

profile of v6, /device:TPU:1, one launch (start us, length us, event | category | flops | bytes accessed | tf_op | source)
XLA Modules:
  0.0 391.4 jit_solution(17543703321371012608)
XLA Ops:
  0.6 185.5 %upper_half.1 = (bf16[128,2048]{1,0:T(8,128)(2,1)}, f32[128,2048]{1,0:T(8,128)}, bf16[128,2048]{1,0:T(8,128)(2,1)}, f32[512,2048]{1,0:T(8,128)}, bf16[512,2048]{...) custom-call(bf16[128,2048]{1,0:T(8,128)(2,1)} %x0_hbm.3, ...), custom_call_target="tpu_custom_call" | custom-call | flops 34359738368 | bytes 16777216 | tf_op jit(solution)/shard_map/upper_half/pallas_call | solution.py:630
  186.2 190.4 %lower_half.1 = (bf16[128,2048]{1,0:T(8,128)(2,1)}, bf16[128,2048]{1,0:T(8,128)(2,1)}, bf16[512,1024]{1,0:T(8,128)(2,1)}, bf16[4,128,1024]{2,1,0:T(8,128)(2,1)},...) custom-call(bf16[128,2048]{1,0:T(8,128)(2,1)} %x0_hbm.3, ...), custom_call_target="tpu_custom_call" | custom-call | flops 34359738368 | bytes 16777216 | tf_op jit(solution)/shard_map/lower_half/pallas_call | solution.py:1123
  376.6 11.0 %assemble.1 = (f32[2,128,8192]{2,1,0:T(8,128)}, f32[2,512,2048]{2,1,0:T(8,128)}) custom-call(f32[4,2,4,128,256]{4,3,2,1,0:T(8,128)} %get-tuple-element.39.top_in, f32[4,2,4,128,256]{4,3,2,1,0:T(8,128)} %get-tuple-element.40.top_out, f32[4,4,2,128,256]{4,3,2,1,0:T(8,128)} %get-tuple-element.41.low_in, f32[4,4,2,128,256]{4,3,2,1,0:T(8,128)} %get-tuple-element.42.low_out), custom_call_target="tpu_custom_call" | custom-call | flops 1073741824 | bytes 33554432 | tf_op jit(solution)/shard_map/assemble/pallas_call | solution.py:1169
  387.7 1.9 copy.10
  389.5 1.9 copy.11

commit v7 on v6

--- a/solution.py
+++ b/solution.py
@@ -16,8 +16,9 @@
 HBM = pltpu.HBM
 VMEM = pltpu.VMEM
 VMEM_BYTES = 67043328
+VMEM_KEPT = 33 << 19
 UPPER = (40, 95)
-LOWER = (69, 116, 49)
+LOWER = (69, 116, 38)
 
 
 class Comm:
@@ -169,6 +170,8 @@
         self.first = Sends(comm, landing.at[pl.ds(0, 2)], before and before.first.sem)
         self.rest = Sends(comm, landing.at[pl.ds(0, 4)], before and before.rest.sem)
         self.sems = before.sems if before else [comm.recv_sem() for _ in range(3)]
+        self.right_sem, self.left_sem, self.rest_sem = self.sems
+        self.pair, self.quad = landing.at[pl.ds(0, 2)], landing.at[pl.ds(0, 4)]
 
     def right_to(self, k, src, group, sem):
         self.comm.send(src, self.landing.at[k], self.to_right, group, sem)
@@ -177,12 +180,12 @@
         self.comm.send(src, self.landing.at[k], self.to_left, group, sem)
 
     def start_far(self, far0, far1):
-        self.right_to(0, far0, self.first, self.sems[0])
-        self.left_to(3, far1, self.first, self.sems[1])
+        self.right_to(0, far0, self.first, self.right_sem)
+        self.left_to(3, far1, self.first, self.left_sem)
 
     def start_near(self, right1, left0):
-        self.right_to(1, right1, self.rest, self.sems[2])
-        self.left_to(4, left0, self.rest, self.sems[2])
+        self.right_to(1, right1, self.rest, self.rest_sem)
+        self.left_to(4, left0, self.rest, self.rest_sem)
 
     def start_all(self):
         part = self.part
@@ -191,23 +194,23 @@
 
     def start_half(self, half):
         if half == 0:
-            self.right_to(0, self.part(self.far, 0), self.first, self.sems[0])
-            self.left_to(4, self.part(self.left, 0), self.rest, self.sems[2])
+            self.right_to(0, self.part(self.far, 0), self.first, self.right_sem)
+            self.left_to(4, self.part(self.left, 0), self.rest, self.rest_sem)
         else:
-            self.left_to(3, self.part(self.far, 1), self.first, self.sems[1])
-            self.right_to(1, self.part(self.right, 1), self.rest, self.sems[2])
+            self.left_to(3, self.part(self.far, 1), self.first, self.left_sem)
+            self.right_to(1, self.part(self.right, 1), self.rest, self.rest_sem)
 
     def wait_right(self):
-        self.comm.wait_recv(self.landing.at[0], self.sems[0])
+        self.comm.wait_recv(self.landing.at[0], self.right_sem)
 
     def wait_left(self):
-        self.comm.wait_recv(self.landing.at[3], self.sems[1])
+        self.comm.wait_recv(self.landing.at[3], self.left_sem)
 
     def pass_right(self):
-        self.right_to(2, self.landing.at[0], self.rest, self.sems[2])
+        self.right_to(2, self.landing.at[0], self.rest, self.rest_sem)
 
     def pass_left(self):
-        self.left_to(5, self.landing.at[3], self.rest, self.sems[2])
+        self.left_to(5, self.landing.at[3], self.rest, self.rest_sem)
 
     def middle_right(self):
         landing = self.landing
@@ -222,7 +225,7 @@
         self.pass_left()
 
     def finish(self):
-        self.comm.wait_recv(self.landing.at[pl.ds(0, 4)], self.sems[2])
+        self.comm.wait_recv(self.quad, self.rest_sem)
 
     def sent(self):
         self.first.wait()
@@ -663,32 +666,30 @@
 
 
 class GradReduce:
-    def __init__(self, comm, axes, operands, column, sends, landing1, landing2, result, credits, before=None):
+    def __init__(self, comm, axes, operands, column, sends, landing1, landing2, result, credits, before=None, unused=None):
         self.comm, self.axes, self.operands, self.column = comm, axes, operands, column
         self.sends, self.landing1, self.landing2, self.result = sends, landing1, landing2, result
-        self.credits, self.before = credits, before
+        self.credits, self.before, self.unused = credits, before, unused
         self.ring = RingReduce(comm, axes[0], None, landing1, before and before.ring)
-        rows = sends.shape[1] // 4
-        self.block = lambda pos, h: sends.at[pos // 2, pl.ds(pl.multiple_of(((pos % 2) * 2 + h) * rows, rows), rows)]
+        half = sends.shape[2] // 2
+        self.block = lambda pos, h: sends.at[pos // 2, pos % 2, pl.ds(h * half, half)]
         self.ring2 = RingReduce(comm, axes[1], self.block, landing2, before and before.ring2)
 
-    def products(self, count, where, store):
-        rows, width = self.sends.shape[1:]
-        t = min(128, rows)
-        per = rows // t
+    def products(self, where, store):
+        rows, width = self.sends.shape[2:]
 
         def step(n, _):
-            i, j = n // per, n % per
+            i, j = n // 2, n % 2
             pos, half = where(i)
-            start = pl.multiple_of((pos * 2 + half) * rows + j * t, t)
+            start = pl.multiple_of(((pos * 2 + half) * 2 + j) * rows, rows)
             value = None
             for at, b in self.operands:
-                term = dot(at[pl.ds(start, t)], b(pl.ds(self.column, width)))
+                term = dot(at[pl.ds(start, rows)], b(pl.ds(self.column, width)))
                 value = term if value is None else value + term
-            store(i, pl.ds(pl.multiple_of(j * t, t), t), value)
+            store(i, j, value)
             return 0
 
-        lax.fori_loop(0, count * per, step, 0)
+        lax.fori_loop(0, 4, step, 0)
 
     def start_far(self):
         me, sends = self.ring.me, self.sends
@@ -696,19 +697,19 @@
             self.before.sent()
             self.comm.wait(self.credits.at[0], self.axes[0])
 
-        def store(i, rows, value):
-            sends[i, rows] = value
-
-        self.products(2, lambda i: ((me + 2) % 4, i), store)
+        def store(i, j, value):
+            sends[i, j] = value
+
+        self.products(lambda i: ((me + 2) % 4, i), store)
         self.ring.start_far(sends.at[0], sends.at[1])
 
     def start_near(self):
         me, sends = self.ring.me, self.sends
 
-        def store(i, rows, value):
-            sends[2 + i, rows] = value
-
-        self.products(2, lambda i: ((me + 1 + 2 * i) % 4, 1 - i), store)
+        def store(i, j, value):
+            sends[2 + i, j] = value
+
+        self.products(lambda i: ((me + 1 + 2 * i) % 4, 1 - i), store)
         self.ring.start_near(sends.at[2], sends.at[3])
 
     def start(self):
@@ -720,10 +721,10 @@
         self.ring.wait_right()
         self.ring.wait_left()
 
-        def store(i, rows, value):
-            landing[3 * i, rows] = landing[3 * i, rows] + value
-
-        self.products(2, lambda i: ((me + 1 + 2 * i) % 4, i), store)
+        def store(i, j, value):
+            landing[3 * i, j] = landing[3 * i, j] + value
+
+        self.products(lambda i: ((me + 1 + 2 * i) % 4, i), store)
         self.ring.pass_right()
         self.ring.pass_left()
 
@@ -732,13 +733,16 @@
         self.ring.finish()
         self.ring.first.wait()
 
-        def store(i, rows, value):
-            sends[i, rows] = value + landing[2 - i, rows] + landing[4 + i, rows]
-
-        self.products(2, lambda i: (me, i), store)
+        def store(i, j, value):
+            sends[i, j] = value + landing[2 - i, j] + landing[4 + i, j]
+
+        self.products(lambda i: (me, i), store)
         if self.before:
             self.comm.wait(self.credits.at[1], self.axes[1])
         self.ring2.start_all()
+        if self.unused is not None:
+            self.ring.sent()
+            self.comm.signal(self.unused, 'xc')
 
     def free1(self):
         self.ring.sent()
@@ -764,55 +768,53 @@
 CHUNKS = 4
 
 
-def grad_buffers(width, slice_):
-    out = []
-    for rows, cols in ((width // 8, slice_ // 2), (slice_ // 8, width // 2)):
-        w = cols // CHUNKS
-        out += [VMEM((CHUNKS, 4, rows, w), F32), VMEM((CHUNKS, 6, rows, w), F32),
-                VMEM((CHUNKS, 6, rows // 4, w), F32)]
-    return out
-
-
-def result_shapes(width, slice_):
-    return [(CHUNKS, width // 16, slice_ // 2 // CHUNKS), (CHUNKS, slice_ // 16, width // 2 // CHUNKS)]
-
-
-def grad_chunks(comm, operands, bufs, results, credits, before=None):
+def grad_shapes(width, slice_):
+    return (width // 16, slice_ // 2 // CHUNKS), (slice_ // 16, width // 2 // CHUNKS)
+
+
+def grad_chunks(comm, operands, bufs, results, credits, before=None, unused=None):
     out = []
     for k in range(CHUNKS):
         pieces = 2 if before and k == CHUNKS - 1 else 1
         for piece in range(pieces):
             both = []
             for i, axes in enumerate(('zy', 'yz')):
-                width = bufs[3 * i].shape[3] // pieces
+                width = bufs[3 * i].shape[4] // pieces
                 cols = pl.ds(piece * width, width)
-                sends, land1, land2 = [ref.at[k, :, :, cols] for ref in bufs[3 * i:3 * i + 3]]
+                sends, land1 = [ref.at[k, :, :, :, cols] for ref in bufs[3 * i:3 * i + 2]]
+                land2 = bufs[3 * i + 2].at[k, :, :, cols]
                 both.append(GradReduce(comm, axes, operands[i], (k * pieces + piece) * width, sends, land1, land2,
-                                       results[i].at[k, :, cols], credits.at[2 * k + i],
-                                       before[k].things[i] if before and piece == 0 else None))
+                                       results(i, k, cols), credits.at[2 * k + i],
+                                       before[k].things[i] if before and piece == 0 else None,
+                                       unused.at[k + piece, i] if before else None))
             out.append(Every(both))
     return out
 
 
 class BlockGather:
-    def __init__(self, comm, own, out):
-        self.comm, self.own, self.out = comm, own, out
+    def __init__(self, comm, own, view, count, unused=None):
+        self.comm, self.own, self.view, self.unused = comm, own, view, unused
         c = comm.c
         n = own.shape[0] // 2
         half = lambda h: pl.ds(h * n, n)
-        self.ring = RingGather(comm, 'x', lambda h: own.at[half(h)], lambda p, h: out.at[p, c, half(h)],
-                               own, out.at[pl.ds(0, 3), c])
-        self.four = out.at[:, c]
+        self.ring = RingGather(comm, 'x', lambda h: own.at[half(h)], lambda p, h: view(p, c).at[half(h)], own, count(3))
+        self.four = count(4)
         self.group, self.sem = Sends(comm, self.four), comm.recv_sem()
+        self.kept = []
 
     def push(self, pos, src):
         c = self.comm
-        c.send(src, self.out.at[pos, c.c], c.partner, self.group, self.sem)
+        c.send(src, self.view(pos, c.c), c.partner, self.group, self.sem)
 
     def start(self):
+        here = self.view(self.ring.me, self.comm.c)
+        if self.unused is None:
+            self.kept = self.comm.local((self.own, here))
+        else:
+            self.comm.wait(self.unused, 'xc')
+            here[...] = self.own[...]
         self.ring.start()
         self.push(self.ring.me, self.own)
-        self.kept = self.comm.local((self.own, self.out.at[self.ring.me, self.comm.c]))
 
     def forward(self):
         self.ring.forward()
@@ -820,13 +822,13 @@
     def near(self):
         ring, c = self.ring, self.comm.c
         ring.near()
-        self.push(ring.left, self.out.at[ring.left, c])
-        self.push(ring.right, self.out.at[ring.right, c])
+        self.push(ring.left, self.view(ring.left, c))
+        self.push(ring.right, self.view(ring.right, c))
 
     def finish(self):
         ring, c = self.ring, self.comm.c
         ring.finish()
-        self.push(ring.far, self.out.at[ring.far, c])
+        self.push(ring.far, self.view(ring.far, c))
 
     def arrived(self):
         self.comm.wait_recv(self.four, self.sem)
@@ -846,10 +848,11 @@
 
 
 def lower_half(x0_hbm, x1_hbm, e1_hbm, d0, part_hbm, w1_hbm, w2_hbm, a_hbm, ut_low, st_low, ut_top, st_top, q_top, d_top,
-               grad_out, x2_out, q_low, d_low, top_all_in, top_all_out, low_all_in, low_all_out,
-               w, df, a, q, x0, x1, grad, x2, e1, part, landing, gut, gst, gq, gd,
-               top_in, top_out, low_in, low_out, *rest):
-    bufs, (send_sems, recv_sems, local_sems, credits, x_free) = rest[:6], rest[6:]
+               grad_out, x2_out, q_low, d_low, top_all_in, landed_in, landed_out, part,
+               w, df, a, q, x0, x1, grad, x2, e1, landing, gut, gst, gq, gd, top_in, top_out, low_in, low_out,
+               sends_in, sends_out, landing2_in, landing2_out,
+               send_sems, recv_sems, local_sems, credits, x_free, part_free, unused):
+    bufs = sends_in, landed_in, landing2_in, sends_out, landed_out, landing2_out
     comm = Comm(send_sems, recv_sems, local_sems)
     tokens = x0.shape[0]
     x, c = comm.x, comm.c
@@ -874,7 +877,9 @@
     load_x = comm.local((x0_hbm, x0), (e1_hbm, e1), (x1_hbm, x1))
     own_b = lambda ref: lambda cols: flat(ref[..., cols])
     top = [[(gut.at[k], own_b(gq.at[k])) for k in (0, 1)], [(gst.at[k], own_b(gd.at[k])) for k in (0, 1)]]
-    upper = grad_chunks(comm, top, bufs, (top_in, top_out), credits)
+    chunk_out = low_out.shape[2]
+    top_results = lambda i, k, cols: top_out.at[:, pl.ds(k * chunk_out, chunk_out)] if i else top_in.at[k]
+    upper = grad_chunks(comm, top, bufs, top_results, credits)
     (t0i, t0o), (t1i, t1o), (t2i, t2o), (t3i, t3o) = [pair.things for pair in upper]
 
     def by_columns(left):
@@ -897,12 +902,22 @@
     done(loads_rest)
     t0i.start_near()
     t0o.start_near()
-    top = Every([BlockGather(comm, top_in, top_all_in), BlockGather(comm, top_out, top_all_out)])
-    w_in, w_out = low_in.shape[2] // 2, low_out.shape[2] // 2
-    low = [(k, slice(None), slice(None)) for k in range(CHUNKS - 1)]
-    low += [(CHUNKS - 1, pl.ds(h * w_in, w_in), pl.ds(h * w_out, w_out)) for h in (0, 1)]
-    low = [Every([BlockGather(comm, low_in.at[k, :, i], low_all_in.at[k, :, :, :, i]),
-                  BlockGather(comm, low_out.at[k, :, o], low_all_out.at[k, :, :, :, o])]) for k, i, o in low]
+    topi = BlockGather(comm, top_in, lambda p, core: top_all_in.at[p, core], lambda n: top_all_in.at[pl.ds(0, n), 0])
+    rows, width = top_out.shape
+    topo = BlockGather(comm, top_out, lambda p, core: part.at[pl.ds(pl.multiple_of(p * rows, rows), rows),
+                                                              pl.ds(pl.multiple_of(core * width, width), width)],
+                       lambda n: part.at[pl.ds(0, n * rows), pl.ds(0, width)], part_free)
+
+    def low_gather(k, piece, pieces, i):
+        res, landed = (low_out, landed_out) if i else (low_in, landed_in)
+        n = res.shape[2] // pieces
+        cols = pl.ds(piece * n, n)
+        return BlockGather(comm, res.at[k, :, cols], lambda p, core: landed.at[k, p, core, :, cols],
+                           lambda m: landed.at[k, pl.ds(0, m), 0, :, cols], unused.at[k + piece, i])
+
+    last = CHUNKS - 1
+    low = [(k, 0, 1) for k in range(last)] + [(last, 0, 2), (last, 1, 2)]
+    low = [Every([low_gather(*piece, i) for i in (0, 1)]) for piece in low]
     (low0i, low0o), (low1i, low1o), (low2i, low2o), (low3i, low3o), (low4i, low4o) = [pair.things for pair in low]
     t3i.start()
     t1i.start()
@@ -938,7 +953,8 @@
     mine = lambda ref: lambda cols: flat(ref[..., pl.ds(pl.multiple_of(c * half + cols.start, cols.size), cols.size)])
     other = lambda first: lambda cols: a[:, pl.ds(first + cols.start, cols.size)]
     operands = [[(w.at[0], mine(q)), (w.at[1], other(0))], [(w.at[2], mine(df)), (w.at[3], other(half))]]
-    lower = grad_chunks(comm, operands, bufs, (low_in, low_out), credits, upper)
+    low_results = lambda i, k, cols: (low_out if i else low_in).at[k, :, cols]
+    lower = grad_chunks(comm, operands, bufs, low_results, credits, upper, unused)
     (g0i, g0o), (g1i, g1o), (g2i, g2o), (g3i, g3o), (g4i, g4o) = [pair.things for pair in lower]
     t0o.free1()
     t2i.start()
@@ -980,12 +996,12 @@
     t0o.free2()
     t3i.free1()
     t2o.free1()
+    t3o.free1()
     t1i.middle2()
     t3o.middle2()
     t1o.middle2()
     t2i.middle2()
     t2o.middle2()
-    t3o.free1()
     g0i.start()
     t3i.middle2()
     t3o.finish()
@@ -1004,7 +1020,7 @@
     ring.middle_right()
     ring.middle_left()
     g0i.middle()
-    top.start()
+    topi.start()
     g0o.middle()
     g2o.start()
     g2i.start()
@@ -1016,6 +1032,9 @@
     ring.finish()
     x2[...] = (x1[...].astype(F32) + jnp.concatenate(ring.sums(), axis=1)).astype(BF16)
     keep += comm.local((x2, x2_out))
+    ring.sent()
+    comm.signal(part_free, 'xc')
+    topo.start()
     g0i.middle2()
     g2o.middle()
     g2i.middle()
@@ -1026,9 +1045,11 @@
     low0o.start()
     g0i.finish()
     low0i.start()
-    top.forward()
-    top.near()
+    topi.forward()
+    topo.forward()
+    topi.near()
     low0o.forward()
+    topo.near()
     g2o.turn()
     g2i.turn()
     low0i.forward()
@@ -1040,10 +1061,10 @@
     g1i.middle2()
     g3o.start()
     g2o.middle2()
-    g1i.finish()
     g2i.finish()
     low2i.start()
     g1o.middle2()
+    g1i.finish()
     low1i.start()
     g4i.start()
     g3o.middle()
@@ -1053,7 +1074,8 @@
     low1o.start()
     low0o.finish()
     g3i.middle()
-    top.finish()
+    topi.finish()
+    topo.finish()
     low2o.start()
     low0i.finish()
     low2i.forward()
@@ -1098,7 +1120,7 @@
     low4i.finish()
     low4o.near()
     low4o.finish()
-    for pair in [top] + low:
+    for pair in [topi, topo] + low:
         pair.arrived()
     done(keep)
     comm.end()
@@ -1107,17 +1129,20 @@
 def call_lower_half(x0, x1, e1, d0, part_hbm, w1_hbm, w2_hbm, a_hbm, ut_low, st_low, ut_top, st_top, q_top, d_top):
     tokens, width = x0.shape
     group, slice_ = a_hbm.shape
-    shapes = result_shapes(width, slice_)
-    tops = [(4, 2) + shape for shape in shapes]
-    lows = [(CHUNKS, 4, 2) + shape[1:] for shape in shapes]
     block = sds((tokens, width), BF16)
-    outs = [block, block, sds(q_top.shape[1:], BF16), sds(d_top.shape[1:], BF16)] + [sds(s, F32) for s in tops + lows]
+    shapes = grad_shapes(width, slice_)
+    landed = [VMEM((CHUNKS, 6, 2) + shape, F32) for shape in shapes]
+    (rows_in, cols_in), (rows_out, cols_out) = shapes
+    outs = [block, block, sds(q_top.shape[1:], BF16), sds(d_top.shape[1:], BF16),
+            sds((4, 2, CHUNKS, rows_in, cols_in), F32)] + landed + [VMEM((group, width), F32)]
     acts = VMEM((group, slice_), BF16)
     scratch = [VMEM((4, width, group), BF16), VMEM((4, tokens, width), BF16), acts, acts]
-    scratch += [VMEM(block.shape, BF16) for _ in range(4)] + [VMEM(block.shape, F32), VMEM((group, width), F32),
-                                                              VMEM((6, tokens, width // 2), F32)]
-    scratch += [VMEM(r.shape, BF16) for r in (ut_top, st_top, q_top, d_top)] + [VMEM(s, F32) for s in shapes + shapes]
-    scratch += grad_buffers(width, slice_)
+    scratch += [VMEM(block.shape, BF16) for _ in range(4)] + [VMEM(block.shape, F32), VMEM((6, tokens, width // 2), F32)]
+    scratch += [VMEM(r.shape, BF16) for r in (ut_top, st_top, q_top, d_top)]
+    scratch += [VMEM(shape, F32) for shape in ((CHUNKS, rows_in, cols_in), (rows_out, CHUNKS * cols_out),
+                                               (CHUNKS, rows_in, cols_in), (CHUNKS, rows_out, cols_out))]
+    scratch += [VMEM((CHUNKS, 4, 2) + shape, F32) for shape in shapes]
+    scratch += [VMEM((CHUNKS, 6, rows // 2, cols), F32) for rows, cols in shapes]
     ins = (x0, x1, e1, d0, part_hbm, w1_hbm.reshape(width, slice_), w2_hbm.reshape(slice_, width), a_hbm,
            ut_low, st_low, ut_top, st_top, q_top, d_top)
     return pl.pallas_call(
@@ -1125,57 +1150,57 @@
         name='lower_half',
         out_shape=tuple(outs),
         in_specs=spaces('h' * 14),
-        out_specs=tuple(spaces('h' * 8)),
+        out_specs=tuple(spaces('hhhhhvvv')),
         scratch_shapes=scratch + [sems(LOWER[0]), sems(LOWER[1]), sems(LOWER[2]), pltpu.SemaphoreType.REGULAR((2 * CHUNKS, 2)),
-                                  pltpu.SemaphoreType.REGULAR],
-        compiler_params=pltpu.CompilerParams(collective_id=2, has_side_effects=True, vmem_limit_bytes=VMEM_BYTES),
+                                  pltpu.SemaphoreType.REGULAR, pltpu.SemaphoreType.REGULAR,
+                                  pltpu.SemaphoreType.REGULAR((CHUNKS + 1, 2))],
+        compiler_params=pltpu.CompilerParams(collective_id=2, has_side_effects=True,
+                                             vmem_limit_bytes=VMEM_BYTES - VMEM_KEPT),
         cost_estimate=pl.CostEstimate(flops=16 * group * width * slice_, bytes_accessed=1 << 24, transcendentals=0),
     )(*ins)
 
 
-def assemble(top_in, top_out, low_in, low_out, grad_in, grad_out, v_top_in, v_top_out, v_low_in, v_low_out,
-             load_sems, store_sems):
-    loads = []
-    refs = (v_low_in, v_low_out, v_top_in, v_top_out)
-    for i, src in enumerate((low_in, low_out, top_in, top_out)):
-        copy = pltpu.make_async_copy(src, refs[i], load_sems.at[i])
-        copy.start()
-        loads.append(copy)
+def assemble(landed_in, landed_out, part, top_in, grad_in, grad_out, v_top_in, load_sem, store_sems):
+    load = pltpu.make_async_copy(top_in, v_top_in, load_sem)
+    load.start()
     strip = grad_in.shape[2] // 64
-    rows, width = low_in.shape[3:]
-    width_out = low_out.shape[4]
-    per = width // strip
-    for i, ref in enumerate(refs):
-        loads[i].wait()
-        layer = i // 2
-        for k in range(CHUNKS):
-            for x in range(4):
-                for c in range(2):
-                    src = ref.at[x, c, k] if layer else ref.at[k, x, c]
-                    if i % 2:
-                        dst = grad_out.at[layer, pl.ds(x * src.shape[0], src.shape[0]),
-                                          pl.ds((c * CHUNKS + k) * width_out, width_out)]
-                        pltpu.make_async_copy(src, dst, store_sems.at[1]).start()
-                        continue
-                    for j in range(per):
-                        y, z = (c * 8 + k * per + j) // 4, (k * per + j) % 4
-                        dst = grad_in.at[layer, :, pl.ds(((4 * z + y) * 4 + x) * strip, strip)]
-                        pltpu.make_async_copy(src.at[:, pl.ds(j * strip, strip)], dst, store_sems.at[0]).start()
+    rows, width = landed_out.shape[-2:]
+    per = landed_in.shape[-1] // strip
+
+    def store_in(layer, block):
+        for x in range(4):
+            for n in range(2 * CHUNKS):
+                c, k = n // CHUNKS, n % CHUNKS
+                for j in range(per):
+                    t = k * per + j
+                    y, z = 2 * c + t // 4, t % 4
+                    dst = grad_in.at[layer, :, pl.ds(((4 * z + y) * 4 + x) * strip, strip)]
+                    pltpu.make_async_copy(block(x, c, k).at[:, pl.ds(j * strip, strip)], dst, store_sems.at[0]).start()
+
+    pltpu.make_async_copy(part, grad_out.at[1], store_sems.at[1]).start()
+    store_in(0, lambda x, c, k: landed_in.at[k, x, c])
+    for x in range(4):
+        for n in range(2 * CHUNKS):
+            dst = grad_out.at[0, pl.ds(x * rows, rows), pl.ds(n * width, width)]
+            pltpu.make_async_copy(landed_out.at[n % CHUNKS, x, n // CHUNKS], dst, store_sems.at[1]).start()
+    load.wait()
+    store_in(1, lambda x, c, k: v_top_in.at[x, c, k])
     pltpu.make_async_copy(grad_in, grad_in, store_sems.at[0]).wait()
     pltpu.make_async_copy(grad_out, grad_out, store_sems.at[1]).wait()
 
 
-def call_assemble(ins, in_shape, out_shape):
+def call_assemble(top_in, kept, in_shape, out_shape):
+    kept = [pltpu.with_memory_space_constraint(ref, VMEM) for ref in kept]
     return pl.pallas_call(
         assemble,
         name='assemble',
         out_shape=(sds(in_shape, F32), sds(out_shape, F32)),
-        in_specs=spaces('hhhh'),
+        in_specs=spaces('vvvh'),
         out_specs=tuple(spaces('hh')),
-        scratch_shapes=[VMEM(r.shape, F32) for r in ins] + [sems(4), sems(2)],
-        compiler_params=pltpu.CompilerParams(vmem_limit_bytes=VMEM_BYTES),
+        scratch_shapes=[VMEM(top_in.shape, F32), pltpu.SemaphoreType.DMA, sems(2)],
+        compiler_params=pltpu.CompilerParams(vmem_limit_bytes=VMEM_BYTES - VMEM_KEPT),
         cost_estimate=pl.CostEstimate(flops=1 << 30, bytes_accessed=1 << 25, transcendentals=0),
-    )(*ins)
+    )(*kept, top_in)
 
 
 def solution(mesh):
@@ -1185,9 +1210,9 @@
     def device_step(tokens, cotangent, w_in, w_out):
         (x1, e1, d0, part_out, a_low, ut_low, st_low, ut_top, st_top, q_top, d_top, w1_low, w2_low) = call_upper_half(
             tokens, cotangent, w_in, w_out)
-        grad, x2, _, _, *gathered = call_lower_half(
+        grad, x2, _, _, top_in, *kept = call_lower_half(
             tokens, x1, e1, d0, part_out, w1_low, w2_low, a_low, ut_low, st_low, ut_top, st_top, q_top, d_top)
-        grad_in, grad_out = call_assemble(gathered, w_in.shape, w_out.shape)
+        grad_in, grad_out = call_assemble(top_in, kept, w_in.shape, w_out.shape)
         return x2, grad_in, grad_out, grad
 
     return jax.shard_map(device_step, mesh=mesh, in_specs=(tok_spec, tok_spec, w_spec, w_spec),

time: 392 us -> 387 us (0.987)
  no operation moved by 1% of the time
where the time goes in v7:
time: 387 us
  Pallas kernels  384 us (99%)
    pallas_call x1, Pallas kernels, call_lower_half(): pl.pallas_call(lower_half, name='lower_half', out_shape=tuple(outs), in_s...  191 us
    pallas_call x1, Pallas kernels, call(): pl.pallas_call(kernel, name=kernel.__name__, out_shape=tuple(outs), in_sp...  186 us

profile of v7, /device:TPU:1, one launch (start us, length us, event | category | flops | bytes accessed | tf_op | source)
XLA Modules:
  0.0 387.1 jit_solution(15901390382815710890)
XLA Ops:
  0.6 185.5 %upper_half.1 = (bf16[128,2048]{1,0:T(8,128)(2,1)}, f32[128,2048]{1,0:T(8,128)}, bf16[128,2048]{1,0:T(8,128)(2,1)}, f32[512,2048]{1,0:T(8,128)}, bf16[512,2048]{...) custom-call(bf16[128,2048]{1,0:T(8,128)(2,1)} %x0_hbm.3, ...), custom_call_target="tpu_custom_call" | custom-call | flops 34359738368 | bytes 16777216 | tf_op jit(solution)/shard_map/upper_half/pallas_call | solution.py:633
  186.2 190.5 %lower_half.1 = (bf16[128,2048]{1,0:T(8,128)(2,1)}, bf16[128,2048]{1,0:T(8,128)(2,1)}, bf16[512,1024]{1,0:T(8,128)(2,1)}, bf16[4,128,1024]{2,1,0:T(8,128)(2,1)},...) custom-call(bf16[128,2048]{1,0:T(8,128)(2,1)} %x0_hbm.3, ...), custom_call_target="tpu_custom_call" | custom-call | flops 34359738368 | bytes 16777216 | tf_op jit(solution)/shard_map/lower_half/pallas_call | solution.py:1148
  376.7 0.0 copy-start
  376.7 7.7 %assemble.1 = (f32[2,128,8192]{2,1,0:T(8,128)}, f32[2,512,2048]{2,1,0:T(8,128)}) custom-call(f32[4,6,2,128,256]{4,3,2,1,0:T(8,128)S(1)} %get-tuple-element.39.landed_in, f32[4,6,2,128,256]{4,3,2,1,0:T(8,128)S(1)} %get-tuple-element.40.landed_out, f32[512,2048]{1,0:T(8,128)S(1)} %get-tuple-element.41.part, f32[4,2,4,128,256]{4,3,2,1,0:T(8,128)} %get-tuple-element.42.top_in), custom_call_target="tpu_custom_call" | custom-call | flops 1073741824 | bytes 33554432 | tf_op jit(solution)/shard_map/assemble/pallas_call | solution.py:1194
  384.4 1.9 copy.10
  386.3 0.0 copy-done
  386.3 0.8 copy.11
Async XLA Ops:
  376.7 9.6 %copy-start = (bf16[128,2048]{1,0:T(8,128)(2,1)S(1)}, bf16[128,2048]{1,0:T(8,128)(2,1)}, u32[]{:S(2)}) copy-start(bf16[128,2048]{1,0:T(8,128)(2,1)} %get-tuple-element.53) | copy-start | bytes 1572868

commit v8 on v7

--- a/solution.py
+++ b/solution.py
@@ -16,9 +16,9 @@
 HBM = pltpu.HBM
 VMEM = pltpu.VMEM
 VMEM_BYTES = 67043328
-VMEM_KEPT = 33 << 19
+VMEM_KEPT = 169 << 17
 UPPER = (40, 95)
-LOWER = (69, 116, 38)
+LOWER = (69, 116, 35)
 
 
 class Comm:
@@ -848,13 +848,13 @@
 
 
 def lower_half(x0_hbm, x1_hbm, e1_hbm, d0, part_hbm, w1_hbm, w2_hbm, a_hbm, ut_low, st_low, ut_top, st_top, q_top, d_top,
-               grad_out, x2_out, q_low, d_low, top_all_in, landed_in, landed_out, part,
-               w, df, a, q, x0, x1, grad, x2, e1, landing, gut, gst, gq, gd, top_in, top_out, low_in, low_out,
+               q_low, d_low, grad, x2, landed_in, landed_out, part, landing,
+               w, df, a, q, xv, e1, gut, gst, gq, gd, top_in, top_out, low_in, low_out,
                sends_in, sends_out, landing2_in, landing2_out,
-               send_sems, recv_sems, local_sems, credits, x_free, part_free, unused):
+               send_sems, recv_sems, local_sems, credits, x_free, in_free, out_free, unused):
     bufs = sends_in, landed_in, landing2_in, sends_out, landed_out, landing2_out
     comm = Comm(send_sems, recv_sems, local_sems)
-    tokens = x0.shape[0]
+    tokens = xv.shape[0]
     x, c = comm.x, comm.c
     group = a.shape[0]
     load_d = comm.local((d0, df.at[x]))
@@ -874,11 +874,11 @@
     done(load_d)
     gather_d.start()
     load2 = load_w(w2_hbm) + comm.local((a_hbm, a))
-    load_x = comm.local((x0_hbm, x0), (e1_hbm, e1), (x1_hbm, x1))
+    load_x = comm.local((x0_hbm, xv), (e1_hbm, e1))
     own_b = lambda ref: lambda cols: flat(ref[..., cols])
     top = [[(gut.at[k], own_b(gq.at[k])) for k in (0, 1)], [(gst.at[k], own_b(gd.at[k])) for k in (0, 1)]]
     chunk_out = low_out.shape[2]
-    top_results = lambda i, k, cols: top_out.at[:, pl.ds(k * chunk_out, chunk_out)] if i else top_in.at[k]
+    top_results = lambda i, k, cols: (top_out if i else top_in).at[:, pl.ds(k * chunk_out, chunk_out)]
     upper = grad_chunks(comm, top, bufs, top_results, credits)
     (t0i, t0o), (t1i, t1o), (t2i, t2o), (t3i, t3o) = [pair.things for pair in upper]
 
@@ -902,32 +902,13 @@
     done(loads_rest)
     t0i.start_near()
     t0o.start_near()
-    topi = BlockGather(comm, top_in, lambda p, core: top_all_in.at[p, core], lambda n: top_all_in.at[pl.ds(0, n), 0])
-    rows, width = top_out.shape
-    topo = BlockGather(comm, top_out, lambda p, core: part.at[pl.ds(pl.multiple_of(p * rows, rows), rows),
-                                                              pl.ds(pl.multiple_of(core * width, width), width)],
-                       lambda n: part.at[pl.ds(0, n * rows), pl.ds(0, width)], part_free)
-
-    def low_gather(k, piece, pieces, i):
-        res, landed = (low_out, landed_out) if i else (low_in, landed_in)
-        n = res.shape[2] // pieces
-        cols = pl.ds(piece * n, n)
-        return BlockGather(comm, res.at[k, :, cols], lambda p, core: landed.at[k, p, core, :, cols],
-                           lambda m: landed.at[k, pl.ds(0, m), 0, :, cols], unused.at[k + piece, i])
-
-    last = CHUNKS - 1
-    low = [(k, 0, 1) for k in range(last)] + [(last, 0, 2), (last, 1, 2)]
-    low = [Every([low_gather(*piece, i) for i in (0, 1)]) for piece in low]
-    (low0i, low0o), (low1i, low1o), (low2i, low2o), (low3i, low3o), (low4i, low4o) = [pair.things for pair in low]
-    t3i.start()
+    t2o.start()
     t1i.start()
     gather_d.forward()
+    t2i.start()
+    t0o.middle()
+    gather_d.near()
     t1o.start()
-    t0o.middle()
-    t0i.middle()
-    t3o.start()
-    gather_d.near()
-    t2o.start()
     gather_d.finish()
     done(load2)
     backward_acts(df, by_columns(df), a, q)
@@ -939,16 +920,52 @@
     product = by_columns(q)
     backward_part(product, part, 0)
     ring.start_half(0)
+    t2i.middle()
+    t2o.middle()
+    t0o.turn()
+    t0o.free1()
+    t0i.middle()
     backward_part(product, part, 1)
     ring.start_half(1)
-    t1o.middle()
-    t0o.turn()
     d_arrived()
     q_arrived()
     half = a.shape[1] // 2
     loads = comm.local(*[(ut_low.at[k], w.at[k]) for k in (0, 1)], *[(st_low.at[k], w.at[2 + k]) for k in (0, 1)],
                        (q_low, a.at[:, pl.ds(0, half)]))
     loads += comm.local(*[(d_low.at[k], a.at[pl.ds(k * tokens, tokens), pl.ds(half, half)]) for k in range(4)])
+    t1o.middle()
+    t2i.turn()
+    t0o.middle2()
+    t2i.free1()
+    t3i.start()
+    ring.middle_right()
+    t2o.turn()
+    topi = BlockGather(comm, top_in, lambda p, core: landing.at[p * 2 + core], lambda n: landing.at[pl.ds(0, n)], in_free)
+    rows, width = top_out.shape
+    topo = BlockGather(comm, top_out, lambda p, core: part.at[pl.ds(pl.multiple_of(p * rows, rows), rows),
+                                                              pl.ds(pl.multiple_of(core * width, width), width)],
+                       lambda n: part.at[pl.ds(0, n * rows), pl.ds(0, width)], out_free)
+
+    def low_gather(k, piece, pieces, i):
+        res, landed = (low_out, landed_out) if i else (low_in, landed_in)
+        n = res.shape[2] // pieces
+        cols = pl.ds(piece * n, n)
+        return BlockGather(comm, res.at[k, :, cols], lambda p, core: landed.at[k, p, core, :, cols],
+                           lambda m: landed.at[k, pl.ds(0, m), 0, :, cols], unused.at[k + piece, i])
+
+    last = CHUNKS - 1
+    low = [(k, 0, 1) for k in range(last)] + [(last, 0, 2), (last, 1, 2)]
+    low = [Every([low_gather(*piece, i) for i in (0, 1)]) for piece in low]
+    (low0i, low0o), (low1i, low1o), (low2i, low2o), (low3i, low3o), (low4i, low4o) = [pair.things for pair in low]
+    t2o.free1()
+    t0i.turn()
+    t0i.free1()
+    t1o.turn()
+    t1o.free1()
+    ring.middle_left()
+    t2i.middle2()
+    t3o.start()
+    t0i.middle2()
     done(loads)
     mine = lambda ref: lambda cols: flat(ref[..., pl.ds(pl.multiple_of(c * half + cols.start, cols.size), cols.size)])
     other = lambda first: lambda cols: a[:, pl.ds(first + cols.start, cols.size)]
@@ -956,32 +973,19 @@
     low_results = lambda i, k, cols: (low_out if i else low_in).at[k, :, cols]
     lower = grad_chunks(comm, operands, bufs, low_results, credits, upper, unused)
     (g0i, g0o), (g1i, g1o), (g2i, g2o), (g3i, g3o), (g4i, g4o) = [pair.things for pair in lower]
-    t0o.free1()
-    t2i.start()
+    t0o.finish()
+    t0o.free2()
+    t2i.finish()
     t1i.middle()
-    t0i.turn()
-    t0i.free1()
+    t2o.middle2()
     t3o.middle()
-    t0o.middle2()
-    ring.middle_right()
-    t2i.middle()
+    t1o.middle2()
     t3i.middle()
-    t2o.middle()
-    ring.middle_left()
-    t0i.middle2()
-    t1i.turn()
-    t1o.turn()
-    t0o.finish()
-    t1i.free1()
-    t1o.free1()
-    t3o.turn()
-    t2i.turn()
-    t2i.free1()
     ring.finish()
     g = jnp.concatenate(ring.sums(), axis=1)
     done(load_x)
-    grad[...] = (e1[...] + norm_rows_vjp(x0[...].astype(F32), g)).astype(BF16)
-    keep = comm.local((grad, grad_out))
+    grad[...] = (e1[...] + norm_rows_vjp(xv[...].astype(F32), g)).astype(BF16)
+    load_x = comm.local((x1_hbm, xv))
     ring.sent()
     comm.signal(x_free, 'x')
     load_part = comm.local((part_hbm, part))
@@ -989,140 +993,136 @@
     done(load_part)
     ring = token_sums(comm, part, landing, tokens, ring)
     ring.start_all()
-    t2o.turn()
     t0i.finish()
+    t1i.turn()
+    t1i.free1()
+    t2i.free2()
+    t2o.finish()
+    g0o.start()
+    t1o.finish()
+    t1o.free2()
+    g2i.start()
     t0i.free2()
+    t3o.turn()
+    t3o.free1()
     t3i.turn()
-    t0o.free2()
+    t1i.middle2()
+    ring.middle_left()
     t3i.free1()
-    t2o.free1()
-    t3o.free1()
-    t1i.middle2()
+    ring.middle_right()
+    g0o.middle()
+    g2i.middle()
+    t3i.middle2()
     t3o.middle2()
-    t1o.middle2()
-    t2i.middle2()
-    t2o.middle2()
     g0i.start()
-    t3i.middle2()
+    t1i.finish()
+    g1o.start()
+    t2o.free2()
+    g2i.turn()
+    g0o.turn()
     t3o.finish()
-    g0o.start()
-    t1i.finish()
-    t2i.finish()
-    t2o.finish()
-    t2o.free2()
-    t1o.finish()
-    t3o.free2()
-    t2i.free2()
-    t1i.free2()
     t3i.finish()
     t3i.free2()
-    t1o.free2()
-    ring.middle_right()
-    ring.middle_left()
+    t1i.free2()
+    t3o.free2()
+    ring.finish()
+    done(load_x)
+    x2[...] = (xv[...].astype(F32) + jnp.concatenate(ring.sums(), axis=1)).astype(BF16)
+    ring.sent()
+    comm.signal(in_free, 'xc')
+    comm.signal(out_free, 'xc')
+    topo.start()
+    topi.start()
     g0i.middle()
-    topi.start()
-    g0o.middle()
+    g1o.middle()
+    topo.forward()
+    g2i.middle2()
+    g0o.middle2()
+    g1i.start()
     g2o.start()
-    g2i.start()
+    topo.near()
     g0i.turn()
-    g0o.turn()
-    g1i.start()
-    g1o.start()
-    g0o.middle2()
-    ring.finish()
-    x2[...] = (x1[...].astype(F32) + jnp.concatenate(ring.sums(), axis=1)).astype(BF16)
-    keep += comm.local((x2, x2_out))
-    ring.sent()
-    comm.signal(part_free, 'xc')
-    topo.start()
-    g0i.middle2()
-    g2o.middle()
-    g2i.middle()
-    g1i.middle()
-    g1o.middle()
-    g3i.start()
     g0o.finish()
+    g1o.turn()
     low0o.start()
-    g0i.finish()
-    low0i.start()
-    topi.forward()
-    topo.forward()
-    topi.near()
-    low0o.forward()
-    topo.near()
-    g2o.turn()
-    g2i.turn()
-    low0i.forward()
-    g1i.turn()
-    low0o.near()
-    low0i.near()
-    g2i.middle2()
-    g1o.turn()
-    g1i.middle2()
-    g3o.start()
-    g2o.middle2()
     g2i.finish()
     low2i.start()
+    g1i.middle()
+    topi.forward()
+    g2o.middle()
     g1o.middle2()
+    g3i.start()
+    g0i.middle2()
+    g3o.start()
+    topo.finish()
+    g1i.turn()
+    low2i.forward()
+    g2o.turn()
+    low0o.forward()
+    g0i.finish()
+    low2i.near()
+    g1o.finish()
+    g4i.start()
+    topi.near()
+    g3i.middle()
+    g3o.middle()
+    low1o.start()
+    low0i.start()
+    low0o.near()
+    low2i.finish()
+    g2o.middle2()
+    g1i.middle2()
+    g4o.start()
+    low1o.forward()
+    low1o.near()
+    low0o.finish()
+    g4i.middle()
     g1i.finish()
     low1i.start()
-    g4i.start()
-    g3o.middle()
-    g2o.finish()
-    g1o.finish()
-    g4o.start()
-    low1o.start()
-    low0o.finish()
-    g3i.middle()
-    topi.finish()
-    topo.finish()
-    low2o.start()
-    low0i.finish()
-    low2i.forward()
-    low2i.near()
-    low1i.forward()
-    low1i.near()
-    g4i.middle()
+    low0i.forward()
     g3o.turn()
-    low1o.forward()
     g4o.middle()
     g3i.turn()
-    low2o.forward()
-    low2o.near()
+    g2o.finish()
+    low2o.start()
+    low1i.forward()
     g4i.turn()
     g3o.middle2()
+    low1o.finish()
+    low0i.near()
     g4o.turn()
+    low2o.forward()
     g3i.middle2()
     g4i.middle2()
     g3o.finish()
     low3o.start()
-    low2i.finish()
     g4o.middle2()
     g3i.finish()
-    low1o.near()
+    low2o.near()
     low3i.start()
+    low1i.near()
+    low2o.finish()
     g4i.finish()
     low4i.start()
+    low0i.finish()
     g4o.finish()
     low4o.start()
+    topi.finish()
+    low1i.finish()
+    low3i.forward()
+    low4i.forward()
+    low4i.near()
     low3o.forward()
+    low4o.forward()
+    low3i.near()
     low3o.near()
-    low2o.finish()
-    low3i.forward()
-    low3i.near()
-    low4i.forward()
-    low1i.finish()
-    low4i.near()
-    low1o.finish()
-    low4o.forward()
+    low4o.near()
     low3o.finish()
     low3i.finish()
     low4i.finish()
-    low4o.near()
     low4o.finish()
     for pair in [topi, topo] + low:
         pair.arrived()
-    done(keep)
     comm.end()
 
 
@@ -1133,13 +1133,14 @@
     shapes = grad_shapes(width, slice_)
     landed = [VMEM((CHUNKS, 6, 2) + shape, F32) for shape in shapes]
     (rows_in, cols_in), (rows_out, cols_out) = shapes
-    outs = [block, block, sds(q_top.shape[1:], BF16), sds(d_top.shape[1:], BF16),
-            sds((4, 2, CHUNKS, rows_in, cols_in), F32)] + landed + [VMEM((group, width), F32)]
+    kept = [VMEM(block.shape, BF16), VMEM(block.shape, BF16)] + landed
+    kept += [VMEM((group, width), F32), VMEM((8, tokens, width // 2), F32)]
+    outs = [sds(q_top.shape[1:], BF16), sds(d_top.shape[1:], BF16)] + kept
     acts = VMEM((group, slice_), BF16)
     scratch = [VMEM((4, width, group), BF16), VMEM((4, tokens, width), BF16), acts, acts]
-    scratch += [VMEM(block.shape, BF16) for _ in range(4)] + [VMEM(block.shape, F32), VMEM((6, tokens, width // 2), F32)]
+    scratch += [VMEM(block.shape, BF16), VMEM(block.shape, F32)]
     scratch += [VMEM(r.shape, BF16) for r in (ut_top, st_top, q_top, d_top)]
-    scratch += [VMEM(shape, F32) for shape in ((CHUNKS, rows_in, cols_in), (rows_out, CHUNKS * cols_out),
+    scratch += [VMEM(shape, F32) for shape in ((rows_in, CHUNKS * cols_in), (rows_out, CHUNKS * cols_out),
                                                (CHUNKS, rows_in, cols_in), (CHUNKS, rows_out, cols_out))]
     scratch += [VMEM((CHUNKS, 4, 2) + shape, F32) for shape in shapes]
     scratch += [VMEM((CHUNKS, 6, rows // 2, cols), F32) for rows, cols in shapes]
@@ -1150,9 +1151,9 @@
         name='lower_half',
         out_shape=tuple(outs),
         in_specs=spaces('h' * 14),
-        out_specs=tuple(spaces('hhhhhvvv')),
+        out_specs=tuple(spaces('hhvvvvvv')),
         scratch_shapes=scratch + [sems(LOWER[0]), sems(LOWER[1]), sems(LOWER[2]), pltpu.SemaphoreType.REGULAR((2 * CHUNKS, 2)),
-                                  pltpu.SemaphoreType.REGULAR, pltpu.SemaphoreType.REGULAR,
+                                  pltpu.SemaphoreType.REGULAR, pltpu.SemaphoreType.REGULAR, pltpu.SemaphoreType.REGULAR,
                                   pltpu.SemaphoreType.REGULAR((CHUNKS + 1, 2))],
         compiler_params=pltpu.CompilerParams(collective_id=2, has_side_effects=True,
                                              vmem_limit_bytes=VMEM_BYTES - VMEM_KEPT),
@@ -1160,47 +1161,45 @@
     )(*ins)
 
 
-def assemble(landed_in, landed_out, part, top_in, grad_in, grad_out, v_top_in, load_sem, store_sems):
-    load = pltpu.make_async_copy(top_in, v_top_in, load_sem)
-    load.start()
+def assemble(grad, x2, landed_in, landed_out, part, landing, grad_in, grad_out, tokens_grad, tokens_out, store_sems):
     strip = grad_in.shape[2] // 64
     rows, width = landed_out.shape[-2:]
     per = landed_in.shape[-1] // strip
-
-    def store_in(layer, block):
-        for x in range(4):
-            for n in range(2 * CHUNKS):
-                c, k = n // CHUNKS, n % CHUNKS
-                for j in range(per):
-                    t = k * per + j
-                    y, z = 2 * c + t // 4, t % 4
-                    dst = grad_in.at[layer, :, pl.ds(((4 * z + y) * 4 + x) * strip, strip)]
-                    pltpu.make_async_copy(block(x, c, k).at[:, pl.ds(j * strip, strip)], dst, store_sems.at[0]).start()
-
+    others = [pltpu.make_async_copy(grad, tokens_grad, store_sems.at[2]), pltpu.make_async_copy(x2, tokens_out, store_sems.at[3])]
+    for copy in others:
+        copy.start()
     pltpu.make_async_copy(part, grad_out.at[1], store_sems.at[1]).start()
-    store_in(0, lambda x, c, k: landed_in.at[k, x, c])
     for x in range(4):
         for n in range(2 * CHUNKS):
+            c, k = n // CHUNKS, n % CHUNKS
             dst = grad_out.at[0, pl.ds(x * rows, rows), pl.ds(n * width, width)]
-            pltpu.make_async_copy(landed_out.at[n % CHUNKS, x, n // CHUNKS], dst, store_sems.at[1]).start()
-    load.wait()
-    store_in(1, lambda x, c, k: v_top_in.at[x, c, k])
+            pltpu.make_async_copy(landed_out.at[k, x, c], dst, store_sems.at[1]).start()
+            for j in range(per):
+                t = k * per + j
+                y, z = 2 * c + t // 4, t % 4
+                cols = pl.ds(((4 * z + y) * 4 + x) * strip, strip)
+                low = landed_in.at[k, x, c, :, pl.ds(j * strip, strip)]
+                top = landing.at[2 * x + c, :, pl.ds(t * strip, strip)]
+                pltpu.make_async_copy(low, grad_in.at[0, :, cols], store_sems.at[0]).start()
+                pltpu.make_async_copy(top, grad_in.at[1, :, cols], store_sems.at[0]).start()
     pltpu.make_async_copy(grad_in, grad_in, store_sems.at[0]).wait()
     pltpu.make_async_copy(grad_out, grad_out, store_sems.at[1]).wait()
-
-
-def call_assemble(top_in, kept, in_shape, out_shape):
+    done(others)
+
+
+def call_assemble(kept, in_shape, out_shape):
     kept = [pltpu.with_memory_space_constraint(ref, VMEM) for ref in kept]
+    block = sds(kept[0].shape, BF16)
     return pl.pallas_call(
         assemble,
         name='assemble',
-        out_shape=(sds(in_shape, F32), sds(out_shape, F32)),
-        in_specs=spaces('vvvh'),
-        out_specs=tuple(spaces('hh')),
-        scratch_shapes=[VMEM(top_in.shape, F32), pltpu.SemaphoreType.DMA, sems(2)],
+        out_shape=(sds(in_shape, F32), sds(out_shape, F32), block, block),
+        in_specs=spaces('vvvvvv'),
+        out_specs=tuple(spaces('hhhh')),
+        scratch_shapes=[sems(4)],
         compiler_params=pltpu.CompilerParams(vmem_limit_bytes=VMEM_BYTES - VMEM_KEPT),
         cost_estimate=pl.CostEstimate(flops=1 << 30, bytes_accessed=1 << 25, transcendentals=0),
-    )(*kept, top_in)
+    )(*kept)
 
 
 def solution(mesh):
@@ -1210,9 +1209,9 @@
     def device_step(tokens, cotangent, w_in, w_out):
         (x1, e1, d0, part_out, a_low, ut_low, st_low, ut_top, st_top, q_top, d_top, w1_low, w2_low) = call_upper_half(
             tokens, cotangent, w_in, w_out)
-        grad, x2, _, _, top_in, *kept = call_lower_half(
+        _, _, *kept = call_lower_half(
             tokens, x1, e1, d0, part_out, w1_low, w2_low, a_low, ut_low, st_low, ut_top, st_top, q_top, d_top)
-        grad_in, grad_out = call_assemble(top_in, kept, w_in.shape, w_out.shape)
+        grad_in, grad_out, grad, x2 = call_assemble(kept, w_in.shape, w_out.shape)
         return x2, grad_in, grad_out, grad
 
     return jax.shard_map(device_step, mesh=mesh, in_specs=(tok_spec, tok_spec, w_spec, w_spec),

time: 387 us -> 382 us (0.987)
  no operation moved by 1% of the time
where the time goes in v8:
time: 382 us
  Pallas kernels  381 us (100%)
    pallas_call x1, Pallas kernels, call_lower_half(): pl.pallas_call(lower_half, name='lower_half', out_shape=tuple(outs), in_s...  190 us
    pallas_call x1, Pallas kernels, call(): pl.pallas_call(kernel, name=kernel.__name__, out_shape=tuple(outs), in_sp...  186 us

profile of v8, /device:TPU:1, one launch (start us, length us, event | category | flops | bytes accessed | tf_op | source)
XLA Modules:
  0.0 382.2 jit_solution(3099832188885093027)
XLA Ops:
  0.6 185.5 %upper_half.1 = (bf16[128,2048]{1,0:T(8,128)(2,1)}, f32[128,2048]{1,0:T(8,128)}, bf16[128,2048]{1,0:T(8,128)(2,1)}, f32[512,2048]{1,0:T(8,128)}, bf16[512,2048]{...) custom-call(bf16[128,2048]{1,0:T(8,128)(2,1)} %x0_hbm.3, ...), custom_call_target="tpu_custom_call" | custom-call | flops 34359738368 | bytes 16777216 | tf_op jit(solution)/shard_map/upper_half/pallas_call | solution.py:633
  186.2 189.8 %lower_half.1 = (bf16[512,1024]{1,0:T(8,128)(2,1)}, bf16[4,128,1024]{2,1,0:T(8,128)(2,1)}, bf16[128,2048]{1,0:T(8,128)(2,1)S(1)}, bf16[128,2048]{1,0:T(8,128)(2,...) custom-call(bf16[128,2048]{1,0:T(8,128)(2,1)} %x0_hbm.3, ...), custom_call_target="tpu_custom_call" | custom-call | flops 34359738368 | bytes 16777216 | tf_op jit(solution)/shard_map/lower_half/pallas_call | solution.py:1149
  375.9 6.1 %assemble.1 = (f32[2,128,8192]{2,1,0:T(8,128)}, f32[2,512,2048]{2,1,0:T(8,128)}, bf16[128,2048]{1,0:T(8,128)(2,1)}, bf16[128,2048]{1,0:T(8,128)(2,1)}) custom-call(bf16[128,2048]{1,0:T(8,128)(2,1)S(1)} %get-tuple-element.40.grad, bf16[128,2048]{1,0:T(8,128)(2,1)S(1)} %get-tuple-element.41.x2, f32[4,6,2,128,256]{4,3,2,1,0:T(8,128)S(1)} %get-tuple-element.42.landed_in, ...), custom_call_target="tpu_custom_call" | custom-call | flops 1073741824 | bytes 33554432 | tf_op jit(solution)/shard_map/assemble/pallas_call | solution.py:1193

commit v9 on v8

--- a/solution.py
+++ b/solution.py
@@ -18,7 +18,7 @@
 VMEM_BYTES = 67043328
 VMEM_KEPT = 169 << 17
 UPPER = (40, 95)
-LOWER = (69, 116, 35)
+LOWER = (69, 116, 34)
 
 
 class Comm:
@@ -310,20 +310,27 @@
     return [Every(out[k:k + 2]) for k in range(0, pieces, 2)]
 
 
-def own_blocks(comm, w_in, w_out, layer, w1, w2):
-    z, y, x, c = comm.z, comm.y, comm.x, comm.c
+def own_first(comm, w_in, layer, w1):
     width = w_in.shape[2] // 64
-    rows1, rows2 = w1.shape[3], w2.shape[3]
-    own = w1.at[z, y, c]
-    k = comm.local_count
+    rows = w1.shape[3]
+    own = w1.at[comm.z, comm.y, comm.c]
+    sem = comm.local_sems.at[comm.local_count]
     comm.local_count += 1
     for j in range(16):
-        start = (4 * (j % 4) + j // 4) * 4 * width + x * width
-        pltpu.make_async_copy(w_in.at[layer, pl.ds(c * rows1, rows1), pl.ds(pl.multiple_of(start, width), width)],
-                              own.at[:, pl.ds(j * width, width)], comm.local_sems.at[k]).start()
-    start = (x * 2 + c) * rows2
-    copies = comm.local((w_out.at[layer, pl.ds(pl.multiple_of(start, rows2), rows2)], w2.at[y, z, c]))
-    return [pltpu.make_async_copy(own, own, comm.local_sems.at[k])] + copies
+        start = (4 * (j % 4) + j // 4) * 4 * width + comm.x * width
+        pltpu.make_async_copy(w_in.at[layer, pl.ds(comm.c * rows, rows), pl.ds(pl.multiple_of(start, width), width)],
+                              own.at[:, pl.ds(j * width, width)], sem).start()
+    return [pltpu.make_async_copy(own, own, sem)]
+
+
+def own_second(comm, w_out, layer, w2):
+    rows = w2.shape[3]
+    start = (comm.x * 2 + comm.c) * rows
+    return comm.local((w_out.at[layer, pl.ds(pl.multiple_of(start, rows), rows)], w2.at[comm.y, comm.z, comm.c]))
+
+
+def own_blocks(comm, w_in, w_out, layer, w1, w2):
+    return own_first(comm, w_in, layer, w1) + own_second(comm, w_out, layer, w2)
 
 
 def ring_of_tokens(comm, full, before=None):
@@ -426,15 +433,21 @@
     lax.fori_loop(0, 8, step, 0)
 
 
-def backward_part(tile_product, part, half):
+def backward_part(tile_product, part, half, which=slice(None)):
     rows = part.shape[1] // 8
 
     def step(j, _):
         i = half * 4 + j
-        part[:, pl.ds(pl.multiple_of(i * rows, rows), rows)] = tile_product(i)
+        part[which, pl.ds(pl.multiple_of(i * rows, rows), rows)] = tile_product(i)
         return 0
 
     lax.fori_loop(0, 4, step, 0)
+
+
+def backward_rows(q, w1, part, pos, tokens, half):
+    rows = pl.ds(pl.multiple_of(pos * tokens, tokens), tokens)
+    tile_product = lambda i: dot_bt(q[rows], row_tile(w1, i))
+    backward_part(tile_product, part, half, rows)
 
 
 def last_dim_half(ref, k):
@@ -443,13 +456,13 @@
 
 
 def upper_half(x0_hbm, cot, w_in, w_out,
-               x1_out, e1_out, d0_out, part_out, a_low, ut_low, st_low, ut_top, st_top, q_top, d_top, w1_low, w2_low,
-               p1, p2, q1, q2, uf, df, a, s, q, ut, st, x0, x1, d0, part, landing, e1,
+               x1_out, e1_out, part_out, a_low, ut_low, st_low, ut_top, st_top, q_top, d_top, w1_low, w2_low,
+               p1, p2, q1, q2, uf, df, a, s, q, ut, st, x0, x1, part, landing, e1,
                send_sems, recv_sems, local_sems, credits):
     comm = Comm(send_sems, recv_sems, local_sems)
     tokens = x0.shape[0]
     x, c = comm.x, comm.c
-    p_free, q_free = credits.at[0], credits.at[1]
+    p_free, q1_free, q2_free = [credits.at[k] for k in range(3)]
 
     comm.arrive('xyzc')
     load_x = comm.local((x0_hbm, x0))
@@ -468,50 +481,48 @@
     n2, = gathers(comm, 'yz', q2, 2)
     done(own0 + load_d)
     g2.start1()
+    gather_d.start()
+    g1.start1()
     gather_u.start()
-    g1.start1()
+    g2.forward1()
     done(own1)
-    g2.forward1()
     g3.start1()
     g1.forward1()
     g2.start2()
     g3.forward1()
-    gather_u.forward()
-    gather_d.start()
+    gather_d.forward()
     g1.start2()
-    gather_u.near()
-    gather_u.finish()
+    gather_d.near()
     g1.forward2()
     g2.forward2()
+    gather_u.forward()
     n2.start1()
+    n1.start1()
     g2.near2()
+    gather_u.near()
     g3.start2()
-    gather_d.forward()
-    n1.start1()
-    transposed(uf, ut)
-    pushed = [comm.push(ut, ut_low.at[1])]
-    kept = comm.local((ut, ut_low.at[0]))
     g1.near2()
-    gather_d.near()
+    gather_d.finish()
     g1.finish2()
+    gather_u.finish()
     g2.finish2()
-    gather_d.finish()
     g1.arrived()
     forward_acts(uf, p1, a, s, st)
+    n1.forward1()
     n2.forward1()
-    g3.forward2()
     g2.arrived()
     gather_u.sent()
     ring = token_sums(comm, part, landing, tokens)
     forward_part(s, p2, part, 0)
     ring.start_half(0)
-    n1.forward1()
+    g3.forward2()
+    g3.near2()
+    transposed(uf, ut)
+    pushed = [comm.push(ut, ut_low.at[1])]
+    kept = comm.local((ut, ut_low.at[0]))
     pushed += [comm.push(st, st_low.at[1])]
     kept += comm.local((st, st_low.at[0]), (a, a_low))
-    g3.near2()
-    pushed += [comm.push(last_dim_half(df, 1 - c), d_top.at[1])]
-    kept_d = comm.local((last_dim_half(df, c), d_top.at[0]))
-    n2.start2()
+    n1.start2()
     g3.finish2()
     g3.arrived()
     forward_part(s, p2, part, 1)
@@ -523,19 +534,22 @@
     own2 = own_blocks(comm, w_in, w_out, 1, p1, p2)
     b1, = gathers(comm, 'zy', p1, 2, g1)
     b2, = gathers(comm, 'yz', p2, 2, g2)
+    n1.forward2()
     done(own2)
     comm.wait(p_free, 'yzc')
+    ring.middle_right()
+    pushed += [comm.push(last_dim_half(df, 1 - c), d_top.at[1])]
+    kept_d = comm.local((last_dim_half(df, c), d_top.at[0]))
+    b2.start1()
     b1.start1()
-    b2.start1()
-    n1.start2()
+    n1.near2()
+    n1.finish2()
+    n2.start2()
+    b2.forward1()
+    ring.middle_left()
+    n1.arrived()
+    b1.forward1()
     n2.forward2()
-    ring.middle_right()
-    n2.near2()
-    b2.forward1()
-    b1.forward1()
-    ring.middle_left()
-    n1.forward2()
-    n1.near2()
     ring.finish()
     x_next = (x0[...].astype(F32) + jnp.concatenate(ring.sums(), axis=1)).astype(BF16)
     x1[...] = x_next
@@ -544,15 +558,14 @@
     ring.sent()
     gather_v = ring_of_tokens(comm, uf, gather_u)
     gather_v.start()
-    n2.finish2()
+    n2.near2()
     done(kept)
     pushed[0][0].wait()
     pushed[1][0].wait()
     b2.start2()
+    n2.finish2()
+    gather_v.forward()
     n2.arrived()
-    n1.finish2()
-    gather_v.forward()
-    n1.arrived()
     b2.forward2()
     gather_v.near()
     b1.start2()
@@ -560,57 +573,67 @@
     gather_v.finish()
     forward_acts(uf, q1, a, s, st)
     b2.finish2()
+    n1.sent()
+    comm.signal(q1_free, 'yzc')
+    own4 = own_first(comm, w_in, 0, q1)
+    l1, = gathers(comm, 'zy', q1, 2, n1, w1_low)
+    done(own4)
+    comm.wait(q1_free, 'yzc')
+    l1.start1()
     forward_part(s, q2, part, 0)
     forward_part(s, q2, part, 1)
     keep_part = comm.local((part, part_out))
     b1.forward2()
-    n1.sent()
     n2.sent()
-    comm.signal(q_free, 'yzc')
-    own3 = own_blocks(comm, w_in, w_out, 0, q1, q2)
-    l1, = gathers(comm, 'zy', q1, 2, n1, w1_low)
+    comm.signal(q2_free, 'yzc')
+    own3 = own_second(comm, w_out, 0, q2)
     l2, = gathers(comm, 'yz', q2, 2, n2, w2_low)
     b2.arrived()
     done(own3)
-    comm.wait(q_free, 'yzc')
-    l2.start1()
+    comm.wait(q2_free, 'yzc')
     b1.near2()
+    l1.forward1()
     backward_acts(df, lambda i: dot_bt(flat(df[...]), row_tile(p2, i)), a, q)
     b1.finish2()
-    l2.forward1()
-    l1.start1()
+    l2.start1()
+    l1.start2()
     transposed(uf, ut)
     pushed += [comm.push(ut, ut_top.at[1]), comm.push(st, st_top.at[1])]
     kept = kept_d + comm.local((ut, ut_top.at[0]), (st, st_top.at[0]))
-    pushed += [comm.push(last_dim_half(q, 1 - c), q_top.at[1])]
-    kept += comm.local((last_dim_half(q, c), q_top.at[0]))
     b1.arrived()
     done(keep_part)
     ring = token_sums(comm, part, landing, tokens, ring)
-    product = lambda i: dot_bt(q[...], row_tile(p1, i))
-    backward_part(product, part, 0)
-    ring.start_half(0)
-    l1.forward1()
+    left, right = halves = range(2)
+    tiles_of = lambda pos, half: backward_rows(q, p1, part, pos, tokens, half)
+    for half in halves:
+        tiles_of(ring.far, half)
+    ring.start_far(*[ring.part(ring.far, half) for half in halves])
+    l2.forward1()
+    pushed += [comm.push(last_dim_half(q, 1 - c), q_top.at[1])]
+    kept += comm.local((last_dim_half(q, c), q_top.at[0]))
+    tiles_of(ring.right, right)
+    tiles_of(ring.left, left)
+    ring.start_near(ring.part(ring.right, right), ring.part(ring.left, left))
+    l1.forward2()
+    tiles_of(ring.right, left)
+    tiles_of(ring.left, right)
+    for half in halves:
+        tiles_of(ring.me, half)
+    l1.near2()
     l2.start2()
-    backward_part(product, part, 1)
-    ring.start_half(1)
+    ring.middle_right()
+    ring.middle_left()
+    l1.finish2()
     l2.forward2()
-    l1.start2()
-    ring.middle_right()
+    l1.arrived()
     l2.near2()
     l2.finish2()
-    ring.middle_left()
-    l1.forward2()
-    l2.arrived()
-    l1.near2()
-    l1.finish2()
     ring.finish()
     g = jnp.concatenate(ring.sums(), axis=1)
     e = df[x].astype(F32) + norm_rows_vjp(x1[...].astype(F32), g)
     e1[...] = e
-    d0[...] = e.astype(BF16)
-    kept += keep_x + comm.local((e1, e1_out), (d0, d0_out))
-    l1.arrived()
+    kept += keep_x + comm.local((e1, e1_out))
+    l2.arrived()
     for _, arrived in pushed:
         arrived()
     done(kept)
@@ -654,14 +677,14 @@
     acts = (group, slice_)
     ut, st = (width, group), (slice_, group)
     pair = lambda shape: sds((2,) + shape, BF16)
-    outs = [block, sds((tokens, width), F32), block, sds((group, width), F32), sds(acts, BF16),
+    outs = [block, sds((tokens, width), F32), sds((group, width), F32), sds(acts, BF16),
             pair(ut), pair(st), pair(ut), pair(st), pair((group, slice_ // 2)), pair((4, tokens, width // 2)),
             sds(w1, BF16), sds(w2, BF16)]
     tok = (4, tokens, width)
     scratch = [VMEM(shape, BF16) for shape in (w1, w2, w1, w2, tok, tok, acts, acts, acts, ut, st, block.shape,
-                                            block.shape, block.shape)]
+                                            block.shape)]
     scratch += [VMEM((group, width), F32), VMEM((6, tokens, width // 2), F32), VMEM(block.shape, F32)]
-    return call(upper_half, (x0, cot, w_in, w_out), 'hhhh', outs, 'h' * 13, scratch, (UPPER, 37), 2, 1,
+    return call(upper_half, (x0, cot, w_in, w_out), 'hhhh', outs, 'h' * 12, scratch, (UPPER, 36), 3, 1,
                 16 * group * width * slice_)
 
 
@@ -847,7 +870,7 @@
     return [(src.at[..., cols], dst.at[..., cols]) for cols in (pl.ds(0, n), pl.ds(n, src.shape[-1] - n))]
 
 
-def lower_half(x0_hbm, x1_hbm, e1_hbm, d0, part_hbm, w1_hbm, w2_hbm, a_hbm, ut_low, st_low, ut_top, st_top, q_top, d_top,
+def lower_half(x0_hbm, x1_hbm, e1_hbm, part_hbm, w1_hbm, w2_hbm, a_hbm, ut_low, st_low, ut_top, st_top, q_top, d_top,
                q_low, d_low, grad, x2, landed_in, landed_out, part, landing,
                w, df, a, q, xv, e1, gut, gst, gq, gd, top_in, top_out, low_in, low_out,
                sends_in, sends_out, landing2_in, landing2_out,
@@ -857,7 +880,7 @@
     tokens = xv.shape[0]
     x, c = comm.x, comm.c
     group = a.shape[0]
-    load_d = comm.local((d0, df.at[x]))
+    load_d = comm.local((e1_hbm, e1))
     far_in, rest_in = rows_from(ut_top, gut, comm.z + 2)
     far_out, rest_out = rows_from(st_top, gst, comm.y + 2)
     q_first, q_rest = columns_from(q_top, gq)
@@ -872,9 +895,10 @@
 
     gather_d = ring_of_tokens(comm, df)
     done(load_d)
+    df[x] = e1[...].astype(BF16)
     gather_d.start()
     load2 = load_w(w2_hbm) + comm.local((a_hbm, a))
-    load_x = comm.local((x0_hbm, xv), (e1_hbm, e1))
+    load_x = comm.local((x0_hbm, xv))
     own_b = lambda ref: lambda cols: flat(ref[..., cols])
     top = [[(gut.at[k], own_b(gq.at[k])) for k in (0, 1)], [(gst.at[k], own_b(gd.at[k])) for k in (0, 1)]]
     chunk_out = low_out.shape[2]
@@ -1126,7 +1150,7 @@
     comm.end()
 
 
-def call_lower_half(x0, x1, e1, d0, part_hbm, w1_hbm, w2_hbm, a_hbm, ut_low, st_low, ut_top, st_top, q_top, d_top):
+def call_lower_half(x0, x1, e1, part_hbm, w1_hbm, w2_hbm, a_hbm, ut_low, st_low, ut_top, st_top, q_top, d_top):
     tokens, width = x0.shape
     group, slice_ = a_hbm.shape
     block = sds((tokens, width), BF16)
@@ -1144,13 +1168,13 @@
                                                (CHUNKS, rows_in, cols_in), (CHUNKS, rows_out, cols_out))]
     scratch += [VMEM((CHUNKS, 4, 2) + shape, F32) for shape in shapes]
     scratch += [VMEM((CHUNKS, 6, rows // 2, cols), F32) for rows, cols in shapes]
-    ins = (x0, x1, e1, d0, part_hbm, w1_hbm.reshape(width, slice_), w2_hbm.reshape(slice_, width), a_hbm,
+    ins = (x0, x1, e1, part_hbm, w1_hbm.reshape(width, slice_), w2_hbm.reshape(slice_, width), a_hbm,
            ut_low, st_low, ut_top, st_top, q_top, d_top)
     return pl.pallas_call(
         lower_half,
         name='lower_half',
         out_shape=tuple(outs),
-        in_specs=spaces('h' * 14),
+        in_specs=spaces('h' * 13),
         out_specs=tuple(spaces('hhvvvvvv')),
         scratch_shapes=scratch + [sems(LOWER[0]), sems(LOWER[1]), sems(LOWER[2]), pltpu.SemaphoreType.REGULAR((2 * CHUNKS, 2)),
                                   pltpu.SemaphoreType.REGULAR, pltpu.SemaphoreType.REGULAR, pltpu.SemaphoreType.REGULAR,
@@ -1207,10 +1231,10 @@
     w_spec = P(None, 'local', None)
 
     def device_step(tokens, cotangent, w_in, w_out):
-        (x1, e1, d0, part_out, a_low, ut_low, st_low, ut_top, st_top, q_top, d_top, w1_low, w2_low) = call_upper_half(
+        (x1, e1, part_out, a_low, ut_low, st_low, ut_top, st_top, q_top, d_top, w1_low, w2_low) = call_upper_half(
             tokens, cotangent, w_in, w_out)
         _, _, *kept = call_lower_half(
-            tokens, x1, e1, d0, part_out, w1_low, w2_low, a_low, ut_low, st_low, ut_top, st_top, q_top, d_top)
+            tokens, x1, e1, part_out, w1_low, w2_low, a_low, ut_low, st_low, ut_top, st_top, q_top, d_top)
         grad_in, grad_out, grad, x2 = call_assemble(kept, w_in.shape, w_out.shape)
         return x2, grad_in, grad_out, grad
 

time: 382 us -> 382 us (level)
  no operation moved by 1% of the time
where the time goes in v9:
time: 382 us
  Pallas kernels  381 us (100%)
    pallas_call x1, Pallas kernels, call_lower_half(): pl.pallas_call(lower_half, name='lower_half', out_shape=tuple(outs), in_s...  190 us
    pallas_call x1, Pallas kernels, call(): pl.pallas_call(kernel, name=kernel.__name__, out_shape=tuple(outs), in_sp...  185 us

profile of v9, /device:TPU:1, one launch (start us, length us, event | category | flops | bytes accessed | tf_op | source)
XLA Modules:
  0.0 381.8 jit_solution(16842591763532932063)
XLA Ops:
  0.6 184.6 %upper_half.1 = (bf16[128,2048]{1,0:T(8,128)(2,1)}, f32[128,2048]{1,0:T(8,128)}, f32[512,2048]{1,0:T(8,128)}, bf16[512,2048]{1,0:T(8,128)(2,1)}, bf16[2,2048,512...) custom-call(bf16[128,2048]{1,0:T(8,128)(2,1)} %x0_hbm.3, ...), custom_call_target="tpu_custom_call" | custom-call | flops 34359738368 | bytes 16777216 | tf_op jit(solution)/shard_map/upper_half/pallas_call | solution.py:656
  185.3 190.2 %lower_half.1 = (bf16[512,1024]{1,0:T(8,128)(2,1)}, bf16[4,128,1024]{2,1,0:T(8,128)(2,1)}, bf16[128,2048]{1,0:T(8,128)(2,1)S(1)}, bf16[128,2048]{1,0:T(8,128)(2,...) custom-call(bf16[128,2048]{1,0:T(8,128)(2,1)} %x0_hbm.3, ...), custom_call_target="tpu_custom_call" | custom-call | flops 34359738368 | bytes 16777216 | tf_op jit(solution)/shard_map/lower_half/pallas_call | solution.py:1173
  375.5 6.1 %assemble.1 = (f32[2,128,8192]{2,1,0:T(8,128)}, f32[2,512,2048]{2,1,0:T(8,128)}, bf16[128,2048]{1,0:T(8,128)(2,1)}, bf16[128,2048]{1,0:T(8,128)(2,1)}) custom-call(bf16[128,2048]{1,0:T(8,128)(2,1)S(1)} %get-tuple-element.38.grad, bf16[128,2048]{1,0:T(8,128)(2,1)S(1)} %get-tuple-element.39.x2, f32[4,6,2,128,256]{4,3,2,1,0:T(8,128)S(1)} %get-tuple-element.40.landed_in, ...), custom_call_target="tpu_custom_call" | custom-call | flops 1073741824 | bytes 33554432 | tf_op jit(solution)/shard_map/assemble/pallas_call | solution.py:1217

commit v10 on v9

--- a/solution.py
+++ b/solution.py
@@ -714,7 +714,7 @@
 
         lax.fori_loop(0, 4, step, 0)
 
-    def start_far(self):
+    def take_far(self):
         me, sends = self.ring.me, self.sends
         if self.before:
             self.before.sent()
@@ -724,7 +724,9 @@
             sends[i, j] = value
 
         self.products(lambda i: ((me + 2) % 4, i), store)
-        self.ring.start_far(sends.at[0], sends.at[1])
+
+    def send_far(self):
+        self.ring.start_far(self.sends.at[0], self.sends.at[1])
 
     def start_near(self):
         me, sends = self.ring.me, self.sends
@@ -736,7 +738,8 @@
         self.ring.start_near(sends.at[2], sends.at[3])
 
     def start(self):
-        self.start_far()
+        self.take_far()
+        self.send_far()
         self.start_near()
 
     def middle(self):
@@ -891,20 +894,23 @@
     loads_rest = comm.local(q_rest, d_rest, *rest_in, *rest_out)
     columns = lambda ref, j: ref.at[:, pl.ds(j * group, group)]
     load_w = lambda ref: comm.local(*[(columns(ref, j), w.at[j]) for j in range(4)])
+    own_b = lambda ref: lambda cols: flat(ref[..., cols])
+    top = [[(at.at[k], own_b(b.at[k])) for k in (0, 1)] for at, b in ((gut, gq), (gst, gd))]
+    chunk_out = low_out.shape[2]
+    top_results = lambda i, k, cols: (top_out if i else top_in).at[:, pl.ds(k * chunk_out, chunk_out)]
+    upper = grad_chunks(comm, top, bufs, top_results, credits)
+    (t0i, t0o), (t1i, t1o), (t2i, t2o), (t3i, t3o) = [pair.things for pair in upper]
+    done(loads_in)
+    t0i.take_far()
     comm.meet('xyzc')
 
+    t0i.send_far()
     gather_d = ring_of_tokens(comm, df)
     done(load_d)
     df[x] = e1[...].astype(BF16)
     gather_d.start()
     load2 = load_w(w2_hbm) + comm.local((a_hbm, a))
     load_x = comm.local((x0_hbm, xv))
-    own_b = lambda ref: lambda cols: flat(ref[..., cols])
-    top = [[(gut.at[k], own_b(gq.at[k])) for k in (0, 1)], [(gst.at[k], own_b(gd.at[k])) for k in (0, 1)]]
-    chunk_out = low_out.shape[2]
-    top_results = lambda i, k, cols: (top_out if i else top_in).at[:, pl.ds(k * chunk_out, chunk_out)]
-    upper = grad_chunks(comm, top, bufs, top_results, credits)
-    (t0i, t0o), (t1i, t1o), (t2i, t2o), (t3i, t3o) = [pair.things for pair in upper]
 
     def by_columns(left):
         rows = w.shape[1] // 8
@@ -919,10 +925,9 @@
 
         return product
 
-    done(loads_in)
-    t0i.start_far()
     done(loads_out)
-    t0o.start_far()
+    t0o.take_far()
+    t0o.send_far()
     done(loads_rest)
     t0i.start_near()
     t0o.start_near()

time: 382 us -> 382 us (level)
  no operation moved by 1% of the time
where the time goes in v10:
time: 382 us
  Pallas kernels  381 us (100%)
    pallas_call x1, Pallas kernels, call_lower_half(): pl.pallas_call(lower_half, name='lower_half', out_shape=tuple(outs), in_s...  190 us
    pallas_call x1, Pallas kernels, call(): pl.pallas_call(kernel, name=kernel.__name__, out_shape=tuple(outs), in_sp...  185 us

profile of v10, /device:TPU:1, one launch (start us, length us, event | category | flops | bytes accessed | tf_op | source)
XLA Modules:
  0.0 381.8 jit_solution(10836603859849474363)
XLA Ops:
  0.6 184.6 %upper_half.1 = (bf16[128,2048]{1,0:T(8,128)(2,1)}, f32[128,2048]{1,0:T(8,128)}, f32[512,2048]{1,0:T(8,128)}, bf16[512,2048]{1,0:T(8,128)(2,1)}, bf16[2,2048,512...) custom-call(bf16[128,2048]{1,0:T(8,128)(2,1)} %x0_hbm.3, ...), custom_call_target="tpu_custom_call" | custom-call | flops 34359738368 | bytes 16777216 | tf_op jit(solution)/shard_map/upper_half/pallas_call | solution.py:656
  185.3 190.2 %lower_half.1 = (bf16[512,1024]{1,0:T(8,128)(2,1)}, bf16[4,128,1024]{2,1,0:T(8,128)(2,1)}, bf16[128,2048]{1,0:T(8,128)(2,1)S(1)}, bf16[128,2048]{1,0:T(8,128)(2,...) custom-call(bf16[128,2048]{1,0:T(8,128)(2,1)} %x0_hbm.3, ...), custom_call_target="tpu_custom_call" | custom-call | flops 34359738368 | bytes 16777216 | tf_op jit(solution)/shard_map/lower_half/pallas_call | solution.py:1178
  375.5 6.1 %assemble.1 = (f32[2,128,8192]{2,1,0:T(8,128)}, f32[2,512,2048]{2,1,0:T(8,128)}, bf16[128,2048]{1,0:T(8,128)(2,1)}, bf16[128,2048]{1,0:T(8,128)(2,1)}) custom-call(bf16[128,2048]{1,0:T(8,128)(2,1)S(1)} %get-tuple-element.38.grad, bf16[128,2048]{1,0:T(8,128)(2,1)S(1)} %get-tuple-element.39.x2, f32[4,6,2,128,256]{4,3,2,1,0:T(8,128)S(1)} %get-tuple-element.40.landed_in, ...), custom_call_target="tpu_custom_call" | custom-call | flops 1073741824 | bytes 33554432 | tf_op jit(solution)/shard_map/assemble/pallas_call | solution.py:1222
